TPU v7x, 32 devices: a whole 2x2x4 slice. The times are simulated.
32 devices in a mesh: batch: 2 (over x), col: 4 (over z), row: 4 (over y, core).
Axes of the slice: x: 2, y: 2, z: 4, core: 2. Of those that a mesh axis runs over, the one named last changes fastest.
Arguments:
- pair_rep: bfloat16 [1536, 768, 128], P(('batch', 'row'), 'col'), parts along dimension 0
- pair_mask: int32 [1536, 768], P(('batch', 'row'), 'col'), parts along dimension 0
- ln_in_scale: bfloat16 [128], replicated
- w_left: bfloat16 [128, 128], replicated
- w_left_gate: bfloat16 [128, 128], replicated
- w_right: bfloat16 [128, 128], replicated
- w_right_gate: bfloat16 [128, 128], replicated
- w_out_gate: bfloat16 [128, 128], replicated
- ln_out_scale: bfloat16 [128], replicated
- w_out: bfloat16 [128, 128], replicated
Outputs:
- output: bfloat16 [1536, 768, 128], P(('batch', 'row'), 'col'), parts along dimension 0
There are 2 independent parts. A program takes and returns all parts, laid end to end along the dimension named above; an argument that names none is the same for every part.
All inputs are finite; a program needn't handle non-finite values.
Results may differ from a plain program's by a relative error of at most 0.00119143.
Values are sent between devices in bfloat16 or wider.
A program may use at most 1 GiB of HBM per device.

v0:
```python
import jax
import jax.numpy as jnp
from jax import lax
from jax.experimental import pallas as pl
from jax.experimental.pallas import tpu as pltpu
from jax.sharding import PartitionSpec as P


LN_EPS = 0.00001
AXES = ('col', 'row')
BF16, F32 = jnp.bfloat16, jnp.float32
VMEM_BYTES = 60 * 2**20
FLOPS_PER_US = 5_000_000


def moves(target):
    pairs = []
    for z in range(4):
        for y in range(2):
            for c in range(2):
                to = target(y, z, c)
                if to is not None:
                    pairs.append((z * 4 + y * 2 + c, to[1] * 4 + to[0] * 2 + to[2]))
    return pairs


TO_Y = moves(lambda y, z, c: (1 - y, z, c))
TO_Z = moves(lambda y, z, c: (y, z ^ 1, c))
TO_CORE = moves(lambda y, z, c: (y, z, 1 - c))
ACROSS = moves(lambda y, z, c: (y, 3 - z if z in (1, 2) else z, c))


def home(from_y, turn):
    def target(y, z, c):
        if y != from_y:
            return None
        half = z // 2
        block_half = 1 - half if z in (1, 2) else half
        to = (block_half, 2 * half + c, half ^ turn)
        return None if to == (y, z, c) else to

    return moves(target)


def send(value, pairs):
    return lax.ppermute(value, AXES, pairs)


def after(value, *others):
    return lax.optimization_barrier((value,) + others)[0]


def cost(us, nbytes):
    return pl.CostEstimate(flops=us * FLOPS_PER_US, bytes_accessed=nbytes, transcendentals=0)


def params():
    return pltpu.CompilerParams(vmem_limit_bytes=VMEM_BYTES)


def normed(values, gain):
    mean_val = jnp.mean(values, axis=-1, keepdims=True)
    centered = values - mean_val
    variance = jnp.mean(centered * centered, axis=-1, keepdims=True)
    return (centered * lax.rsqrt(variance + LN_EPS) * gain).astype(BF16)


def dot_nt(lhs, rhs):
    return lax.dot_general(lhs, rhs, (((1,), (1,)), ((), ())), preferred_element_type=F32)


def project_body(pieces, gain_ref, w_ref, out_refs, s_ref):
    tri = s_ref.shape[1]
    gain = gain_ref[...].astype(F32)
    x = jnp.concatenate([normed(p.astype(F32), gain) for p in pieces], axis=0)
    x = jnp.swapaxes(x, 0, 1)
    for i in range(x.shape[0]):
        proj = dot_nt(w_ref[...], x[i])
        s_ref[i] = jax.nn.sigmoid(proj[tri:]) * proj[:tri]
    part = tri // len(out_refs)
    for q, out_ref in enumerate(out_refs):
        out_ref[...] = jnp.swapaxes(s_ref[:, q * part:(q + 1) * part, :], 0, 1).astype(BF16)


def project_kernel(p0_ref, p1_ref, gain_ref, w_ref, *refs):
    project_body((p0_ref[...], p1_ref[...]), gain_ref, w_ref, refs[:-1], refs[-1])


def project_pick_kernel(flag_ref, p0_ref, p1_ref, q0_ref, q1_ref, gain_ref, w_ref, out_ref, s_ref):
    pick = flag_ref[0] != 0
    project_body((jnp.where(pick, p0_ref[...], q0_ref[...]), jnp.where(pick, p1_ref[...], q1_ref[...])), gain_ref, w_ref, (out_ref,), s_ref)


def project(pieces, gain, w_t, n_out=1, blk=16):
    rows, cols, dim = pieces[0].shape
    wide = w_t.shape[0]
    tri = wide // 2
    return pl.pallas_call(
        project_kernel,
        grid=(cols // blk,),
        in_specs=[pl.BlockSpec((rows, blk, dim), lambda g: (0, g, 0))] * 2
        + [pl.BlockSpec((1, dim), lambda g: (0, 0)), pl.BlockSpec((wide, dim), lambda g: (0, 0))],
        out_specs=[pl.BlockSpec((tri // n_out, blk, 2 * rows), lambda g: (0, g, 0))] * n_out,
        out_shape=[jax.ShapeDtypeStruct((tri // n_out, cols, 2 * rows), BF16)] * n_out,
        scratch_shapes=[pltpu.VMEM((blk, tri, 2 * rows), F32)],
        compiler_params=params(),
        cost_estimate=cost(23, 4 * rows * cols * (dim + tri)),
        name='project',
    )(*pieces, gain, w_t)


def project_pick(flag, yes, no, gain, w_t, blk=16):
    rows, cols, dim = yes[0].shape
    wide = w_t.shape[0]
    tri = wide // 2
    return pl.pallas_call(
        project_pick_kernel,
        grid_spec=pltpu.PrefetchScalarGridSpec(
            num_scalar_prefetch=1,
            grid=(cols // blk,),
            in_specs=[pl.BlockSpec((rows, blk, dim), lambda g, f: (0, g * f[0], 0))] * 2
            + [pl.BlockSpec((rows, blk, dim), lambda g, f: (0, g * (1 - f[0]), 0))] * 2
            + [pl.BlockSpec((1, dim), lambda g, f: (0, 0)), pl.BlockSpec((wide, dim), lambda g, f: (0, 0))],
            out_specs=pl.BlockSpec((tri, blk, 2 * rows), lambda g, f: (0, g, 0)),
            scratch_shapes=[pltpu.VMEM((blk, tri, 2 * rows), F32)],
        ),
        out_shape=jax.ShapeDtypeStruct((tri, cols, 2 * rows), BF16),
        compiler_params=params(),
        cost_estimate=cost(23, 4 * rows * cols * (dim + tri)),
        name='project_pick',
    )(flag, *yes, *no, gain, w_t)


def triangle_kernel(n_prev, last, *refs):
    (a0_ref, a1_ref), b_refs, refs = refs[:2], refs[2:6], refs[6:]
    step, steps = pl.program_id(0), pl.num_programs(0)
    n_h, n_i, _ = a0_ref.shape
    n_j = 2 * b_refs[0].shape[1]
    pitch = n_i + 8
    spans = [(at, min(128, n_j - at)) for at in range(0, n_j, 128)]
    n_o = len(spans)
    if last:
        prev_refs, gain_ref, out_ref, o_refs = refs[:n_o * n_prev], refs[n_o * n_prev], refs[n_o * n_prev + 1], refs[n_o * n_prev + 2:]
    else:
        o_refs = refs
    base = (step + n_prev * steps) * n_h if last else 0
    for h in range(n_h):
        acc = dot_nt(a0_ref[h], jnp.concatenate([b_refs[0][h], b_refs[1][h]], axis=0))
        acc += dot_nt(a1_ref[h], jnp.concatenate([b_refs[2][h], b_refs[3][h]], axis=0))
        start = pl.multiple_of((base + h) * pitch, 8)
        for (at, width), o_ref in zip(spans, o_refs):
            o_ref[pl.ds(start, n_i), :width] = acc[:, at:at + width]
    if not last:
        return
    if n_prev:
        for prev_ref, o_ref in zip(prev_refs, o_refs):
            o_ref[pl.ds(pl.multiple_of(step * n_h * pitch, 8), n_h * pitch), :] = prev_ref[...]

    @pl.when(step == steps - 1)
    def _():
        tri = o_refs[0].shape[0] // pitch
        gain = gain_ref[...].astype(F32)

        @pl.loop(0, n_i)
        def _(i):
            for (at, width), o_ref in zip(spans, o_refs):
                values = o_ref[pl.ds(i, tri, stride=pitch), :][:, :width]
                mean_val = jnp.mean(values, axis=0, keepdims=True)
                centered = values - mean_val
                variance = jnp.mean(centered * centered, axis=0, keepdims=True)
                unit = centered * lax.rsqrt(variance + LN_EPS)
                out_ref[i, pl.ds(at, width), :] = (unit.T * gain).astype(BF16)


def triangle(a_pair, b_parts, gain, first=0, prev=None, last=True, blk=8):
    part, n_i, n_k = a_pair[0].shape
    tri, half_j, _ = b_parts[0].shape
    n_j = 2 * half_j
    pitch, n_o = n_i + 8, pl.cdiv(n_j, 128)
    n_prev = 0 if prev is None else 1
    o_spec = pl.BlockSpec((blk * pitch, 128), lambda g: (g, 0))
    in_specs = [pl.BlockSpec((blk, n_i, n_k), lambda g: (g, 0, 0))] * 2
    in_specs += [pl.BlockSpec((blk, half_j, n_k), lambda g: (g + first // blk, 0, 0))] * 4
    operands = [*a_pair, *b_parts]
    if last:
        in_specs += [o_spec] * (n_o * n_prev) + [pl.BlockSpec((1, tri), lambda g: (0, 0))]
        operands += list(prev or []) + [gain]
        out_specs = pl.BlockSpec((n_i, n_j, tri), lambda g: (0, 0, 0))
        out_shape = jax.ShapeDtypeStruct((n_i, n_j, tri), BF16)
        scratch = [pltpu.VMEM((tri * pitch, 128), F32)] * n_o
    else:
        out_specs = [o_spec] * n_o
        out_shape = [jax.ShapeDtypeStruct((part * pitch, 128), F32)] * n_o
        scratch = []
    return pl.pallas_call(
        lambda *refs: triangle_kernel(n_prev, last, *refs),
        grid=(part // blk,),
        in_specs=in_specs,
        out_specs=out_specs,
        out_shape=out_shape,
        scratch_shapes=scratch,
        compiler_params=params(),
        cost_estimate=cost(30 * part // tri + (15 if last else 0), 2 * part * n_k * 2 * (n_i + n_j)),
        name='triangle',
    )(*operands)


def gate_kernel(z_ref, gain_ref, wg_ref, out_ref):
    rows, cols, dim = z_ref.shape
    x = normed(z_ref[...].astype(F32).reshape(rows * cols, dim), gain_ref[...].astype(F32))
    out_ref[...] = jax.nn.sigmoid(jnp.dot(x, wg_ref[...], preferred_element_type=F32)).reshape(rows, cols, dim)


def out_gate(pair_tile, gain, w_gate, blk=16):
    rows, cols, dim = pair_tile.shape
    blk = min(blk, rows)
    spec = pl.BlockSpec((blk, cols, dim), lambda g: (g, 0, 0))
    return pl.pallas_call(
        gate_kernel,
        grid=(rows // blk,),
        in_specs=[spec, pl.BlockSpec((1, dim), lambda g: (0, 0)), pl.BlockSpec((dim, dim), lambda g: (0, 0))],
        out_specs=spec,
        out_shape=jax.ShapeDtypeStruct(pair_tile.shape, F32),
        compiler_params=params(),
        cost_estimate=cost(18, 6 * rows * cols * dim),
        name='out_gate',
    )(pair_tile, gain, w_gate)


def finish_kernel(pick_ref, z_ref, gate_ref, *refs):
    y_refs, wo_ref, out_ref = refs[:-2], refs[-2], refs[-1]
    rows, cols, dim = z_ref.shape
    n_cand = len(y_refs) // 2

    for s in (0, 1):
        for q in range(n_cand):
            @pl.when((pl.program_id(0) == s) & (pick_ref[s] == q))
            def _(y_ref=y_refs[s * n_cand + q]):
                update = jnp.dot(y_ref[...].reshape(rows * cols, -1), wo_ref[...], preferred_element_type=F32)
                out_ref[...] = (z_ref[...].astype(F32) + gate_ref[...] * update.reshape(rows, cols, dim)).astype(BF16)


def finish(pick, pair_tile, gate, candidates, w_out, blk=24):
    rows, cols, dim = pair_tile.shape
    half_rows, half_cols = rows // 2, cols // 2
    blk = min(blk, half_rows)
    per = half_rows // blk
    tri = w_out.shape[0]

    def y_spec(half, cand):
        def index(s, g, j, pick_ref):
            on = (s == half) & (pick_ref[half] == cand)
            return jnp.where(on, g, 0), jnp.where(on, j ^ half, 0), 0

        return pl.BlockSpec((blk, half_cols, tri), index)

    tile_spec = pl.BlockSpec((blk, half_cols, dim), lambda s, g, j, pick_ref: (s * per + g, j, 0))
    y_specs = [y_spec(s, q) for s in (0, 1) for q in range(len(candidates[s]))]
    return pl.pallas_call(
        finish_kernel,
        grid_spec=pltpu.PrefetchScalarGridSpec(
            num_scalar_prefetch=1,
            grid=(2, per, 2),
            in_specs=[tile_spec, tile_spec] + y_specs + [pl.BlockSpec(w_out.shape, lambda s, g, j, pick_ref: (0, 0))],
            out_specs=tile_spec,
        ),
        out_shape=jax.ShapeDtypeStruct(pair_tile.shape, BF16),
        compiler_params=params(),
        cost_estimate=cost(16, 10 * rows * cols * dim),
        name='finish',
    )(pick, pair_tile, gate, *candidates[0], *candidates[1], w_out)


def solution(mesh):
    tile_spec = P(('batch', 'row'), 'col', None)
    mask_spec = P(('batch', 'row'), 'col')
    replicated = P()

    def local_step(pair_tile, mask_tile, ln_in_scale, w_left, w_left_gate, w_right, w_right_gate, w_out_gate, ln_out_scale, w_out):
        _, cols, _ = pair_tile.shape
        half_cols = cols // 2
        tri = w_left.shape[1]
        row, z = lax.axis_index('row'), lax.axis_index('col')
        y, c = row // 2, row % 2
        half = z // 2
        w_a = jnp.concatenate([w_left, w_left_gate], axis=1).T
        w_b = jnp.concatenate([w_right, w_right_gate], axis=1).T
        gain_in, gain_out = ln_in_scale[None], ln_out_scale[None]

        masked = jnp.where((mask_tile != 0)[:, :, None], pair_tile, jnp.zeros((), BF16))
        t_a = jnp.where(y == 0, masked[:, :half_cols], masked[:, half_cols:])
        t_b = jnp.where(y == 0, masked[:, half_cols:], masked[:, :half_cols])
        gate = out_gate(pair_tile, gain_in, w_out_gate)
        y_a = send(t_b, TO_Y)
        z_a = send(t_a, TO_Z)
        m_0 = send(t_a, ACROSS)
        y_b = send(after(t_a, z_a), TO_Y)
        yz_a = send(after(y_a, gate), TO_Z)
        m_1 = send(y_a, ACROSS)
        z_b = send(after(t_b, yz_a), TO_Z)
        yz_b = send(after(z_a, y_b), TO_Y)

        keep = ((z % 2) == c).astype(jnp.int32)[None]
        sets = [((t_a, y_a), (z_a, yz_a)), ((t_b, y_b), (z_b, yz_b))]
        a_1 = project((z_a, yz_a), gain_in, w_a, n_out=2)
        a_1_own = [send(part, ACROSS) for part in a_1]
        give_0 = project_pick(1 - keep, *sets[0], gain_in, after(w_b, a_1[0]))
        a_0_own, = project((m_0, m_1), gain_in, after(w_a, give_0))
        a_0_sib = send(a_0_own, TO_CORE)
        keep_0 = project_pick(keep, *sets[0], gain_in, after(w_b, a_0_own))
        give_1 = project_pick(1 - keep, *sets[1], gain_in, after(w_b, keep_0))
        keep_1 = project_pick(keep, *sets[1], gain_in, after(w_b, give_1))
        b_parts = [keep_0, keep_1, send(give_0, TO_CORE), send(give_1, TO_CORE)]

        done_0 = triangle((a_0_own, a_0_sib), b_parts, gain_out)
        a_2_sib = send(a_1_own[0], TO_CORE)
        part_1 = triangle((after(a_1_own[0], done_0), a_2_sib), b_parts, gain_out, last=False)
        a_3_sib = send(after(a_1_own[1], part_1[0]), TO_CORE)
        done_1 = triangle((a_1_own[1], a_3_sib), b_parts, gain_out, first=tri // 2, prev=part_1)
        done = (done_0, done_1)

        got = [[send(done[turn], home(from_y, turn)) for turn in (0, 1)] for from_y in (0, 1)]
        inner = (z == 1) | (z == 2)
        block_half = jnp.where(inner, 1 - half, half)
        turn = half ^ c
        own = (block_half == y) & (2 * half + c == z)
        pick = jnp.stack([turn + jnp.where(own & (y == from_y), 2, 0) for from_y in (0, 1)]).astype(jnp.int32)
        return finish(pick, pair_tile, gate, [list(got[from_y]) + list(done) for from_y in (0, 1)], w_out)

    return jax.shard_map(local_step, mesh=mesh, in_specs=(tile_spec, mask_spec) + (replicated,) * 8, out_specs=tile_spec, check_vma=False)
```

profile of v0, /device:TPU:9, one launch (start us, length us, event | category | flops | bytes accessed | tf_op | source)
XLA Modules:
  0.0 738.0 jit_solution(9204588747889772387)
XLA Ops:
  0.0 1.0 broadcast_compare_fusion
  1.0 8.0 %broadcast_select_fusion = bf16[192,192,128]{2,1,0:T(8,128)(2,1)S(1)} fusion(bf16[192,192,128]{2,1,0:T(8,128)(2,1)} %z_ref.3, pred[192,192]{1,0:T(8,128)(4,1)S(1)} %broadcast_compare_fusion), kind=kLoop, calls=%fused_computation | loop fusion | flops 4718592 | bytes 18911232 | tf_op jit(solution)/shard_map/jit(_where)/select_n | solution.py:290
  8.9 3.9 broadcast_select_fusion.1
  12.8 0.0 collective-permute-start.3
  12.8 1.4 collective-permute-start.1
  14.3 0.0 copy-start
  14.3 18.9 %out_gate.1.gate_ref = f32[192,192,128]{2,1,0:T(8,128)} custom-call(bf16[192,192,128]{2,1,0:T(8,128)(2,1)} %z_ref.3, bf16[1,128]{1,0:T(2,128)(2,1)} %bitcast.9, bf16[128,128]{1,0:T(8,128)(2,1)} %wg_ref.1), custom_call_target="tpu_custom_call" | custom-call | flops 90000000 | bytes 28311552 | tf_op jit(solution)/shard_map/out_gate/pallas_call | solution.py:218
  33.2 82.7 %collective-permute-done.3.p0_ref.q0_ref = bf16[192,96,128]{2,1,0:T(8,128)(2,1)} collective-permute-done((bf16[192,96,128]{2,1,0:T(8,128)(2,1)}, bf16[192,96,128]{2,1,0:T(8,128)(2,1)}, u32[]{:S(2)}, u32[]{:S(2)}) %collective-permute-start.3) | collective-permute-done | bytes 4718624 | tf_op jit(solution)/shard_map/ppermute | solution.py:46
  115.9 1.2 collective-permute-start.6
  117.1 0.0 collective-permute-done.1.p1_ref
  117.1 0.2 collective-permute-start.4
  117.3 4.3 collective-permute-start
  121.6 2.1 collective-permute-start.2
  123.7 94.3 %collective-permute-done.6.p1_ref = bf16[192,96,128]{2,1,0:T(8,128)(2,1)} collective-permute-done((bf16[192,96,128]{2,1,0:T(8,128)(2,1)}, bf16[192,96,128]{2,1,0:T(8,128)(2,1)}, u32[]{:S(2)}, u32[]{:S(2)}) %collective-permute-start.6) | collective-permute-done | bytes 4718624 | tf_op jit(solution)/shard_map/ppermute | solution.py:46
  218.0 1.2 collective-permute-start.8
  219.2 0.0 collective-permute-done.4.p1_ref.q1_ref
  219.2 0.2 collective-permute-start.7
  219.4 0.0 copy-done
  219.4 0.1 copy.11
  219.5 0.0 copy-done.1
  219.5 0.1 copy.12
  219.7 0.0 copy-done.2
  219.7 0.1 copy.13
  219.8 0.0 copy-done.3
  219.8 0.1 copy.14
  219.9 0.6 maximum_bitcast_fusion.w_ref
  220.6 0.6 maximum_bitcast_fusion.1.w_ref
  221.2 21.7 %project.2 = (bf16[64,96,384]{2,1,0:T(8,128)(2,1)}, bf16[64,96,384]{2,1,0:T(8,128)(2,1)}) custom-call(bf16[192,96,128]{2,1,0:T(8,128)(2,1)} %collective-permute-done.3.p0_ref.q0_ref, bf16[192,96,128]{2,1,0:T(8,128)(2,1)} %collective-permute-done.4.p1_ref.q1_ref, bf16[1,128]{1,0:T(2,128)(2,1)} %bitcast.10, bf16[256,128]{1,0:T(8,128)(2,1)} %maximum_bitcast_fusion.w_ref), custom_call_target="tpu_custom_call" | custom-call | flops 115000000 | bytes 18874368 | tf_op jit(solution)/shard_map/project/pallas_call | solution.py:98
  242.9 23.1 %project_pick.4 = bf16[128,96,384]{2,1,0:T(8,128)(2,1)} custom-call(s32[1]{0:T(128)S(6)} %sub.17.flag_ref, bf16[192,96,128]{2,1,0:T(8,128)(2,1)} %get-tuple-element.25.p0_ref, bf16[192,96,128]{2,1,0:T(8,128)(2,1)} %collective-permute-done.1.p1_ref, bf16[192,96,128]{2,1,0:T(8,128)(2,1)} %collective-permute-done.3.p0_ref.q0_ref, ...), custom_call_target="tpu_custom_call" | custom-call | flops 115000000 | bytes 18874368 | tf_op jit(solution)/shard_map/project_pick/pallas_call | solution.py:116
  266.0 0.0 collective-permute-done.p0_ref
  266.0 57.1 %collective-permute-done.2.p1_ref = bf16[192,96,128]{2,1,0:T(8,128)(2,1)} collective-permute-done((bf16[192,96,128]{2,1,0:T(8,128)(2,1)}, bf16[192,96,128]{2,1,0:T(8,128)(2,1)}, u32[]{:S(2)}, u32[]{:S(2)}) %collective-permute-start.2) | collective-permute-done | bytes 4718624 | tf_op jit(solution)/shard_map/ppermute | solution.py:46
  323.1 21.5 %project.3.refs_0_ = bf16[128,96,384]{2,1,0:T(8,128)(2,1)} custom-call(bf16[192,96,128]{2,1,0:T(8,128)(2,1)} %collective-permute-done.p0_ref, bf16[192,96,128]{2,1,0:T(8,128)(2,1)} %collective-permute-done.2.p1_ref, bf16[1,128]{1,0:T(2,128)(2,1)} %bitcast.12, bf16[256,128]{1,0:T(8,128)(2,1)} %maximum_bitcast_fusion.w_ref), custom_call_target="tpu_custom_call" | custom-call | flops 115000000 | bytes 18874368 | tf_op jit(solution)/shard_map/project/pallas_call | solution.py:98
  344.6 2.7 collective-permute-start.5
  347.3 0.0 collective-permute-start.9
  347.3 23.2 %project_pick.5.refs_2_ = bf16[128,96,384]{2,1,0:T(8,128)(2,1)} custom-call(s32[1]{0:T(128)} %bitcast.4.flag_ref, bf16[192,96,128]{2,1,0:T(8,128)(2,1)} %get-tuple-element.25.p0_ref, bf16[192,96,128]{2,1,0:T(8,128)(2,1)} %collective-permute-done.1.p1_ref, bf16[192,96,128]{2,1,0:T(8,128)(2,1)} %collective-permute-done.3.p0_ref.q0_ref, ...), custom_call_target="tpu_custom_call" | custom-call | flops 115000000 | bytes 18874368 | tf_op jit(solution)/shard_map/project_pick/pallas_call | solution.py:116
  370.5 0.0 collective-permute-done.8.q1_ref
  370.5 0.0 collective-permute-done.7.q0_ref
  370.5 23.1 %project_pick.6 = bf16[128,96,384]{2,1,0:T(8,128)(2,1)} custom-call(s32[1]{0:T(128)S(6)} %sub.17.flag_ref, bf16[192,96,128]{2,1,0:T(8,128)(2,1)} %get-tuple-element.26.p0_ref, bf16[192,96,128]{2,1,0:T(8,128)(2,1)} %collective-permute-done.6.p1_ref, bf16[192,96,128]{2,1,0:T(8,128)(2,1)} %collective-permute-done.7.q0_ref, ...), custom_call_target="tpu_custom_call" | custom-call | flops 115000000 | bytes 18874368 | tf_op jit(solution)/shard_map/project_pick/pallas_call | solution.py:116
  393.6 0.2 collective-permute-start.10
  393.8 3.4 collective-permute-start.13
  397.2 101.9 %collective-permute-done.13.refs_0_ = bf16[64,96,384]{2,1,0:T(8,128)(2,1)} collective-permute-done((bf16[64,96,384]{2,1,0:T(8,128)(2,1)}, bf16[64,96,384]{2,1,0:T(8,128)(2,1)}, u32[]{:S(2)}, u32[]{:S(2)}) %collective-permute-start.13) | collective-permute-done | bytes 4718624 | tf_op jit(solution)/shard_map/ppermute | solution.py:46
  499.1 1.1 collective-permute-start.14
  500.3 3.4 collective-permute-start.12
  503.6 23.0 %project_pick.7.refs_3_ = bf16[128,96,384]{2,1,0:T(8,128)(2,1)} custom-call(s32[1]{0:T(128)} %bitcast.4.flag_ref, bf16[192,96,128]{2,1,0:T(8,128)(2,1)} %get-tuple-element.26.p0_ref, bf16[192,96,128]{2,1,0:T(8,128)(2,1)} %collective-permute-done.6.p1_ref, bf16[192,96,128]{2,1,0:T(8,128)(2,1)} %collective-permute-done.7.q0_ref, ...), custom_call_target="tpu_custom_call" | custom-call | flops 115000000 | bytes 18874368 | tf_op jit(solution)/shard_map/project_pick/pallas_call | solution.py:116
  526.6 0.0 collective-permute-done.5.refs_1_
  526.6 0.0 collective-permute-done.9.refs_4_
  526.6 0.0 collective-permute-done.10.refs_5_
  526.6 44.6 %triangle.3.refs_2_.refs_6_ = bf16[96,192,128]{2,1,0:T(8,128)(2,1)} custom-call(bf16[128,96,384]{2,1,0:T(8,128)(2,1)} %project.3.refs_0_, bf16[128,96,384]{2,1,0:T(8,128)(2,1)} %collective-permute-done.5.refs_1_, bf16[128,96,384]{2,1,0:T(8,128)(2,1)} %project_pick.5.refs_2_, bf16[128,96,384]{2,1,0:T(8,128)(2,1)} %project_pick.7.refs_3_, ...), custom_call_target="tpu_custom_call" | custom-call | flops 225000000 | bytes 56623104 | tf_op jit(solution)/shard_map/triangle/pallas_call | solution.py:195
  571.3 0.0 collective-permute-done.14.refs_1_
  571.3 16.4 %triangle.4 = (f32[6656,128]{1,0:T(8,128)}, f32[6656,128]{1,0:T(8,128)}) custom-call(bf16[64,96,384]{2,1,0:T(8,128)(2,1)} %collective-permute-done.13.refs_0_, bf16[64,96,384]{2,1,0:T(8,128)(2,1)} %collective-permute-done.14.refs_1_, bf16[128,96,384]{2,1,0:T(8,128)(2,1)} %project_pick.5.refs_2_, bf16[128,96,384]{2,1,0:T(8,128)(2,1)} %project_pick.7.refs_3_, ...), custom_call_target="tpu_custom_call" | custom-call | flops 75000000 | bytes 28311552 | tf_op jit(solution)/shard_map/triangle/pallas_call | solution.py:195
  587.7 18.1 %collective-permute-done.12.refs_0_ = bf16[64,96,384]{2,1,0:T(8,128)(2,1)} collective-permute-done((bf16[64,96,384]{2,1,0:T(8,128)(2,1)}, bf16[64,96,384]{2,1,0:T(8,128)(2,1)}, u32[]{:S(2)}, u32[]{:S(2)}) %collective-permute-start.12) | collective-permute-done | bytes 4718624 | tf_op jit(solution)/shard_map/ppermute | solution.py:46
  605.8 0.9 collective-permute-start.15
  606.7 4.1 collective-permute-start.11
  610.8 2.8 collective-permute-start.17
  613.6 0.9 collective-permute-done.15.refs_1_
  614.6 33.4 %triangle.5.refs_3_.refs_7_ = bf16[96,192,128]{2,1,0:T(8,128)(2,1)} custom-call(bf16[64,96,384]{2,1,0:T(8,128)(2,1)} %collective-permute-done.12.refs_0_, bf16[64,96,384]{2,1,0:T(8,128)(2,1)} %collective-permute-done.15.refs_1_, bf16[128,96,384]{2,1,0:T(8,128)(2,1)} %project_pick.5.refs_2_, bf16[128,96,384]{2,1,0:T(8,128)(2,1)} %project_pick.7.refs_3_, ...), custom_call_target="tpu_custom_call" | custom-call | flops 150000000 | bytes 28311552 | tf_op jit(solution)/shard_map/triangle/pallas_call | solution.py:195
  648.0 2.1 collective-permute-start.16
  650.1 1.3 collective-permute-start.18
  651.4 0.7 pad_add_fusion.pick_ref
  652.1 8.0 %collective-permute-done.11.refs_0_ = bf16[96,192,128]{2,1,0:T(8,128)(2,1)} collective-permute-done((bf16[96,192,128]{2,1,0:T(8,128)(2,1)}, bf16[96,192,128]{2,1,0:T(8,128)(2,1)}, u32[]{:S(2)}, u32[]{:S(2)}) %collective-permute-start.11) | collective-permute-done | bytes 4718624 | tf_op jit(solution)/shard_map/ppermute | solution.py:46
  660.1 0.0 collective-permute-done.17.refs_4_
  660.1 52.2 %collective-permute-done.16.refs_1_ = bf16[96,192,128]{2,1,0:T(8,128)(2,1)} collective-permute-done((bf16[96,192,128]{2,1,0:T(8,128)(2,1)}, bf16[96,192,128]{2,1,0:T(8,128)(2,1)}, u32[]{:S(2)}, u32[]{:S(2)}) %collective-permute-start.16) | collective-permute-done | bytes 4718624 | tf_op jit(solution)/shard_map/ppermute | solution.py:46
  712.3 2.8 collective-permute-done.18.refs_5_
  715.1 22.9 %finish.1 = bf16[192,192,128]{2,1,0:T(8,128)(2,1)} custom-call(s32[2]{0:T(128)} %pad_add_fusion.pick_ref, bf16[192,192,128]{2,1,0:T(8,128)(2,1)} %z_ref.3, f32[192,192,128]{2,1,0:T(8,128)} %out_gate.1.gate_ref, bf16[96,192,128]{2,1,0:T(8,128)(2,1)} %collective-permute-done.11.refs_0_, bf16[96,192,128]{2,1,0:T(8,128)(2,1)} %collective-permute-done.16.refs_1_, ...), custom_call_target="tpu_custom_call" | custom-call | flops 80000000 | bytes 47185920 | tf_op jit(solution)/shard_map/finish/pallas_call | solution.py:259
  (3 shorter events, 0.0 us)
Async XLA Ops:
  12.8 103.0 %collective-permute-start.3 = (bf16[192,96,128]{2,1,0:T(8,128)(2,1)}, bf16[192,96,128]{2,1,0:T(8,128)(2,1)}, u32[]{:S(2)}, u32[]{:S(2)}) collective-permute-start(bf16[192,96,128]{2,1,0:T(8,128)(2,1)} %get-tuple-element.25.p0_ref), channel_id=1, source_target_pairs={{0,4},{1,5},{2,6},{3,7},{4,0},{5,1},{6,2},{7,3},{8,12},{9,13},{10,... | collective-permute-start | bytes 14155784 | tf_op jit(solution)/shard_map/ppermute | solution.py:46
  12.8 104.2 %collective-permute-start.1 = (bf16[192,96,128]{2,1,0:T(8,128)(2,1)}, bf16[192,96,128]{2,1,0:T(8,128)(2,1)}, u32[]{:S(2)}, u32[]{:S(2)}) collective-permute-start(bf16[192,96,128]{2,1,0:T(8,128)(2,1)} %get-tuple-element.26.p0_ref), channel_id=1, source_target_pairs={{0,2},{1,3},{2,0},{3,1},{4,6},{5,7},{6,4},{7,5},{8,10},{9,11},{10,... | collective-permute-start | bytes 14155784 | tf_op jit(solution)/shard_map/ppermute | solution.py:46
  14.3 205.2 %copy-start = (bf16[128,128]{1,0:T(8,128)(2,1)S(1)}, bf16[128,128]{1,0:T(8,128)(2,1)}, u32[]{:S(2)}) copy-start(bf16[128,128]{1,0:T(8,128)(2,1)} %param.13) | copy-start | bytes 98308
  14.3 205.3 %copy-start.1 = (bf16[128,128]{1,0:T(8,128)(2,1)S(1)}, bf16[128,128]{1,0:T(8,128)(2,1)}, u32[]{:S(2)}) copy-start(bf16[128,128]{1,0:T(8,128)(2,1)} %param.14) | copy-start | bytes 98308
  14.3 205.4 %copy-start.2 = (bf16[128,128]{1,0:T(8,128)(2,1)S(1)}, bf16[128,128]{1,0:T(8,128)(2,1)}, u32[]{:S(2)}) copy-start(bf16[128,128]{1,0:T(8,128)(2,1)} %param.15) | copy-start | bytes 98308
  14.3 205.5 %copy-start.3 = (bf16[128,128]{1,0:T(8,128)(2,1)S(1)}, bf16[128,128]{1,0:T(8,128)(2,1)}, u32[]{:S(2)}) copy-start(bf16[128,128]{1,0:T(8,128)(2,1)} %param.16) | copy-start | bytes 98308
  115.9 102.2 %collective-permute-start.6 = (bf16[192,96,128]{2,1,0:T(8,128)(2,1)}, bf16[192,96,128]{2,1,0:T(8,128)(2,1)}, u32[]{:S(2)}, u32[]{:S(2)}) collective-permute-start(bf16[192,96,128]{2,1,0:T(8,128)(2,1)} %get-tuple-element.25.p0_ref), channel_id=1, source_target_pairs={{0,2},{1,3},{2,0},{3,1},{4,6},{5,7},{6,4},{7,5},{8,10},{9,11},{10,... | collective-permute-start | bytes 14155784 | tf_op jit(solution)/shard_map/ppermute | solution.py:46
  117.1 102.2 %collective-permute-start.4 = (bf16[192,96,128]{2,1,0:T(8,128)(2,1)}, bf16[192,96,128]{2,1,0:T(8,128)(2,1)}, u32[]{:S(2)}, u32[]{:S(2)}) collective-permute-start(bf16[192,96,128]{2,1,0:T(8,128)(2,1)} %collective-permute-done.1.p1_ref), channel_id=1, source_target_pairs={{0,4},{1,5},{2,6},{3,7},{4,0},{5,1},{6,2},{7,3},{8,12},{9,13},{10,... | collective-permute-start | bytes 14155784 | tf_op jit(solution)/shard_map/ppermute | solution.py:46
  117.3 148.7 %collective-permute-start = (bf16[192,96,128]{2,1,0:T(8,128)(2,1)}, bf16[192,96,128]{2,1,0:T(8,128)(2,1)}, u32[]{:S(2)}, u32[]{:S(2)}) collective-permute-start(bf16[192,96,128]{2,1,0:T(8,128)(2,1)} %get-tuple-element.25.p0_ref), channel_id=1, source_target_pairs={{0,0},{1,1},{2,2},{3,3},{4,8},{5,9},{6,10},{7,11},{8,4},{9,5},{10,... | collective-permute-start | bytes 14155784 | tf_op jit(solution)/shard_map/ppermute | solution.py:46
  121.6 201.5 %collective-permute-start.2 = (bf16[192,96,128]{2,1,0:T(8,128)(2,1)}, bf16[192,96,128]{2,1,0:T(8,128)(2,1)}, u32[]{:S(2)}, u32[]{:S(2)}) collective-permute-start(bf16[192,96,128]{2,1,0:T(8,128)(2,1)} %collective-permute-done.1.p1_ref), channel_id=1, source_target_pairs={{0,0},{1,1},{2,2},{3,3},{4,8},{5,9},{6,10},{7,11},{8,4},{9,5},{10,... | collective-permute-start | bytes 14155784 | tf_op jit(solution)/shard_map/ppermute | solution.py:46
  218.0 152.5 %collective-permute-start.8 = (bf16[192,96,128]{2,1,0:T(8,128)(2,1)}, bf16[192,96,128]{2,1,0:T(8,128)(2,1)}, u32[]{:S(2)}, u32[]{:S(2)}) collective-permute-start(bf16[192,96,128]{2,1,0:T(8,128)(2,1)} %collective-permute-done.3.p0_ref.q0_ref), channel_id=1, source_target_pairs={{0,2},{1,3},{2,0},{3,1},{4,6},{5,7},{6,4},{7,5},{8,10},{9,11},{10,... | collective-permute-start | bytes 14155784 | tf_op jit(solution)/shard_map/ppermute | solution.py:46
  219.2 151.3 %collective-permute-start.7 = (bf16[192,96,128]{2,1,0:T(8,128)(2,1)}, bf16[192,96,128]{2,1,0:T(8,128)(2,1)}, u32[]{:S(2)}, u32[]{:S(2)}) collective-permute-start(bf16[192,96,128]{2,1,0:T(8,128)(2,1)} %get-tuple-element.26.p0_ref), channel_id=1, source_target_pairs={{0,4},{1,5},{2,6},{3,7},{4,0},{5,1},{6,2},{7,3},{8,12},{9,13},{10,... | collective-permute-start | bytes 14155784 | tf_op jit(solution)/shard_map/ppermute | solution.py:46
  344.6 182.0 %collective-permute-start.5 = (bf16[128,96,384]{2,1,0:T(8,128)(2,1)}, bf16[128,96,384]{2,1,0:T(8,128)(2,1)}, u32[]{:S(2)}, u32[]{:S(2)}) collective-permute-start(bf16[128,96,384]{2,1,0:T(8,128)(2,1)} %project.3.refs_0_), channel_id=1, source_target_pairs={{0,1},{1,0},{2,3},{3,2},{4,5},{5,4},{6,7},{7,6},{8,9},{9,8},{10,11... | collective-permute-start | bytes 28311560 | tf_op jit(solution)/shard_map/ppermute | solution.py:46
  347.3 179.3 %collective-permute-start.9 = (bf16[128,96,384]{2,1,0:T(8,128)(2,1)}, bf16[128,96,384]{2,1,0:T(8,128)(2,1)}, u32[]{:S(2)}, u32[]{:S(2)}) collective-permute-start(bf16[128,96,384]{2,1,0:T(8,128)(2,1)} %project_pick.4), channel_id=1, source_target_pairs={{0,1},{1,0},{2,3},{3,2},{4,5},{5,4},{6,7},{7,6},{8,9},{9,8},{10,11... | collective-permute-start | bytes 28311560 | tf_op jit(solution)/shard_map/ppermute | solution.py:46
  393.6 133.0 %collective-permute-start.10 = (bf16[128,96,384]{2,1,0:T(8,128)(2,1)}, bf16[128,96,384]{2,1,0:T(8,128)(2,1)}, u32[]{:S(2)}, u32[]{:S(2)}) collective-permute-start(bf16[128,96,384]{2,1,0:T(8,128)(2,1)} %project_pick.6), channel_id=1, source_target_pairs={{0,1},{1,0},{2,3},{3,2},{4,5},{5,4},{6,7},{7,6},{8,9},{9,8},{10,11... | collective-permute-start | bytes 28311560 | tf_op jit(solution)/shard_map/ppermute | solution.py:46
  393.8 105.3 %collective-permute-start.13 = (bf16[64,96,384]{2,1,0:T(8,128)(2,1)}, bf16[64,96,384]{2,1,0:T(8,128)(2,1)}, u32[]{:S(2)}, u32[]{:S(2)}) collective-permute-start(bf16[64,96,384]{2,1,0:T(8,128)(2,1)} %get-tuple-element.21), channel_id=1, source_target_pairs={{0,0},{1,1},{2,2},{3,3},{4,8},{5,9},{6,10},{7,11},{8,4},{9,5},{10,... | collective-permute-start | bytes 14155784 | tf_op jit(solution)/shard_map/ppermute | solution.py:46
  499.1 72.1 %collective-permute-start.14 = (bf16[64,96,384]{2,1,0:T(8,128)(2,1)}, bf16[64,96,384]{2,1,0:T(8,128)(2,1)}, u32[]{:S(2)}, u32[]{:S(2)}) collective-permute-start(bf16[64,96,384]{2,1,0:T(8,128)(2,1)} %collective-permute-done.13.refs_0_), channel_id=1, source_target_pairs={{0,1},{1,0},{2,3},{3,2},{4,5},{5,4},{6,7},{7,6},{8,9},{9,8},{10,11... | collective-permute-start | bytes 14155784 | tf_op jit(solution)/shard_map/ppermute | solution.py:46
  500.3 105.6 %collective-permute-start.12 = (bf16[64,96,384]{2,1,0:T(8,128)(2,1)}, bf16[64,96,384]{2,1,0:T(8,128)(2,1)}, u32[]{:S(2)}, u32[]{:S(2)}) collective-permute-start(bf16[64,96,384]{2,1,0:T(8,128)(2,1)} %get-tuple-element.30), channel_id=1, source_target_pairs={{0,0},{1,1},{2,2},{3,3},{4,8},{5,9},{6,10},{7,11},{8,4},{9,5},{10,... | collective-permute-start | bytes 14155784 | tf_op jit(solution)/shard_map/ppermute | solution.py:46
  605.8 8.7 %collective-permute-start.15 = (bf16[64,96,384]{2,1,0:T(8,128)(2,1)}, bf16[64,96,384]{2,1,0:T(8,128)(2,1)}, u32[]{:S(2)}, u32[]{:S(2)}) collective-permute-start(bf16[64,96,384]{2,1,0:T(8,128)(2,1)} %collective-permute-done.12.refs_0_), channel_id=1, source_target_pairs={{0,1},{1,0},{2,3},{3,2},{4,5},{5,4},{6,7},{7,6},{8,9},{9,8},{10,11... | collective-permute-start | bytes 14155784 | tf_op jit(solution)/shard_map/ppermute | solution.py:46
  606.7 53.4 %collective-permute-start.11 = (bf16[96,192,128]{2,1,0:T(8,128)(2,1)}, bf16[96,192,128]{2,1,0:T(8,128)(2,1)}, u32[]{:S(2)}, u32[]{:S(2)}) collective-permute-start(bf16[96,192,128]{2,1,0:T(8,128)(2,1)} %triangle.3.refs_2_.refs_6_), channel_id=1, source_target_pairs={{1,4},{4,2},{5,6},{8,9},{9,13},{12,11},{13,15},{17,20},{20,18},{21... | collective-permute-start | bytes 14155784 | tf_op jit(solution)/shard_map/ppermute | solution.py:46
  610.8 49.2 %collective-permute-start.17 = (bf16[96,192,128]{2,1,0:T(8,128)(2,1)}, bf16[96,192,128]{2,1,0:T(8,128)(2,1)}, u32[]{:S(2)}, u32[]{:S(2)}) collective-permute-start(bf16[96,192,128]{2,1,0:T(8,128)(2,1)} %triangle.3.refs_2_.refs_6_), channel_id=1, source_target_pairs={{2,0},{3,4},{6,2},{7,6},{10,9},{11,13},{14,11},{18,16},{19,20},{22... | collective-permute-start | bytes 14155784 | tf_op jit(solution)/shard_map/ppermute | solution.py:46
  648.0 64.3 %collective-permute-start.16 = (bf16[96,192,128]{2,1,0:T(8,128)(2,1)}, bf16[96,192,128]{2,1,0:T(8,128)(2,1)}, u32[]{:S(2)}, u32[]{:S(2)}) collective-permute-start(bf16[96,192,128]{2,1,0:T(8,128)(2,1)} %triangle.5.refs_3_.refs_7_), channel_id=1, source_target_pairs={{0,1},{1,5},{4,3},{5,7},{9,12},{12,10},{13,14},{16,17},{17,21},{20... | collective-permute-start | bytes 14155784 | tf_op jit(solution)/shard_map/ppermute | solution.py:46
  650.1 65.0 %collective-permute-start.18 = (bf16[96,192,128]{2,1,0:T(8,128)(2,1)}, bf16[96,192,128]{2,1,0:T(8,128)(2,1)}, u32[]{:S(2)}, u32[]{:S(2)}) collective-permute-start(bf16[96,192,128]{2,1,0:T(8,128)(2,1)} %triangle.5.refs_3_.refs_7_), channel_id=1, source_target_pairs={{2,1},{3,5},{6,3},{10,8},{11,12},{14,10},{15,14},{18,17},{19,21},{... | collective-permute-start | bytes 14155784 | tf_op jit(solution)/shard_map/ppermute | solution.py:46
where the time goes:
time: 749 us; the launch traced here: 738 us
  waiting for transfers between devices  418 us (56%)
  Pallas kernels  272 us (36%)
  starting transfers between devices  32.6 us (4%)
  other arithmetic  14.7 us (2%)
    ppermute x19, waiting for transfers between devices, send(): return lax.ppermute(value, AXES, pairs)  418 us
    pallas_call x3, Pallas kernels, triangle(): pl.pallas_call(lambda *refs: triangle_kernel(n_prev, last, *refs), grid=(...  94.5 us
    pallas_call x4, Pallas kernels, project_pick(): pl.pallas_call(project_pick_kernel, grid_spec=pltpu.PrefetchScalarGridSpe...  92.3 us
    pallas_call x2, Pallas kernels, project(): pl.pallas_call(project_kernel, grid=(cols // blk,), in_specs=[pl.BlockSpe...  43.3 us
    ppermute x19, starting transfers between devices, send(): return lax.ppermute(value, AXES, pairs)  32.6 us
    pallas_call x1, Pallas kernels, finish(): pl.pallas_call(finish_kernel, grid_spec=pltpu.PrefetchScalarGridSpec(num_...  22.9 us
    pallas_call x1, Pallas kernels, out_gate(): pl.pallas_call(gate_kernel, grid=(rows // blk,), in_specs=[spec, pl.Block...  18.9 us
  transfers between devices with their start and end apart: 19, of which 9 were waited for; matrix products, arithmetic and copies ran while one was open for 0% of the time, Pallas kernels for 34%

commit v1 on v0

v1 whole, which is shorter than its diff:
```python
import jax
import jax.numpy as jnp
from jax import lax
from jax.experimental import pallas as pl
from jax.experimental.pallas import tpu as pltpu
from jax.sharding import PartitionSpec as P


LN_EPS = 0.00001
AXES = ('col', 'row')
BF16, F32 = jnp.bfloat16, jnp.float32
VMEM_BYTES = 60 * 2**20
FLOPS_PER_US = 5_000_000


def moves(target):
    pairs = []
    for z in range(4):
        for y in range(2):
            for c in range(2):
                to = target(y, z, c)
                if to is not None:
                    pairs.append((z * 4 + y * 2 + c, to[1] * 4 + to[0] * 2 + to[2]))
    return pairs


TO_Y = moves(lambda y, z, c: (1 - y, z, c))
TO_Z = moves(lambda y, z, c: (y, z ^ 1, c))
TO_CORE = moves(lambda y, z, c: (y, z, 1 - c))
ACROSS = moves(lambda y, z, c: (y, 3 - z, c) if z in (1, 2) else None)
INNER_CORE = moves(lambda y, z, c: (y, z, 1 - c) if z in (1, 2) else None)
OUTER_CORE = moves(lambda y, z, c: (y, z, 1 - c) if z in (0, 3) else None)


def home(from_y, turn):
    def target(y, z, c):
        if y != from_y:
            return None
        half = z // 2
        block_half = 1 - half if z in (1, 2) else half
        to = (block_half, 2 * half + c, half ^ turn)
        return None if to == (y, z, c) else to

    return moves(target)


def send(value, pairs):
    return lax.ppermute(value, AXES, pairs)


def after(value, *others):
    return lax.optimization_barrier((value,) + others)[0]


def cost(us, nbytes):
    return pl.CostEstimate(flops=us * FLOPS_PER_US, bytes_accessed=nbytes, transcendentals=0)


def params():
    return pltpu.CompilerParams(vmem_limit_bytes=VMEM_BYTES)


def normed(values, gain):
    mean_val = jnp.mean(values, axis=-1, keepdims=True)
    centered = values - mean_val
    variance = jnp.mean(centered * centered, axis=-1, keepdims=True)
    return (centered * lax.rsqrt(variance + LN_EPS) * gain).astype(BF16)


def dot_nt(lhs, rhs):
    return lax.dot_general(lhs, rhs, (((1,), (1,)), ((), ())), preferred_element_type=F32)


def project_body(pieces, gain_ref, w_ref, out_ref, s_ref):
    tri = s_ref.shape[1]
    gain = gain_ref[...].astype(F32)
    x = jnp.concatenate([normed(p.astype(F32), gain) for p in pieces], axis=0)
    x = jnp.swapaxes(x, 0, 1)
    for i in range(x.shape[0]):
        proj = dot_nt(w_ref[...], x[i])
        s_ref[i] = jax.nn.sigmoid(proj[tri:]) * proj[:tri]
    out_ref[...] = jnp.swapaxes(s_ref[...], 0, 1).astype(BF16)


def project_kernel(flag_ref, *refs):
    *piece_refs, gain_ref, w_ref, out_ref, s_ref = refs
    pieces = [ref[...] for ref in piece_refs]
    if len(pieces) == 4:
        pick = flag_ref[0] != 0
        pieces = [jnp.where(pick, yes, no) for yes, no in zip(pieces[:2], pieces[2:])]
    project_body(pieces, gain_ref, w_ref, out_ref, s_ref)


def project(flag, yes, no, gain, w_t, first=0, count=None, blk=16):
    rows, cols, dim = yes[0].shape
    count = count or cols
    blk = min(blk, count)
    wide = w_t.shape[0]
    tri = wide // 2
    at = first // blk
    specs = [pl.BlockSpec((rows, blk, dim), lambda g, f: (0, at + g * f[0], 0) if no else (0, at + g, 0))] * 2
    if no:
        specs += [pl.BlockSpec((rows, blk, dim), lambda g, f: (0, at + g * (1 - f[0]), 0))] * 2
    whole = [pl.BlockSpec((1, dim), lambda g, f: (0, 0)), pl.BlockSpec((wide, dim), lambda g, f: (0, 0))]
    return pl.pallas_call(
        project_kernel,
        grid_spec=pltpu.PrefetchScalarGridSpec(
            num_scalar_prefetch=1,
            grid=(count // blk,),
            in_specs=specs + whole,
            out_specs=pl.BlockSpec((tri, blk, 2 * rows), lambda g, f: (0, g, 0)),
            scratch_shapes=[pltpu.VMEM((blk, tri, 2 * rows), F32)],
        ),
        out_shape=jax.ShapeDtypeStruct((tri, count, 2 * rows), BF16),
        compiler_params=params(),
        cost_estimate=cost(23 * count // cols, 4 * rows * count * (dim + tri)),
        name='project',
    )(flag, *yes, *(no or ()), gain, w_t)


def triangle_kernel(n_pair, flag_ref, *refs):
    a_refs, b_refs = refs[:2 * n_pair], refs[2 * n_pair:2 * n_pair + 4]
    gain_ref, out_ref, *o_refs = refs[2 * n_pair + 4:]
    step, steps = pl.program_id(0), pl.num_programs(0)
    n_h, n_i, _ = a_refs[0].shape
    n_j = out_ref.shape[1]
    tri, pitch = n_h * steps, n_i + 8
    spans = [(at, min(128, n_j - at)) for at in range(0, n_j, 128)]
    pick = flag_ref[0] != 0
    for h in range(n_h):
        a_0, a_1 = a_refs[0][h], a_refs[1][h]
        if n_pair == 2:
            a_0, a_1 = jnp.where(pick, a_0, a_refs[2][h]), jnp.where(pick, a_1, a_refs[3][h])
        acc = dot_nt(a_0, jnp.concatenate([b_refs[0][h], b_refs[1][h]], axis=0))
        acc += dot_nt(a_1, jnp.concatenate([b_refs[2][h], b_refs[3][h]], axis=0))
        start = pl.multiple_of((step * n_h + h) * pitch, 8)
        for (at, width), o_ref in zip(spans, o_refs):
            o_ref[pl.ds(start, n_i), :width] = acc[:, at:at + width]

    @pl.when(step == steps - 1)
    def _():
        gain = gain_ref[...].astype(F32)

        @pl.loop(0, n_i, step=4)
        def _(first):
            for i in range(4):
                for (at, width), o_ref in zip(spans, o_refs):
                    values = o_ref[pl.ds(first + i, tri, stride=pitch), :][:, :width]
                    mean_val = jnp.mean(values, axis=0, keepdims=True)
                    centered = values - mean_val
                    variance = jnp.mean(centered * centered, axis=0, keepdims=True)
                    unit = centered * lax.rsqrt(variance + LN_EPS)
                    out_ref[first + i, pl.ds(at, width), :] = (unit.T * gain).astype(BF16)


def triangle(flag, a_pairs, b_parts, gain, blk=8):
    n_pair = len(a_pairs)
    tri, n_i, n_k = a_pairs[0][0].shape
    half_j = b_parts[0].shape[1]
    n_j = 2 * half_j
    specs = []
    for q in range(n_pair):
        specs += [pl.BlockSpec((blk, n_i, n_k), lambda g, f, q=q: (jnp.where(f[0] == 1 - q, g, 0) if n_pair == 2 else g, 0, 0))] * 2
    return pl.pallas_call(
        lambda *refs: triangle_kernel(n_pair, *refs),
        grid_spec=pltpu.PrefetchScalarGridSpec(
            num_scalar_prefetch=1,
            grid=(tri // blk,),
            in_specs=specs + [pl.BlockSpec((blk, half_j, n_k), lambda g, f: (g, 0, 0))] * 4 + [pl.BlockSpec((1, tri), lambda g, f: (0, 0))],
            out_specs=pl.BlockSpec((n_i, n_j, tri), lambda g, f: (0, 0, 0)),
            scratch_shapes=[pltpu.VMEM((tri * (n_i + 8), 128), F32)] * pl.cdiv(n_j, 128),
        ),
        out_shape=jax.ShapeDtypeStruct((n_i, n_j, tri), BF16),
        compiler_params=params(),
        cost_estimate=cost(40, 2 * tri * n_k * 2 * (n_i + n_j)),
        name='triangle',
    )(flag, *[a for pair in a_pairs for a in pair], *b_parts, gain)


def gate_kernel(z_ref, gain_ref, wg_ref, out_ref):
    rows, cols, dim = z_ref.shape
    x = normed(z_ref[...].astype(F32).reshape(rows * cols, dim), gain_ref[...].astype(F32))
    out_ref[...] = jax.nn.sigmoid(jnp.dot(x, wg_ref[...], preferred_element_type=F32)).reshape(rows, cols, dim)


def out_gate(pair_tile, gain, w_gate, blk=16):
    rows, cols, dim = pair_tile.shape
    blk = min(blk, rows)
    spec = pl.BlockSpec((blk, cols, dim), lambda g: (g, 0, 0))
    return pl.pallas_call(
        gate_kernel,
        grid=(rows // blk,),
        in_specs=[spec, pl.BlockSpec((1, dim), lambda g: (0, 0)), pl.BlockSpec((dim, dim), lambda g: (0, 0))],
        out_specs=spec,
        out_shape=jax.ShapeDtypeStruct(pair_tile.shape, F32),
        compiler_params=params(),
        cost_estimate=cost(18, 6 * rows * cols * dim),
        name='out_gate',
    )(pair_tile, gain, w_gate)


def finish_kernel(n_cand, pick_ref, z_ref, gate_ref, *refs):
    y_refs, wo_ref, out_ref = refs[:2 * n_cand], refs[2 * n_cand], refs[-1]
    rows, cols, dim = z_ref.shape
    half_cols = cols // 2
    for s in (0, 1):
        for q in range(n_cand):
            @pl.when((pl.program_id(0) == s) & (pick_ref[s] == q))
            def _(s=s, y_ref=y_refs[s * n_cand + q]):
                for j in (0, 1):
                    to, at = pl.ds(j * half_cols, half_cols), pl.ds((j ^ s) * half_cols, half_cols)
                    update = jnp.dot(y_ref[:, at, :].reshape(rows * half_cols, -1), wo_ref[...], preferred_element_type=F32)
                    total = z_ref[:, to, :].astype(F32) + gate_ref[:, to, :] * update.reshape(rows, half_cols, dim)
                    out_ref[:, to, :] = total.astype(BF16)


def finish(pick, pair_tile, gate, candidates, w_out, part, so_far=None, blk=12):
    rows, cols, dim = pair_tile.shape
    half_rows = rows // 2
    quarter = half_rows // 2
    blk = blk if quarter % blk == 0 else quarter
    per = quarter // blk
    tri = w_out.shape[0]
    n_cand = len(candidates[0])

    def y_spec(half, cand):
        skip = part * per if candidates[half][cand].shape[0] == half_rows else 0

        def index(s, g, pick_ref):
            return jnp.where((s == half) & (pick_ref[half] == cand), skip + g, 0), 0, 0

        return pl.BlockSpec((blk, cols, tri), index)

    tile_spec = pl.BlockSpec((blk, cols, dim), lambda s, g, pick_ref: (s * 2 * per + part * per + g, 0, 0))
    y_specs = [y_spec(s, q) for s in (0, 1) for q in range(n_cand)]
    operands = [pick, pair_tile, gate, *candidates[0], *candidates[1], w_out]
    specs = [tile_spec, tile_spec] + y_specs + [pl.BlockSpec(w_out.shape, lambda s, g, pick_ref: (0, 0))]
    aliases = {}
    if so_far is not None:
        aliases = {len(operands): 0}
        operands.append(so_far)
        specs.append(pl.BlockSpec(memory_space=pl.ANY))
    return pl.pallas_call(
        lambda *refs: finish_kernel(n_cand, *refs),
        grid_spec=pltpu.PrefetchScalarGridSpec(num_scalar_prefetch=1, grid=(2, per), in_specs=specs, out_specs=tile_spec),
        out_shape=jax.ShapeDtypeStruct(pair_tile.shape, BF16),
        input_output_aliases=aliases,
        compiler_params=params(),
        cost_estimate=cost(8, 5 * rows * cols * dim),
        name='finish',
    )(*operands)


def solution(mesh):
    tile_spec = P(('batch', 'row'), 'col', None)
    mask_spec = P(('batch', 'row'), 'col')
    replicated = P()

    def local_step(pair_tile, mask_tile, ln_in_scale, w_left, w_left_gate, w_right, w_right_gate, w_out_gate, ln_out_scale, w_out):
        _, cols, _ = pair_tile.shape
        half_cols = cols // 2
        row, z = lax.axis_index('row'), lax.axis_index('col')
        y, c = row // 2, row % 2
        half = z // 2
        w_a = jnp.concatenate([w_left, w_left_gate], axis=1).T
        w_b = jnp.concatenate([w_right, w_right_gate], axis=1).T
        gain_in, gain_out = ln_in_scale[None], ln_out_scale[None]

        inner = (z == 1) | (z == 2)
        inner_flag, outer_flag = inner.astype(jnp.int32)[None], (1 - inner.astype(jnp.int32))[None]

        def masked(pairs, mask, upper):
            pairs = jnp.where(upper, pairs[:, half_cols:], pairs[:, :half_cols])
            mask = jnp.where(upper, mask[:, half_cols:], mask[:, :half_cols])
            return jnp.where((mask != 0)[:, :, None], pairs, jnp.zeros((), BF16))

        t_b = masked(pair_tile, mask_tile, y == 0)
        t_a = masked(*after((pair_tile, mask_tile), t_b), y == 1)
        y_a = send(t_b, TO_Y)
        z_a = send(t_a, TO_Z)
        m_0 = send(t_a, ACROSS)
        gate = out_gate(pair_tile, gain_in, w_out_gate)
        y_b = send(after(t_a, z_a), TO_Y)
        yz_a = send(after(y_a, gate), TO_Z)
        m_1 = send(y_a, ACROSS)
        z_b = send(after(t_b, yz_a), TO_Z)
        yz_b = send(after(z_a, y_b), TO_Y)

        keep = ((z % 2) == c).astype(jnp.int32)[None]
        sets = [((t_a, y_a), (z_a, yz_a)), ((t_b, y_b), (z_b, yz_b))]
        part = half_cols // 2
        a_1 = project(keep, (z_a, yz_a), None, gain_in, w_a, 0, part)
        a_2 = project(keep, (z_a, yz_a), None, gain_in, after(w_a, a_1), part, part)
        got_1, got_2 = send(a_1, ACROSS), send(a_2, ACROSS)
        give_0 = project(1 - keep, *sets[0], gain_in, after(w_b, a_2))
        a_0 = project(inner_flag, (m_0, m_1), (t_a, y_a), gain_in, after(w_a, give_0))
        a_0_sib = send(a_0, TO_CORE)
        keep_0 = project(keep, *sets[0], gain_in, after(w_b, a_0))
        give_1 = project(1 - keep, *sets[1], gain_in, after(w_b, keep_0))
        keep_1 = project(keep, *sets[1], gain_in, after(w_b, give_1))
        b_parts = [keep_0, keep_1, send(give_0, TO_CORE), send(give_1, TO_CORE)]

        done_0 = triangle(inner_flag, [(a_0, a_0_sib)], b_parts, gain_out)
        pair_1 = [(got_1, send(got_1, INNER_CORE)), (a_1, send(a_1, OUTER_CORE))]
        done_1 = triangle(inner_flag, pair_1, b_parts, after(gain_out, done_0))
        pair_2 = [(got_2, send(after(got_2, done_1), INNER_CORE)), (a_2, send(a_2, OUTER_CORE))]
        done_2 = triangle(inner_flag, pair_2, b_parts, after(gain_out, done_1))
        done = (done_0, done_1, done_2)

        got = [[send(v, home(from_y, min(turn, 1))) for turn, v in enumerate(done)] for from_y in (0, 1)]
        block_half = jnp.where(inner, 1 - half, half)
        turn = half ^ c
        own = (block_half == y) & (2 * half + c == z)
        pick = jnp.stack([turn + jnp.where(own & (y == from_y), 2, 0) for from_y in (0, 1)]).astype(jnp.int32)
        out = None
        for q in (0, 1):
            candidates = [(got[s][0], got[s][1 + q], done_0, done[1 + q]) for s in (0, 1)]
            out = finish(pick, pair_tile, gate, candidates, w_out, q, out)
        return out

    return jax.shard_map(local_step, mesh=mesh, in_specs=(tile_spec, mask_spec) + (replicated,) * 8, out_specs=tile_spec, check_vma=False)
```

time: 749 us -> 740 us (0.988)
  the two profiles are of different devices: /device:TPU:9 before, /device:TPU:20 now
where the time goes in v1:
time: 740 us; the launch traced here: 738 us
  waiting for transfers between devices  401 us (54%)
  Pallas kernels  280 us (38%)
  starting transfers between devices  40.3 us (5%)
  other arithmetic  13.8 us (2%)
    ppermute x23, waiting for transfers between devices, send(): return lax.ppermute(value, AXES, pairs)  401 us
    pallas_call x7, Pallas kernels, project(): pl.pallas_call(project_kernel, grid_spec=pltpu.PrefetchScalarGridSpec(num...  139 us
    pallas_call x3, Pallas kernels, triangle(): pl.pallas_call(lambda *refs: triangle_kernel(n_pair, *refs), grid_spec=pl...  95.3 us
    ppermute x23, starting transfers between devices, send(): return lax.ppermute(value, AXES, pairs)  40.3 us
    pallas_call x2, Pallas kernels, finish(): pl.pallas_call(lambda *refs: finish_kernel(n_cand, *refs), grid_spec=pltp...  26.9 us
    pallas_call x1, Pallas kernels, out_gate(): pl.pallas_call(gate_kernel, grid=(rows // blk,), in_specs=[spec, pl.Block...  18.9 us
  transfers between devices with their start and end apart: 23, of which 10 were waited for; matrix products, arithmetic and copies ran while one was open for 0% of the time, Pallas kernels for 36%

profile of v1, /device:TPU:20, one launch (start us, length us, event | category | flops | bytes accessed | tf_op | source)
XLA Modules:
  0.0 738.1 jit_solution(12488382664903243462)
XLA Ops:
  0.0 1.1 select_compare_fusion.1
  1.1 0.0 copy-start.2
  1.1 0.0 copy-start
  1.1 6.6 select_select_fusion.1.refs_0_
  7.7 0.1 select_compare_fusion
  7.8 1.6 copy-done
  9.4 4.2 select_select_fusion.refs_0_.refs_2_
  13.6 1.6 collective-permute-start.3
  15.2 0.5 collective-permute-start.1
  15.7 18.9 %out_gate.1.refs_2_ = f32[192,192,128]{2,1,0:T(8,128)} custom-call(bf16[192,192,128]{2,1,0:T(8,128)(2,1)} %refs_1_.3, bf16[1,128]{1,0:T(2,128)(2,1)} %bitcast.10, bf16[128,128]{1,0:T(8,128)(2,1)} %wg_ref.1), custom_call_target="tpu_custom_call" | custom-call | flops 90000000 | bytes 28311552 | tf_op jit(solution)/shard_map/out_gate/pallas_call | solution.py:190
  34.6 82.9 %collective-permute-done.3.refs_0_.refs_2_ = bf16[192,96,128]{2,1,0:T(8,128)(2,1)} collective-permute-done((bf16[192,96,128]{2,1,0:T(8,128)(2,1)}, bf16[192,96,128]{2,1,0:T(8,128)(2,1)}, u32[]{:S(2)}, u32[]{:S(2)}) %collective-permute-start.3) | collective-permute-done | bytes 4718624 | tf_op jit(solution)/shard_map/ppermute | solution.py:48
  117.5 0.5 collective-permute-start.6
  118.0 0.8 collective-permute-done.1.refs_1_.refs_3_
  118.8 0.8 collective-permute-start.4
  119.6 2.0 collective-permute-start
  121.6 4.0 collective-permute-start.2
  125.6 0.1 copy.12
  125.8 0.1 copy.13
  125.9 0.1 copy.14
  126.0 0.1 copy.15
  126.1 0.6 maximum_bitcast_fusion.refs_3_.refs_5_
  126.8 93.8 %collective-permute-done.6.refs_1_ = bf16[192,96,128]{2,1,0:T(8,128)(2,1)} collective-permute-done((bf16[192,96,128]{2,1,0:T(8,128)(2,1)}, bf16[192,96,128]{2,1,0:T(8,128)(2,1)}, u32[]{:S(2)}, u32[]{:S(2)}) %collective-permute-start.6) | collective-permute-done | bytes 4718624 | tf_op jit(solution)/shard_map/ppermute | solution.py:48
  220.5 0.5 collective-permute-start.8
  221.0 0.5 collective-permute-done.4.refs_1_.refs_3_
  221.5 1.1 collective-permute-start.7
  222.6 0.6 maximum_bitcast_fusion.1.refs_5_
  223.2 12.1 %project.7.refs_3_ = bf16[128,48,384]{2,1,0:T(8,128)(2,1)} custom-call(s32[1]{0:T(128)} %bitcast.5.flag_ref, bf16[192,96,128]{2,1,0:T(8,128)(2,1)} %collective-permute-done.3.refs_0_.refs_2_, bf16[192,96,128]{2,1,0:T(8,128)(2,1)} %collective-permute-done.4.refs_1_.refs_3_, bf16[1,128]{1,0:T(2,128)(2,1)} %bitcast.11, ...), custom_call_target="tpu_custom_call" | custom-call | flops 55000000 | bytes 9437184 | tf_op jit(solution)/shard_map/project/pallas_call | solution.py:105
  235.3 12.1 %project.8.refs_3_ = bf16[128,48,384]{2,1,0:T(8,128)(2,1)} custom-call(s32[1]{0:T(128)} %bitcast.5.flag_ref, bf16[192,96,128]{2,1,0:T(8,128)(2,1)} %collective-permute-done.3.refs_0_.refs_2_, bf16[192,96,128]{2,1,0:T(8,128)(2,1)} %collective-permute-done.4.refs_1_.refs_3_, bf16[1,128]{1,0:T(2,128)(2,1)} %bitcast.12, ...), custom_call_target="tpu_custom_call" | custom-call | flops 55000000 | bytes 9437184 | tf_op jit(solution)/shard_map/project/pallas_call | solution.py:105
  247.5 23.0 %project.9 = bf16[128,96,384]{2,1,0:T(8,128)(2,1)} custom-call(s32[1]{0:T(128)S(6)} %sub.17.flag_ref, bf16[192,96,128]{2,1,0:T(8,128)(2,1)} %select_select_fusion.refs_0_.refs_2_, bf16[192,96,128]{2,1,0:T(8,128)(2,1)} %collective-permute-done.1.refs_1_.refs_3_, bf16[192,96,128]{2,1,0:T(8,128)(2,1)} %collective-permute-done.3.refs_0_.refs_2_, ...), custom_call_target="tpu_custom_call" | custom-call | flops 115000000 | bytes 18874368 | tf_op jit(solution)/shard_map/project/pallas_call | solution.py:105
  270.5 0.0 collective-permute-done.refs_0_
  270.5 54.6 %collective-permute-done.2.refs_1_ = bf16[192,96,128]{2,1,0:T(8,128)(2,1)} collective-permute-done((bf16[192,96,128]{2,1,0:T(8,128)(2,1)}, bf16[192,96,128]{2,1,0:T(8,128)(2,1)}, u32[]{:S(2)}, u32[]{:S(2)}) %collective-permute-start.2) | collective-permute-done | bytes 4718624 | tf_op jit(solution)/shard_map/ppermute | solution.py:48
  325.0 22.9 %project.10.refs_1_ = bf16[128,96,384]{2,1,0:T(8,128)(2,1)} custom-call(s32[1]{0:T(128)} %bitcast.3.flag_ref.refs_0_, bf16[192,96,128]{2,1,0:T(8,128)(2,1)} %collective-permute-done.refs_0_, bf16[192,96,128]{2,1,0:T(8,128)(2,1)} %collective-permute-done.2.refs_1_, bf16[192,96,128]{2,1,0:T(8,128)(2,1)} %select_select_fusion.refs_0_.refs_2_, ...), custom_call_target="tpu_custom_call" | custom-call | flops 115000000 | bytes 18874368 | tf_op jit(solution)/shard_map/project/pallas_call | solution.py:105
  347.9 0.0 collective-permute-start.5
  347.9 0.5 collective-permute-start.9
  348.4 23.0 %project.11.refs_3_.refs_5_ = bf16[128,96,384]{2,1,0:T(8,128)(2,1)} custom-call(s32[1]{0:T(128)} %bitcast.5.flag_ref, bf16[192,96,128]{2,1,0:T(8,128)(2,1)} %select_select_fusion.refs_0_.refs_2_, bf16[192,96,128]{2,1,0:T(8,128)(2,1)} %collective-permute-done.1.refs_1_.refs_3_, bf16[192,96,128]{2,1,0:T(8,128)(2,1)} %collective-permute-done.3.refs_0_.refs_2_, ...), custom_call_target="tpu_custom_call" | custom-call | flops 115000000 | bytes 18874368 | tf_op jit(solution)/shard_map/project/pallas_call | solution.py:105
  371.4 0.0 collective-permute-done.8.refs_3_
  371.4 0.0 collective-permute-done.7.refs_2_
  371.4 23.0 %project.12 = bf16[128,96,384]{2,1,0:T(8,128)(2,1)} custom-call(s32[1]{0:T(128)S(6)} %sub.17.flag_ref, bf16[192,96,128]{2,1,0:T(8,128)(2,1)} %select_select_fusion.1.refs_0_, bf16[192,96,128]{2,1,0:T(8,128)(2,1)} %collective-permute-done.6.refs_1_, bf16[192,96,128]{2,1,0:T(8,128)(2,1)} %collective-permute-done.7.refs_2_, ...), custom_call_target="tpu_custom_call" | custom-call | flops 115000000 | bytes 18874368 | tf_op jit(solution)/shard_map/project/pallas_call | solution.py:105
  394.4 0.1 collective-permute-start.10
  394.5 2.2 collective-permute-start.13
  396.7 2.9 collective-permute-start.15
  399.6 101.3 %collective-permute-done.13.refs_1_ = bf16[128,48,384]{2,1,0:T(8,128)(2,1)} collective-permute-done((bf16[128,48,384]{2,1,0:T(8,128)(2,1)}, bf16[128,48,384]{2,1,0:T(8,128)(2,1)}, u32[]{:S(2)}, u32[]{:S(2)}) %collective-permute-start.13) | collective-permute-done | bytes 4718624 | tf_op jit(solution)/shard_map/ppermute | solution.py:48
  500.8 1.9 collective-permute-start.14
  502.8 2.2 collective-permute-start.12
  505.0 23.3 %project.13.refs_4_.refs_6_ = bf16[128,96,384]{2,1,0:T(8,128)(2,1)} custom-call(s32[1]{0:T(128)} %bitcast.5.flag_ref, bf16[192,96,128]{2,1,0:T(8,128)(2,1)} %select_select_fusion.1.refs_0_, bf16[192,96,128]{2,1,0:T(8,128)(2,1)} %collective-permute-done.6.refs_1_, bf16[192,96,128]{2,1,0:T(8,128)(2,1)} %collective-permute-done.7.refs_2_, ...), custom_call_target="tpu_custom_call" | custom-call | flops 115000000 | bytes 18874368 | tf_op jit(solution)/shard_map/project/pallas_call | solution.py:105
  528.3 2.8 collective-permute-start.17
  531.1 0.0 collective-permute-done.10.refs_6_.refs_8_
  531.1 36.0 %triangle.3.refs_5_.refs_9_ = bf16[96,192,128]{2,1,0:T(8,128)(2,1)} custom-call(s32[1]{0:T(128)} %bitcast.3.flag_ref.refs_0_, bf16[128,96,384]{2,1,0:T(8,128)(2,1)} %project.10.refs_1_, bf16[128,96,384]{2,1,0:T(8,128)(2,1)} %collective-permute-done.5.refs_2_, bf16[128,96,384]{2,1,0:T(8,128)(2,1)} %project.11.refs_3_.refs_5_, ...), custom_call_target="tpu_custom_call" | custom-call | flops 200000000 | bytes 56623104 | tf_op jit(solution)/shard_map/triangle/pallas_call | solution.py:164
  567.1 29.7 %triangle.4.refs_6_.refs_10_ = bf16[48,192,128]{2,1,0:T(8,128)(2,1)} custom-call(s32[1]{0:T(128)} %bitcast.3.flag_ref.refs_0_, bf16[128,48,384]{2,1,0:T(8,128)(2,1)} %collective-permute-done.13.refs_1_, bf16[128,48,384]{2,1,0:T(8,128)(2,1)} %collective-permute-done.14.refs_2_, bf16[128,48,384]{2,1,0:T(8,128)(2,1)} %project.7.refs_3_, ...), custom_call_target="tpu_custom_call" | custom-call | flops 200000000 | bytes 47185920 | tf_op jit(solution)/shard_map/triangle/pallas_call | solution.py:164
  596.8 12.4 %collective-permute-done.12.refs_1_ = bf16[128,48,384]{2,1,0:T(8,128)(2,1)} collective-permute-done((bf16[128,48,384]{2,1,0:T(8,128)(2,1)}, bf16[128,48,384]{2,1,0:T(8,128)(2,1)}, u32[]{:S(2)}, u32[]{:S(2)}) %collective-permute-start.12) | collective-permute-done | bytes 4718624 | tf_op jit(solution)/shard_map/ppermute | solution.py:48
  609.2 1.9 collective-permute-start.16
  611.1 3.0 collective-permute-start.11
  614.1 4.6 collective-permute-start.19
  618.7 1.3 collective-permute-start.21
  620.0 2.8 collective-permute-start.22
  622.8 29.6 %triangle.5.refs_6_.refs_10_ = bf16[48,192,128]{2,1,0:T(8,128)(2,1)} custom-call(s32[1]{0:T(128)} %bitcast.3.flag_ref.refs_0_, bf16[128,48,384]{2,1,0:T(8,128)(2,1)} %collective-permute-done.12.refs_1_, bf16[128,48,384]{2,1,0:T(8,128)(2,1)} %collective-permute-done.16.refs_2_, bf16[128,48,384]{2,1,0:T(8,128)(2,1)} %project.8.refs_3_, ...), custom_call_target="tpu_custom_call" | custom-call | flops 200000000 | bytes 47185920 | tf_op jit(solution)/shard_map/triangle/pallas_call | solution.py:164
  652.4 1.3 collective-permute-start.18
  653.7 39.9 %collective-permute-done.21.refs_4_ = bf16[48,192,128]{2,1,0:T(8,128)(2,1)S(1)} collective-permute-done((bf16[48,192,128]{2,1,0:T(8,128)(2,1)}, bf16[48,192,128]{2,1,0:T(8,128)(2,1)S(1)}, u32[]{:S(2)}, u32[]{:S(2)}) %collective-permute-start.21) | collective-permute-done | bytes 2359328 | tf_op jit(solution)/shard_map/ppermute | solution.py:48
  693.6 1.9 collective-permute-start.20
  695.6 0.6 pad_add_fusion.refs_0_
  696.3 13.5 %finish.2.refs_12_ = bf16[192,192,128]{2,1,0:T(8,128)(2,1)} custom-call(s32[2]{0:T(128)} %pad_add_fusion.refs_0_, bf16[192,192,128]{2,1,0:T(8,128)(2,1)} %refs_1_.3, f32[192,192,128]{2,1,0:T(8,128)} %out_gate.1.refs_2_, bf16[96,192,128]{2,1,0:T(8,128)(2,1)} %collective-permute-done.11.refs_3_, bf16[48,192,128]{2,1,0:T(8,128)(2,1)} %copy-done.1, ...), custom_call_target="tpu_custom_call" | custom-call | flops 40000000 | bytes 23592960 | tf_op jit(solution)/shard_map/finish/pallas_call | solution.py:243
  709.7 9.3 %collective-permute-done.18.refs_4_ = bf16[48,192,128]{2,1,0:T(8,128)(2,1)} collective-permute-done((bf16[48,192,128]{2,1,0:T(8,128)(2,1)}, bf16[48,192,128]{2,1,0:T(8,128)(2,1)}, u32[]{:S(2)}, u32[]{:S(2)}) %collective-permute-start.18) | collective-permute-done | bytes 2359328 | tf_op jit(solution)/shard_map/ppermute | solution.py:48
  719.0 5.7 collective-permute-done.20.refs_8_
  724.7 13.4 %finish.3 = bf16[192,192,128]{2,1,0:T(8,128)(2,1)} custom-call(s32[2]{0:T(128)} %pad_add_fusion.refs_0_, bf16[192,192,128]{2,1,0:T(8,128)(2,1)} %refs_1_.3, f32[192,192,128]{2,1,0:T(8,128)} %out_gate.1.refs_2_, bf16[96,192,128]{2,1,0:T(8,128)(2,1)} %collective-permute-done.11.refs_3_, ...), custom_call_target="tpu_custom_call", output_to_operand_aliasing={{}: (12, {})} | custom-call | flops 40000000 | bytes 23592960 | tf_op jit(solution)/shard_map/finish/pallas_call | solution.py:243
  (20 shorter events, 0.0 us)
Async XLA Ops:
  1.1 6.6 copy-start.2
  1.1 8.3 %copy-start = (bf16[192,192,128]{2,1,0:T(8,128)(2,1)S(1)}, bf16[192,192,128]{2,1,0:T(8,128)(2,1)}, u32[]{:S(2)}) copy-start(bf16[192,192,128]{2,1,0:T(8,128)(2,1)} %refs_1_.3) | copy-start | bytes 28311556
  13.6 103.9 %collective-permute-start.3 = (bf16[192,96,128]{2,1,0:T(8,128)(2,1)}, bf16[192,96,128]{2,1,0:T(8,128)(2,1)}, u32[]{:S(2)}, u32[]{:S(2)}) collective-permute-start(bf16[192,96,128]{2,1,0:T(8,128)(2,1)} %select_select_fusion.refs_0_.refs_2_), channel_id=1, source_target_pairs={{0,4},{1,5},{2,6},{3,7},{4,0},{5,1},{6,2},{7,3},{8,12},{9,13},{10,... | collective-permute-start | bytes 14155784 | tf_op jit(solution)/shard_map/ppermute | solution.py:48
  15.2 103.6 %collective-permute-start.1 = (bf16[192,96,128]{2,1,0:T(8,128)(2,1)}, bf16[192,96,128]{2,1,0:T(8,128)(2,1)}, u32[]{:S(2)}, u32[]{:S(2)}) collective-permute-start(bf16[192,96,128]{2,1,0:T(8,128)(2,1)} %select_select_fusion.1.refs_0_), channel_id=1, source_target_pairs={{0,2},{1,3},{2,0},{3,1},{4,6},{5,7},{6,4},{7,5},{8,10},{9,11},{10,... | collective-permute-start | bytes 14155784 | tf_op jit(solution)/shard_map/ppermute | solution.py:48
  15.7 109.9 %copy-start.3 = (bf16[128,128]{1,0:T(8,128)(2,1)S(1)}, bf16[128,128]{1,0:T(8,128)(2,1)}, u32[]{:S(2)}) copy-start(bf16[128,128]{1,0:T(8,128)(2,1)} %param.13) | copy-start | bytes 98308
  15.7 110.0 %copy-start.4 = (bf16[128,128]{1,0:T(8,128)(2,1)S(1)}, bf16[128,128]{1,0:T(8,128)(2,1)}, u32[]{:S(2)}) copy-start(bf16[128,128]{1,0:T(8,128)(2,1)} %param.14) | copy-start | bytes 98308
  15.7 110.1 %copy-start.5 = (bf16[128,128]{1,0:T(8,128)(2,1)S(1)}, bf16[128,128]{1,0:T(8,128)(2,1)}, u32[]{:S(2)}) copy-start(bf16[128,128]{1,0:T(8,128)(2,1)} %param.15) | copy-start | bytes 98308
  15.7 110.3 %copy-start.6 = (bf16[128,128]{1,0:T(8,128)(2,1)S(1)}, bf16[128,128]{1,0:T(8,128)(2,1)}, u32[]{:S(2)}) copy-start(bf16[128,128]{1,0:T(8,128)(2,1)} %param.16) | copy-start | bytes 98308
  117.5 103.0 %collective-permute-start.6 = (bf16[192,96,128]{2,1,0:T(8,128)(2,1)}, bf16[192,96,128]{2,1,0:T(8,128)(2,1)}, u32[]{:S(2)}, u32[]{:S(2)}) collective-permute-start(bf16[192,96,128]{2,1,0:T(8,128)(2,1)} %select_select_fusion.refs_0_.refs_2_), channel_id=1, source_target_pairs={{0,2},{1,3},{2,0},{3,1},{4,6},{5,7},{6,4},{7,5},{8,10},{9,11},{10,... | collective-permute-start | bytes 14155784 | tf_op jit(solution)/shard_map/ppermute | solution.py:48
  118.8 102.7 %collective-permute-start.4 = (bf16[192,96,128]{2,1,0:T(8,128)(2,1)}, bf16[192,96,128]{2,1,0:T(8,128)(2,1)}, u32[]{:S(2)}, u32[]{:S(2)}) collective-permute-start(bf16[192,96,128]{2,1,0:T(8,128)(2,1)} %collective-permute-done.1.refs_1_.refs_3_), channel_id=1, source_target_pairs={{0,4},{1,5},{2,6},{3,7},{4,0},{5,1},{6,2},{7,3},{8,12},{9,13},{10,... | collective-permute-start | bytes 14155784 | tf_op jit(solution)/shard_map/ppermute | solution.py:48
  119.6 150.9 %collective-permute-start = (bf16[192,96,128]{2,1,0:T(8,128)(2,1)}, bf16[192,96,128]{2,1,0:T(8,128)(2,1)}, u32[]{:S(2)}, u32[]{:S(2)}) collective-permute-start(bf16[192,96,128]{2,1,0:T(8,128)(2,1)} %select_select_fusion.refs_0_.refs_2_), channel_id=1, source_target_pairs={{4,8},{5,9},{6,10},{7,11},{8,4},{9,5},{10,6},{11,7},{20,24},{21,25... | collective-permute-start | bytes 14155784 | tf_op jit(solution)/shard_map/ppermute | solution.py:48
  121.6 203.4 %collective-permute-start.2 = (bf16[192,96,128]{2,1,0:T(8,128)(2,1)}, bf16[192,96,128]{2,1,0:T(8,128)(2,1)}, u32[]{:S(2)}, u32[]{:S(2)}) collective-permute-start(bf16[192,96,128]{2,1,0:T(8,128)(2,1)} %collective-permute-done.1.refs_1_.refs_3_), channel_id=1, source_target_pairs={{4,8},{5,9},{6,10},{7,11},{8,4},{9,5},{10,6},{11,7},{20,24},{21,25... | collective-permute-start | bytes 14155784 | tf_op jit(solution)/shard_map/ppermute | solution.py:48
  220.5 150.9 %collective-permute-start.8 = (bf16[192,96,128]{2,1,0:T(8,128)(2,1)}, bf16[192,96,128]{2,1,0:T(8,128)(2,1)}, u32[]{:S(2)}, u32[]{:S(2)}) collective-permute-start(bf16[192,96,128]{2,1,0:T(8,128)(2,1)} %collective-permute-done.3.refs_0_.refs_2_), channel_id=1, source_target_pairs={{0,2},{1,3},{2,0},{3,1},{4,6},{5,7},{6,4},{7,5},{8,10},{9,11},{10,... | collective-permute-start | bytes 14155784 | tf_op jit(solution)/shard_map/ppermute | solution.py:48
  221.5 149.9 %collective-permute-start.7 = (bf16[192,96,128]{2,1,0:T(8,128)(2,1)}, bf16[192,96,128]{2,1,0:T(8,128)(2,1)}, u32[]{:S(2)}, u32[]{:S(2)}) collective-permute-start(bf16[192,96,128]{2,1,0:T(8,128)(2,1)} %select_select_fusion.1.refs_0_), channel_id=1, source_target_pairs={{0,4},{1,5},{2,6},{3,7},{4,0},{5,1},{6,2},{7,3},{8,12},{9,13},{10,... | collective-permute-start | bytes 14155784 | tf_op jit(solution)/shard_map/ppermute | solution.py:48
  347.9 154.8 %collective-permute-start.5 = (bf16[128,96,384]{2,1,0:T(8,128)(2,1)}, bf16[128,96,384]{2,1,0:T(8,128)(2,1)}, u32[]{:S(2)}, u32[]{:S(2)}) collective-permute-start(bf16[128,96,384]{2,1,0:T(8,128)(2,1)} %project.10.refs_1_), channel_id=1, source_target_pairs={{0,1},{1,0},{2,3},{3,2},{4,5},{5,4},{6,7},{7,6},{8,9},{9,8},{10,11... | collective-permute-start | bytes 28311560 | tf_op jit(solution)/shard_map/ppermute | solution.py:48
  347.9 180.4 %collective-permute-start.9 = (bf16[128,96,384]{2,1,0:T(8,128)(2,1)}, bf16[128,96,384]{2,1,0:T(8,128)(2,1)}, u32[]{:S(2)}, u32[]{:S(2)}) collective-permute-start(bf16[128,96,384]{2,1,0:T(8,128)(2,1)} %project.9), channel_id=1, source_target_pairs={{0,1},{1,0},{2,3},{3,2},{4,5},{5,4},{6,7},{7,6},{8,9},{9,8},{10,11... | collective-permute-start | bytes 28311560 | tf_op jit(solution)/shard_map/ppermute | solution.py:48
  394.4 136.7 %collective-permute-start.10 = (bf16[128,96,384]{2,1,0:T(8,128)(2,1)}, bf16[128,96,384]{2,1,0:T(8,128)(2,1)}, u32[]{:S(2)}, u32[]{:S(2)}) collective-permute-start(bf16[128,96,384]{2,1,0:T(8,128)(2,1)} %project.12), channel_id=1, source_target_pairs={{0,1},{1,0},{2,3},{3,2},{4,5},{5,4},{6,7},{7,6},{8,9},{9,8},{10,11... | collective-permute-start | bytes 28311560 | tf_op jit(solution)/shard_map/ppermute | solution.py:48
  394.5 106.4 %collective-permute-start.13 = (bf16[128,48,384]{2,1,0:T(8,128)(2,1)}, bf16[128,48,384]{2,1,0:T(8,128)(2,1)}, u32[]{:S(2)}, u32[]{:S(2)}) collective-permute-start(bf16[128,48,384]{2,1,0:T(8,128)(2,1)} %project.7.refs_3_), channel_id=1, source_target_pairs={{4,8},{5,9},{6,10},{7,11},{8,4},{9,5},{10,6},{11,7},{20,24},{21,25... | collective-permute-start | bytes 14155784 | tf_op jit(solution)/shard_map/ppermute | solution.py:48
  396.7 170.4 %collective-permute-start.15 = (bf16[128,48,384]{2,1,0:T(8,128)(2,1)}, bf16[128,48,384]{2,1,0:T(8,128)(2,1)}, u32[]{:S(2)}, u32[]{:S(2)}) collective-permute-start(bf16[128,48,384]{2,1,0:T(8,128)(2,1)} %project.7.refs_3_), channel_id=1, source_target_pairs={{0,1},{1,0},{2,3},{3,2},{12,13},{13,12},{14,15},{15,14},{16,17},{1... | collective-permute-start | bytes 14155784 | tf_op jit(solution)/shard_map/ppermute | solution.py:48
  500.8 66.2 %collective-permute-start.14 = (bf16[128,48,384]{2,1,0:T(8,128)(2,1)}, bf16[128,48,384]{2,1,0:T(8,128)(2,1)}, u32[]{:S(2)}, u32[]{:S(2)}) collective-permute-start(bf16[128,48,384]{2,1,0:T(8,128)(2,1)} %collective-permute-done.13.refs_1_), channel_id=1, source_target_pairs={{4,5},{5,4},{6,7},{7,6},{8,9},{9,8},{10,11},{11,10},{20,21},{21,20... | collective-permute-start | bytes 14155784 | tf_op jit(solution)/shard_map/ppermute | solution.py:48
  502.8 106.4 %collective-permute-start.12 = (bf16[128,48,384]{2,1,0:T(8,128)(2,1)}, bf16[128,48,384]{2,1,0:T(8,128)(2,1)}, u32[]{:S(2)}, u32[]{:S(2)}) collective-permute-start(bf16[128,48,384]{2,1,0:T(8,128)(2,1)} %project.8.refs_3_), channel_id=1, source_target_pairs={{4,8},{5,9},{6,10},{7,11},{8,4},{9,5},{10,6},{11,7},{20,24},{21,25... | collective-permute-start | bytes 14155784 | tf_op jit(solution)/shard_map/ppermute | solution.py:48
  528.3 91.7 %collective-permute-start.17 = (bf16[128,48,384]{2,1,0:T(8,128)(2,1)}, bf16[128,48,384]{2,1,0:T(8,128)(2,1)}, u32[]{:S(2)}, u32[]{:S(2)}) collective-permute-start(bf16[128,48,384]{2,1,0:T(8,128)(2,1)} %project.8.refs_3_), channel_id=1, source_target_pairs={{0,1},{1,0},{2,3},{3,2},{12,13},{13,12},{14,15},{15,14},{16,17},{1... | collective-permute-start | bytes 14155784 | tf_op jit(solution)/shard_map/ppermute | solution.py:48
  609.2 13.6 %collective-permute-start.16 = (bf16[128,48,384]{2,1,0:T(8,128)(2,1)}, bf16[128,48,384]{2,1,0:T(8,128)(2,1)}, u32[]{:S(2)}, u32[]{:S(2)}) collective-permute-start(bf16[128,48,384]{2,1,0:T(8,128)(2,1)} %collective-permute-done.12.refs_1_), channel_id=1, source_target_pairs={{4,5},{5,4},{6,7},{7,6},{8,9},{9,8},{10,11},{11,10},{20,21},{21,20... | collective-permute-start | bytes 14155784 | tf_op jit(solution)/shard_map/ppermute | solution.py:48
  611.1 85.1 %collective-permute-start.11 = (bf16[96,192,128]{2,1,0:T(8,128)(2,1)}, bf16[96,192,128]{2,1,0:T(8,128)(2,1)}, u32[]{:S(2)}, u32[]{:S(2)}) collective-permute-start(bf16[96,192,128]{2,1,0:T(8,128)(2,1)} %triangle.3.refs_5_.refs_9_), channel_id=1, source_target_pairs={{1,4},{4,2},{5,6},{8,9},{9,13},{12,11},{13,15},{17,20},{20,18},{21... | collective-permute-start | bytes 14155784 | tf_op jit(solution)/shard_map/ppermute | solution.py:48
  614.1 82.2 %collective-permute-start.19 = (bf16[96,192,128]{2,1,0:T(8,128)(2,1)}, bf16[96,192,128]{2,1,0:T(8,128)(2,1)}, u32[]{:S(2)}, u32[]{:S(2)}) collective-permute-start(bf16[96,192,128]{2,1,0:T(8,128)(2,1)} %triangle.3.refs_5_.refs_9_), channel_id=1, source_target_pairs={{2,0},{3,4},{6,2},{7,6},{10,9},{11,13},{14,11},{18,16},{19,20},{22... | collective-permute-start | bytes 14155784 | tf_op jit(solution)/shard_map/ppermute | solution.py:48
  618.7 74.9 %collective-permute-start.21 = (bf16[48,192,128]{2,1,0:T(8,128)(2,1)}, bf16[48,192,128]{2,1,0:T(8,128)(2,1)S(1)}, u32[]{:S(2)}, u32[]{:S(2)}) collective-permute-start(bf16[48,192,128]{2,1,0:T(8,128)(2,1)} %triangle.4.refs_6_.refs_10_), channel_id=1, source_target_pairs={{0,1},{1,5},{4,3},{5,7},{9,12},{12,10},{13,14},{16,17},{17,21},{20... | collective-permute-start | bytes 7077896 | tf_op jit(solution)/shard_map/ppermute | solution.py:48
  620.0 76.3 %collective-permute-start.22 = (bf16[48,192,128]{2,1,0:T(8,128)(2,1)}, bf16[48,192,128]{2,1,0:T(8,128)(2,1)}, u32[]{:S(2)}, u32[]{:S(2)}) collective-permute-start(bf16[48,192,128]{2,1,0:T(8,128)(2,1)} %triangle.4.refs_6_.refs_10_), channel_id=1, source_target_pairs={{2,1},{3,5},{6,3},{10,8},{11,12},{14,10},{15,14},{18,17},{19,21},{... | collective-permute-start | bytes 7077896 | tf_op jit(solution)/shard_map/ppermute | solution.py:48
  652.4 66.6 %collective-permute-start.18 = (bf16[48,192,128]{2,1,0:T(8,128)(2,1)}, bf16[48,192,128]{2,1,0:T(8,128)(2,1)}, u32[]{:S(2)}, u32[]{:S(2)}) collective-permute-start(bf16[48,192,128]{2,1,0:T(8,128)(2,1)} %triangle.5.refs_6_.refs_10_), channel_id=1, source_target_pairs={{0,1},{1,5},{4,3},{5,7},{9,12},{12,10},{13,14},{16,17},{17,21},{20... | collective-permute-start | bytes 7077896 | tf_op jit(solution)/shard_map/ppermute | solution.py:48
  693.6 2.6 copy-start.1
  693.6 31.0 %collective-permute-start.20 = (bf16[48,192,128]{2,1,0:T(8,128)(2,1)}, bf16[48,192,128]{2,1,0:T(8,128)(2,1)}, u32[]{:S(2)}, u32[]{:S(2)}) collective-permute-start(bf16[48,192,128]{2,1,0:T(8,128)(2,1)} %triangle.5.refs_6_.refs_10_), channel_id=1, source_target_pairs={{2,1},{3,5},{6,3},{10,8},{11,12},{14,10},{15,14},{18,17},{19,21},{... | collective-permute-start | bytes 7077896 | tf_op jit(solution)/shard_map/ppermute | solution.py:48

commit v2 on v1

--- a/solution.py
+++ b/solution.py
@@ -1,3 +1,5 @@
+import math
+
 import jax
 import jax.numpy as jnp
 from jax import lax
@@ -118,9 +120,9 @@
     )(flag, *yes, *(no or ()), gain, w_t)
 
 
-def triangle_kernel(n_pair, flag_ref, *refs):
-    a_refs, b_refs = refs[:2 * n_pair], refs[2 * n_pair:2 * n_pair + 4]
-    gain_ref, out_ref, *o_refs = refs[2 * n_pair + 4:]
+def triangle_kernel(n_pair, n_part, flag_ref, *refs):
+    a_refs, b_refs = refs[:2 * n_pair], refs[2 * n_pair:2 * n_pair + 2 * n_part]
+    gain_ref, out_ref, *o_refs = refs[2 * n_pair + 2 * n_part:]
     step, steps = pl.program_id(0), pl.num_programs(0)
     n_h, n_i, _ = a_refs[0].shape
     n_j = out_ref.shape[1]
@@ -131,8 +133,8 @@
         a_0, a_1 = a_refs[0][h], a_refs[1][h]
         if n_pair == 2:
             a_0, a_1 = jnp.where(pick, a_0, a_refs[2][h]), jnp.where(pick, a_1, a_refs[3][h])
-        acc = dot_nt(a_0, jnp.concatenate([b_refs[0][h], b_refs[1][h]], axis=0))
-        acc += dot_nt(a_1, jnp.concatenate([b_refs[2][h], b_refs[3][h]], axis=0))
+        acc = dot_nt(a_0, jnp.concatenate([ref[h] for ref in b_refs[:n_part]], axis=0))
+        acc += dot_nt(a_1, jnp.concatenate([ref[h] for ref in b_refs[n_part:]], axis=0))
         start = pl.multiple_of((step * n_h + h) * pitch, 8)
         for (at, width), o_ref in zip(spans, o_refs):
             o_ref[pl.ds(start, n_i), :width] = acc[:, at:at + width]
@@ -154,19 +156,19 @@
 
 
 def triangle(flag, a_pairs, b_parts, gain, blk=8):
-    n_pair = len(a_pairs)
+    n_pair, n_part = len(a_pairs), len(b_parts) // 2
     tri, n_i, n_k = a_pairs[0][0].shape
-    half_j = b_parts[0].shape[1]
-    n_j = 2 * half_j
+    part_j = b_parts[0].shape[1]
+    n_j = n_part * part_j
     specs = []
     for q in range(n_pair):
         specs += [pl.BlockSpec((blk, n_i, n_k), lambda g, f, q=q: (jnp.where(f[0] == 1 - q, g, 0) if n_pair == 2 else g, 0, 0))] * 2
     return pl.pallas_call(
-        lambda *refs: triangle_kernel(n_pair, *refs),
+        lambda *refs: triangle_kernel(n_pair, n_part, *refs),
         grid_spec=pltpu.PrefetchScalarGridSpec(
             num_scalar_prefetch=1,
             grid=(tri // blk,),
-            in_specs=specs + [pl.BlockSpec((blk, half_j, n_k), lambda g, f: (g, 0, 0))] * 4 + [pl.BlockSpec((1, tri), lambda g, f: (0, 0))],
+            in_specs=specs + [pl.BlockSpec((blk, part_j, n_k), lambda g, f: (g, 0, 0))] * (2 * n_part) + [pl.BlockSpec((1, tri), lambda g, f: (0, 0))],
             out_specs=pl.BlockSpec((n_i, n_j, tri), lambda g, f: (0, 0, 0)),
             scratch_shapes=[pltpu.VMEM((tri * (n_i + 8), 128), F32)] * pl.cdiv(n_j, 128),
         ),
@@ -199,41 +201,45 @@
     )(pair_tile, gain, w_gate)
 
 
-def finish_kernel(n_cand, pick_ref, z_ref, gate_ref, *refs):
-    y_refs, wo_ref, out_ref = refs[:2 * n_cand], refs[2 * n_cand], refs[-1]
+def finish_kernel(sizes, pick_ref, z_ref, gate_ref, *refs):
+    wo_ref, out_ref = refs[2 * sum(sizes)], refs[-1]
     rows, cols, dim = z_ref.shape
     half_cols = cols // 2
     for s in (0, 1):
-        for q in range(n_cand):
+        for q, size in enumerate(sizes):
+            first = s * sum(sizes) + sum(sizes[:q])
+
             @pl.when((pl.program_id(0) == s) & (pick_ref[s] == q))
-            def _(s=s, y_ref=y_refs[s * n_cand + q]):
-                for j in (0, 1):
-                    to, at = pl.ds(j * half_cols, half_cols), pl.ds((j ^ s) * half_cols, half_cols)
-                    update = jnp.dot(y_ref[:, at, :].reshape(rows * half_cols, -1), wo_ref[...], preferred_element_type=F32)
-                    total = z_ref[:, to, :].astype(F32) + gate_ref[:, to, :] * update.reshape(rows, half_cols, dim)
-                    out_ref[:, to, :] = total.astype(BF16)
-
-
-def finish(pick, pair_tile, gate, candidates, w_out, part, so_far=None, blk=12):
+            def _(s=s, y_refs=refs[first:first + size]):
+                @pl.loop(0, rows, step=4)
+                def _(r):
+                    at = pl.ds(r, 4)
+                    for j in (0, 1):
+                        to, part = pl.ds(j * half_cols, half_cols), j ^ s
+                        y_part = y_refs[part][at] if len(y_refs) == 2 else y_refs[0][at, pl.ds(part * half_cols, half_cols), :]
+                        update = jnp.dot(y_part.reshape(4 * half_cols, -1), wo_ref[...], preferred_element_type=F32)
+                        total = z_ref[at, to, :].astype(F32) + gate_ref[at, to, :] * update.reshape(4, half_cols, dim)
+                        out_ref[at, to, :] = total.astype(BF16)
+
+
+def finish(pick, pair_tile, gate, candidates, w_out, first, count, so_far=None, blk=16):
     rows, cols, dim = pair_tile.shape
     half_rows = rows // 2
-    quarter = half_rows // 2
-    blk = blk if quarter % blk == 0 else quarter
-    per = quarter // blk
+    blk = math.gcd(blk, math.gcd(first, count))
     tri = w_out.shape[0]
-    n_cand = len(candidates[0])
-
-    def y_spec(half, cand):
-        skip = part * per if candidates[half][cand].shape[0] == half_rows else 0
+    sizes = tuple(len(c) for c in candidates[0])
+
+    def y_spec(half, cand, array):
+        skip = first // blk if array.shape[0] == half_rows else 0
 
         def index(s, g, pick_ref):
             return jnp.where((s == half) & (pick_ref[half] == cand), skip + g, 0), 0, 0
 
-        return pl.BlockSpec((blk, cols, tri), index)
-
-    tile_spec = pl.BlockSpec((blk, cols, dim), lambda s, g, pick_ref: (s * 2 * per + part * per + g, 0, 0))
-    y_specs = [y_spec(s, q) for s in (0, 1) for q in range(n_cand)]
-    operands = [pick, pair_tile, gate, *candidates[0], *candidates[1], w_out]
+        return pl.BlockSpec((blk, array.shape[1], tri), index)
+
+    tile_spec = pl.BlockSpec((blk, cols, dim), lambda s, g, pick_ref: (s * (half_rows // blk) + first // blk + g, 0, 0))
+    y_specs = [y_spec(s, q, v) for s in (0, 1) for q, c in enumerate(candidates[s]) for v in c]
+    operands = [pick, pair_tile, gate] + [v for s in (0, 1) for c in candidates[s] for v in c] + [w_out]
     specs = [tile_spec, tile_spec] + y_specs + [pl.BlockSpec(w_out.shape, lambda s, g, pick_ref: (0, 0))]
     aliases = {}
     if so_far is not None:
@@ -241,8 +247,8 @@
         operands.append(so_far)
         specs.append(pl.BlockSpec(memory_space=pl.ANY))
     return pl.pallas_call(
-        lambda *refs: finish_kernel(n_cand, *refs),
-        grid_spec=pltpu.PrefetchScalarGridSpec(num_scalar_prefetch=1, grid=(2, per), in_specs=specs, out_specs=tile_spec),
+        lambda *refs: finish_kernel(sizes, *refs),
+        grid_spec=pltpu.PrefetchScalarGridSpec(num_scalar_prefetch=1, grid=(2, count // blk), in_specs=specs, out_specs=tile_spec),
         out_shape=jax.ShapeDtypeStruct(pair_tile.shape, BF16),
         input_output_aliases=aliases,
         compiler_params=params(),
@@ -288,34 +294,37 @@
 
         keep = ((z % 2) == c).astype(jnp.int32)[None]
         sets = [((t_a, y_a), (z_a, yz_a)), ((t_b, y_b), (z_b, yz_b))]
-        part = half_cols // 2
-        a_1 = project(keep, (z_a, yz_a), None, gain_in, w_a, 0, part)
-        a_2 = project(keep, (z_a, yz_a), None, gain_in, after(w_a, a_1), part, part)
+        big = half_cols * 2 // 3
+        small = half_cols - big
+        a_1 = project(keep, (z_a, yz_a), None, gain_in, w_a, 0, big)
+        a_2 = project(keep, (z_a, yz_a), None, gain_in, after(w_a, a_1), big, small)
         got_1, got_2 = send(a_1, ACROSS), send(a_2, ACROSS)
         give_0 = project(1 - keep, *sets[0], gain_in, after(w_b, a_2))
         a_0 = project(inner_flag, (m_0, m_1), (t_a, y_a), gain_in, after(w_a, give_0))
-        a_0_sib = send(a_0, TO_CORE)
+        a_pair = [(a_0, send(a_0, TO_CORE))]
         keep_0 = project(keep, *sets[0], gain_in, after(w_b, a_0))
-        give_1 = project(1 - keep, *sets[1], gain_in, after(w_b, keep_0))
+        b_0 = [keep_0, send(give_0, TO_CORE)]
+        done_0 = triangle(inner_flag, a_pair, b_0, gain_out)
+        give_1 = project(1 - keep, *sets[1], gain_in, after(w_b, done_0))
         keep_1 = project(keep, *sets[1], gain_in, after(w_b, give_1))
-        b_parts = [keep_0, keep_1, send(give_0, TO_CORE), send(give_1, TO_CORE)]
-
-        done_0 = triangle(inner_flag, [(a_0, a_0_sib)], b_parts, gain_out)
+        b_1 = [keep_1, send(give_1, TO_CORE)]
+        b_parts = [b_0[0], b_1[0], b_0[1], b_1[1]]
+        done_1 = triangle(inner_flag, a_pair, b_1, gain_out)
         pair_1 = [(got_1, send(got_1, INNER_CORE)), (a_1, send(a_1, OUTER_CORE))]
-        done_1 = triangle(inner_flag, pair_1, b_parts, after(gain_out, done_0))
-        pair_2 = [(got_2, send(after(got_2, done_1), INNER_CORE)), (a_2, send(a_2, OUTER_CORE))]
-        done_2 = triangle(inner_flag, pair_2, b_parts, after(gain_out, done_1))
-        done = (done_0, done_1, done_2)
-
-        got = [[send(v, home(from_y, min(turn, 1))) for turn, v in enumerate(done)] for from_y in (0, 1)]
+        done_2 = triangle(inner_flag, pair_1, b_parts, after(gain_out, done_1))
+        pair_2 = [(got_2, send(after(got_2, done_2), INNER_CORE)), (a_2, send(a_2, OUTER_CORE))]
+        done_3 = triangle(inner_flag, pair_2, b_parts, after(gain_out, done_2))
+        done = (done_0, done_1, done_2, done_3)
+
+        got = [[send(v, home(from_y, n // 2)) for n, v in enumerate(done)] for from_y in (0, 1)]
         block_half = jnp.where(inner, 1 - half, half)
         turn = half ^ c
         own = (block_half == y) & (2 * half + c == z)
         pick = jnp.stack([turn + jnp.where(own & (y == from_y), 2, 0) for from_y in (0, 1)]).astype(jnp.int32)
         out = None
-        for q in (0, 1):
-            candidates = [(got[s][0], got[s][1 + q], done_0, done[1 + q]) for s in (0, 1)]
-            out = finish(pick, pair_tile, gate, candidates, w_out, q, out)
+        for n, first, count in ((2, 0, big), (3, big, small)):
+            candidates = [(tuple(got[s][:2]), (got[s][n],), (done_0, done_1), (done[n],)) for s in (0, 1)]
+            out = finish(pick, pair_tile, gate, candidates, w_out, first, count, out)
         return out
 
     return jax.shard_map(local_step, mesh=mesh, in_specs=(tile_spec, mask_spec) + (replicated,) * 8, out_specs=tile_spec, check_vma=False)

time: 740 us -> 806 us (1.089)
  the two profiles are of different devices: /device:TPU:20 before, /device:TPU:0 now
where the time goes in v2:
time: 806 us; the launch traced here: 804 us
  waiting for transfers between devices  374 us (46%)
  Pallas kernels  299 us (37%)
  starting transfers between devices  111 us (14%)
  other arithmetic  15.6 us (2%)
    ppermute x25, waiting for transfers between devices, send(): return lax.ppermute(value, AXES, pairs)  374 us
    pallas_call x7, Pallas kernels, project(): pl.pallas_call(project_kernel, grid_spec=pltpu.PrefetchScalarGridSpec(num...  139 us
    pallas_call x4, Pallas kernels, triangle(): pl.pallas_call(lambda *refs: triangle_kernel(n_pair, n_part, *refs), grid...  111 us
    ppermute x25, starting transfers between devices, send(): return lax.ppermute(value, AXES, pairs)  111 us
    pallas_call x2, Pallas kernels, finish(): pl.pallas_call(lambda *refs: finish_kernel(sizes, *refs), grid_spec=pltpu...  28.8 us
    pallas_call x1, Pallas kernels, out_gate(): pl.pallas_call(gate_kernel, grid=(rows // blk,), in_specs=[spec, pl.Block...  18.9 us
  transfers between devices with their start and end apart: 25, of which 7 were waited for; matrix products, arithmetic and copies ran while one was open for 1% of the time, Pallas kernels for 33%

profile of v2, /device:TPU:0, one launch (start us, length us, event | category | flops | bytes accessed | tf_op | source)
XLA Modules:
  0.0 804.1 jit_solution(4530750398399002837)
XLA Ops:
  0.0 1.1 select_compare_fusion.1
  1.1 0.0 copy-start.4
  1.1 6.3 select_select_fusion.1.refs_0_
  7.4 3.0 collective-permute-start.1
  10.4 0.1 select_compare_fusion
  10.5 6.3 select_select_fusion.refs_0_.refs_2_
  16.7 1.6 collective-permute-start.3
  18.3 18.9 %out_gate.1.refs_2_ = f32[192,192,128]{2,1,0:T(8,128)} custom-call(bf16[192,192,128]{2,1,0:T(8,128)(2,1)} %refs_1_.3, bf16[1,128]{1,0:T(2,128)(2,1)} %bitcast.10, bf16[128,128]{1,0:T(8,128)(2,1)} %wg_ref.1), custom_call_target="tpu_custom_call" | custom-call | flops 90000000 | bytes 28311552 | tf_op jit(solution)/shard_map/out_gate/pallas_call | solution.py:192
  37.2 75.3 %collective-permute-done.1.refs_1_.refs_3_ = bf16[192,96,128]{2,1,0:T(8,128)(2,1)} collective-permute-done((bf16[192,96,128]{2,1,0:T(8,128)(2,1)}, bf16[192,96,128]{2,1,0:T(8,128)(2,1)}, u32[]{:S(2)}, u32[]{:S(2)}) %collective-permute-start.1) | collective-permute-done | bytes 4718624 | tf_op jit(solution)/shard_map/ppermute | solution.py:50
  112.5 1.8 collective-permute-start.4
  114.3 2.8 collective-permute-start
  117.1 2.8 collective-permute-start.2
  119.9 0.1 copy.12
  120.0 0.1 copy.13
  120.1 0.1 copy.14
  120.2 0.1 copy.15
  120.4 0.6 maximum_bitcast_fusion.refs_3_.refs_5_
  121.0 0.6 maximum_bitcast_fusion.1.refs_5_
  121.6 0.1 collective-permute-done.3.refs_0_.refs_2_
  121.7 99.7 %collective-permute-done.4.refs_1_.refs_3_ = bf16[192,96,128]{2,1,0:T(8,128)(2,1)} collective-permute-done((bf16[192,96,128]{2,1,0:T(8,128)(2,1)}, bf16[192,96,128]{2,1,0:T(8,128)(2,1)}, u32[]{:S(2)}, u32[]{:S(2)}) %collective-permute-start.4) | collective-permute-done | bytes 4718624 | tf_op jit(solution)/shard_map/ppermute | solution.py:50
  221.4 15.3 %project.7.refs_3_ = bf16[128,64,384]{2,1,0:T(8,128)(2,1)} custom-call(s32[1]{0:T(128)} %bitcast.5.flag_ref, bf16[192,96,128]{2,1,0:T(8,128)(2,1)} %collective-permute-done.3.refs_0_.refs_2_, bf16[192,96,128]{2,1,0:T(8,128)(2,1)} %collective-permute-done.4.refs_1_.refs_3_, bf16[1,128]{1,0:T(2,128)(2,1)} %bitcast.11, ...), custom_call_target="tpu_custom_call" | custom-call | flops 75000000 | bytes 12582912 | tf_op jit(solution)/shard_map/project/pallas_call | solution.py:107
  236.7 8.9 %project.8.refs_3_ = bf16[128,32,384]{2,1,0:T(8,128)(2,1)} custom-call(s32[1]{0:T(128)} %bitcast.5.flag_ref, bf16[192,96,128]{2,1,0:T(8,128)(2,1)} %collective-permute-done.3.refs_0_.refs_2_, bf16[192,96,128]{2,1,0:T(8,128)(2,1)} %collective-permute-done.4.refs_1_.refs_3_, bf16[1,128]{1,0:T(2,128)(2,1)} %bitcast.12, ...), custom_call_target="tpu_custom_call" | custom-call | flops 35000000 | bytes 6291456 | tf_op jit(solution)/shard_map/project/pallas_call | solution.py:107
  245.6 23.0 %project.9 = bf16[128,96,384]{2,1,0:T(8,128)(2,1)} custom-call(s32[1]{0:T(128)S(6)} %sub.17.flag_ref, bf16[192,96,128]{2,1,0:T(8,128)(2,1)} %select_select_fusion.refs_0_.refs_2_, bf16[192,96,128]{2,1,0:T(8,128)(2,1)} %collective-permute-done.1.refs_1_.refs_3_, bf16[192,96,128]{2,1,0:T(8,128)(2,1)} %collective-permute-done.3.refs_0_.refs_2_, ...), custom_call_target="tpu_custom_call" | custom-call | flops 115000000 | bytes 18874368 | tf_op jit(solution)/shard_map/project/pallas_call | solution.py:107
  268.6 0.0 collective-permute-done.refs_0_
  268.6 0.0 collective-permute-done.2.refs_1_
  268.6 23.2 %project.10.refs_1_ = bf16[128,96,384]{2,1,0:T(8,128)(2,1)} custom-call(s32[1]{0:T(128)} %bitcast.3.flag_ref.refs_0_, bf16[192,96,128]{2,1,0:T(8,128)(2,1)} %collective-permute-done.refs_0_, bf16[192,96,128]{2,1,0:T(8,128)(2,1)} %collective-permute-done.2.refs_1_, bf16[192,96,128]{2,1,0:T(8,128)(2,1)} %select_select_fusion.refs_0_.refs_2_, ...), custom_call_target="tpu_custom_call" | custom-call | flops 115000000 | bytes 18874368 | tf_op jit(solution)/shard_map/project/pallas_call | solution.py:107
  291.8 0.0 collective-permute-start.5
  291.8 0.5 collective-permute-start.6
  292.3 0.3 collective-permute-start.8
  292.6 103.8 %collective-permute-done.8.refs_1_ = bf16[192,96,128]{2,1,0:T(8,128)(2,1)} collective-permute-done((bf16[192,96,128]{2,1,0:T(8,128)(2,1)}, bf16[192,96,128]{2,1,0:T(8,128)(2,1)}, u32[]{:S(2)}, u32[]{:S(2)}) %collective-permute-start.8) | collective-permute-done | bytes 4718624 | tf_op jit(solution)/shard_map/ppermute | solution.py:50
  396.4 0.3 collective-permute-start.10
  396.7 53.7 %collective-permute-start.9 = (bf16[192,96,128]{2,1,0:T(8,128)(2,1)}, bf16[192,96,128]{2,1,0:T(8,128)(2,1)}, u32[]{:S(2)}, u32[]{:S(2)}) collective-permute-start(bf16[192,96,128]{2,1,0:T(8,128)(2,1)} %select_select_fusion.1.refs_0_), channel_id=1, source_target_pairs={{0,4},{1,5},{2,6},{3,7},{4,0},{5,1},{6,2},{7,3},{8,12},{9,13},{10,... | collective-permute-start | bytes 14155784 | tf_op jit(solution)/shard_map/ppermute | solution.py:50
  450.5 3.3 collective-permute-start.14
  453.7 23.0 %project.11.refs_3_.refs_5_ = bf16[128,96,384]{2,1,0:T(8,128)(2,1)} custom-call(s32[1]{0:T(128)} %bitcast.5.flag_ref, bf16[192,96,128]{2,1,0:T(8,128)(2,1)} %select_select_fusion.refs_0_.refs_2_, bf16[192,96,128]{2,1,0:T(8,128)(2,1)} %collective-permute-done.1.refs_1_.refs_3_, bf16[192,96,128]{2,1,0:T(8,128)(2,1)} %collective-permute-done.3.refs_0_.refs_2_, ...), custom_call_target="tpu_custom_call" | custom-call | flops 115000000 | bytes 18874368 | tf_op jit(solution)/shard_map/project/pallas_call | solution.py:107
  476.7 0.0 collective-permute-done.5.refs_2_
  476.7 0.0 collective-permute-done.6.refs_4_.refs_7_
  476.7 25.7 %triangle.4.refs_6_.refs_12_ = bf16[96,96,128]{2,1,0:T(8,128)(2,1)} custom-call(s32[1]{0:T(128)} %bitcast.3.flag_ref.refs_0_, bf16[128,96,384]{2,1,0:T(8,128)(2,1)} %project.10.refs_1_, bf16[128,96,384]{2,1,0:T(8,128)(2,1)} %collective-permute-done.5.refs_2_, bf16[128,96,384]{2,1,0:T(8,128)(2,1)} %project.11.refs_3_.refs_5_, ...), custom_call_target="tpu_custom_call" | custom-call | flops 200000000 | bytes 37748736 | tf_op jit(solution)/shard_map/triangle/pallas_call | solution.py:166
  502.4 49.3 %collective-permute-done.9.refs_2_ = bf16[192,96,128]{2,1,0:T(8,128)(2,1)} collective-permute-done((bf16[192,96,128]{2,1,0:T(8,128)(2,1)}, bf16[192,96,128]{2,1,0:T(8,128)(2,1)}, u32[]{:S(2)}, u32[]{:S(2)}) %collective-permute-start.9) | collective-permute-done | bytes 4718624 | tf_op jit(solution)/shard_map/ppermute | solution.py:50
  551.7 22.9 %project.12 = bf16[128,96,384]{2,1,0:T(8,128)(2,1)} custom-call(s32[1]{0:T(128)S(6)} %sub.17.flag_ref, bf16[192,96,128]{2,1,0:T(8,128)(2,1)} %select_select_fusion.1.refs_0_, bf16[192,96,128]{2,1,0:T(8,128)(2,1)} %collective-permute-done.8.refs_1_, bf16[192,96,128]{2,1,0:T(8,128)(2,1)} %collective-permute-done.9.refs_2_, ...), custom_call_target="tpu_custom_call" | custom-call | flops 115000000 | bytes 18874368 | tf_op jit(solution)/shard_map/project/pallas_call | solution.py:107
  574.6 2.4 collective-permute-start.16
  577.0 3.3 collective-permute-start.15
  580.3 2.4 collective-permute-start.13
  582.7 1.9 collective-permute-start.18
  584.6 23.3 %project.13.refs_3_.refs_6_ = bf16[128,96,384]{2,1,0:T(8,128)(2,1)} custom-call(s32[1]{0:T(128)} %bitcast.5.flag_ref, bf16[192,96,128]{2,1,0:T(8,128)(2,1)} %select_select_fusion.1.refs_0_, bf16[192,96,128]{2,1,0:T(8,128)(2,1)} %collective-permute-done.8.refs_1_, bf16[192,96,128]{2,1,0:T(8,128)(2,1)} %collective-permute-done.9.refs_2_, ...), custom_call_target="tpu_custom_call" | custom-call | flops 115000000 | bytes 18874368 | tf_op jit(solution)/shard_map/project/pallas_call | solution.py:107
  607.9 25.7 %triangle.5.refs_7_.refs_13_ = bf16[96,96,128]{2,1,0:T(8,128)(2,1)} custom-call(s32[1]{0:T(128)} %bitcast.3.flag_ref.refs_0_, bf16[128,96,384]{2,1,0:T(8,128)(2,1)} %project.10.refs_1_, bf16[128,96,384]{2,1,0:T(8,128)(2,1)} %collective-permute-done.5.refs_2_, bf16[128,96,384]{2,1,0:T(8,128)(2,1)} %project.13.refs_3_.refs_6_, ...), custom_call_target="tpu_custom_call" | custom-call | flops 200000000 | bytes 37748736 | tf_op jit(solution)/shard_map/triangle/pallas_call | solution.py:166
  633.6 32.4 %triangle.6.refs_8_.refs_14_ = bf16[64,192,128]{2,1,0:T(8,128)(2,1)} custom-call(s32[1]{0:T(128)} %bitcast.3.flag_ref.refs_0_, bf16[128,64,384]{2,1,0:T(8,128)(2,1)} %collective-permute-done.14.refs_1_, bf16[128,64,384]{2,1,0:T(8,128)(2,1)} %collective-permute-done.15.refs_2_, bf16[128,64,384]{2,1,0:T(8,128)(2,1)} %project.7.refs_3_, ...), custom_call_target="tpu_custom_call" | custom-call | flops 200000000 | bytes 50331648 | tf_op jit(solution)/shard_map/triangle/pallas_call | solution.py:166
  665.9 2.4 collective-permute-start.17
  668.3 1.3 collective-permute-start.20
  669.6 2.1 collective-permute-start.7
  671.7 2.1 collective-permute-start.12
  673.8 17.2 %collective-permute-start.23 = (bf16[64,192,128]{2,1,0:T(8,128)(2,1)}, bf16[64,192,128]{2,1,0:T(8,128)(2,1)}, u32[]{:S(2)}, u32[]{:S(2)}) collective-permute-start(bf16[64,192,128]{2,1,0:T(8,128)(2,1)} %triangle.6.refs_8_.refs_14_), channel_id=1, source_target_pairs={{0,1},{1,5},{4,3},{5,7},{9,12},{12,10},{13,14},{16,17},{17,21},{20... | collective-permute-start | bytes 9437192 | tf_op jit(solution)/shard_map/ppermute | solution.py:50
  691.0 8.0 collective-permute-done.20.refs_9_
  699.0 1.4 copy-done.1
  700.4 2.3 collective-permute-start.24
  702.7 1.3 collective-permute-start.21
  704.0 27.7 %triangle.7.refs_8_.refs_14_ = bf16[32,192,128]{2,1,0:T(8,128)(2,1)} custom-call(s32[1]{0:T(128)} %bitcast.3.flag_ref.refs_0_, bf16[128,32,384]{2,1,0:T(8,128)(2,1)} %collective-permute-done.13.refs_1_, bf16[128,32,384]{2,1,0:T(8,128)(2,1)} %collective-permute-done.17.refs_2_, bf16[128,32,384]{2,1,0:T(8,128)(2,1)} %project.8.refs_3_, ...), custom_call_target="tpu_custom_call" | custom-call | flops 200000000 | bytes 44040192 | tf_op jit(solution)/shard_map/triangle/pallas_call | solution.py:166
  731.7 1.4 collective-permute-start.19
  733.1 0.8 collective-permute-start.22
  733.9 0.6 pad_add_fusion.refs_0_
  734.5 38.2 %collective-permute-done.21.refs_10_ = bf16[96,96,128]{2,1,0:T(8,128)(2,1)} collective-permute-done((bf16[96,96,128]{2,1,0:T(8,128)(2,1)}, bf16[96,96,128]{2,1,0:T(8,128)(2,1)}, u32[]{:S(2)}, u32[]{:S(2)}) %collective-permute-start.21) | collective-permute-done | bytes 2359328 | tf_op jit(solution)/shard_map/ppermute | solution.py:50
  772.7 17.6 %finish.2.refs_16_ = bf16[192,192,128]{2,1,0:T(8,128)(2,1)} custom-call(s32[2]{0:T(128)} %pad_add_fusion.refs_0_, bf16[192,192,128]{2,1,0:T(8,128)(2,1)} %refs_1_.3, f32[192,192,128]{2,1,0:T(8,128)} %out_gate.1.refs_2_, bf16[96,96,128]{2,1,0:T(8,128)(2,1)} %collective-permute-done.7.refs_3_, bf16[96,96,128]{2,1,0:T(8,128)(2,1)} %collective-permute-done.12.refs_4_, ...), custom_call_target="tpu_custom_call" | custom-call | flops 40000000 | bytes 23592960 | tf_op jit(solution)/shard_map/finish/pallas_call | solution.py:249
  790.3 1.1 copy-done.2
  791.5 1.2 copy-done.3
  792.7 11.3 %finish.3 = bf16[192,192,128]{2,1,0:T(8,128)(2,1)} custom-call(s32[2]{0:T(128)} %pad_add_fusion.refs_0_, bf16[192,192,128]{2,1,0:T(8,128)(2,1)} %refs_1_.3, f32[192,192,128]{2,1,0:T(8,128)} %out_gate.1.refs_2_, bf16[96,96,128]{2,1,0:T(8,128)(2,1)} %collective-permute-done.7.refs_3_, ...), custom_call_target="tpu_custom_call", output_to_operand_aliasing={{}: (16, {})} | custom-call | flops 40000000 | bytes 23592960 | tf_op jit(solution)/shard_map/finish/pallas_call | solution.py:249
  (29 shorter events, 0.1 us)
Async XLA Ops:
  1.1 9.3 %copy-start.4 = (s32[192,192]{1,0:T(8,128)S(1)}, s32[192,192]{1,0:T(8,128)}, u32[]{:S(2)}) copy-start(s32[192,192]{1,0:T(8,128)} %param.11) | copy-start | bytes 442372
  7.4 105.1 %collective-permute-start.1 = (bf16[192,96,128]{2,1,0:T(8,128)(2,1)}, bf16[192,96,128]{2,1,0:T(8,128)(2,1)}, u32[]{:S(2)}, u32[]{:S(2)}) collective-permute-start(bf16[192,96,128]{2,1,0:T(8,128)(2,1)} %select_select_fusion.1.refs_0_), channel_id=1, source_target_pairs={{0,2},{1,3},{2,0},{3,1},{4,6},{5,7},{6,4},{7,5},{8,10},{9,11},{10,... | collective-permute-start | bytes 14155784 | tf_op jit(solution)/shard_map/ppermute | solution.py:50
  16.7 105.0 %collective-permute-start.3 = (bf16[192,96,128]{2,1,0:T(8,128)(2,1)}, bf16[192,96,128]{2,1,0:T(8,128)(2,1)}, u32[]{:S(2)}, u32[]{:S(2)}) collective-permute-start(bf16[192,96,128]{2,1,0:T(8,128)(2,1)} %select_select_fusion.refs_0_.refs_2_), channel_id=1, source_target_pairs={{0,4},{1,5},{2,6},{3,7},{4,0},{5,1},{6,2},{7,3},{8,12},{9,13},{10,... | collective-permute-start | bytes 14155784 | tf_op jit(solution)/shard_map/ppermute | solution.py:50
  18.3 101.5 %copy-start.5 = (bf16[128,128]{1,0:T(8,128)(2,1)S(1)}, bf16[128,128]{1,0:T(8,128)(2,1)}, u32[]{:S(2)}) copy-start(bf16[128,128]{1,0:T(8,128)(2,1)} %param.13) | copy-start | bytes 98308
  18.3 101.7 %copy-start.6 = (bf16[128,128]{1,0:T(8,128)(2,1)S(1)}, bf16[128,128]{1,0:T(8,128)(2,1)}, u32[]{:S(2)}) copy-start(bf16[128,128]{1,0:T(8,128)(2,1)} %param.14) | copy-start | bytes 98308
  18.3 101.8 %copy-start.7 = (bf16[128,128]{1,0:T(8,128)(2,1)S(1)}, bf16[128,128]{1,0:T(8,128)(2,1)}, u32[]{:S(2)}) copy-start(bf16[128,128]{1,0:T(8,128)(2,1)} %param.15) | copy-start | bytes 98308
  18.3 101.9 %copy-start.8 = (bf16[128,128]{1,0:T(8,128)(2,1)S(1)}, bf16[128,128]{1,0:T(8,128)(2,1)}, u32[]{:S(2)}) copy-start(bf16[128,128]{1,0:T(8,128)(2,1)} %param.16) | copy-start | bytes 98308
  112.5 108.9 %collective-permute-start.4 = (bf16[192,96,128]{2,1,0:T(8,128)(2,1)}, bf16[192,96,128]{2,1,0:T(8,128)(2,1)}, u32[]{:S(2)}, u32[]{:S(2)}) collective-permute-start(bf16[192,96,128]{2,1,0:T(8,128)(2,1)} %collective-permute-done.1.refs_1_.refs_3_), channel_id=1, source_target_pairs={{0,4},{1,5},{2,6},{3,7},{4,0},{5,1},{6,2},{7,3},{8,12},{9,13},{10,... | collective-permute-start | bytes 14155784 | tf_op jit(solution)/shard_map/ppermute | solution.py:50
  114.3 154.3 %collective-permute-start = (bf16[192,96,128]{2,1,0:T(8,128)(2,1)}, bf16[192,96,128]{2,1,0:T(8,128)(2,1)}, u32[]{:S(2)}, u32[]{:S(2)}) collective-permute-start(bf16[192,96,128]{2,1,0:T(8,128)(2,1)} %select_select_fusion.refs_0_.refs_2_), channel_id=1, source_target_pairs={{4,8},{5,9},{6,10},{7,11},{8,4},{9,5},{10,6},{11,7},{20,24},{21,25... | collective-permute-start | bytes 14155784 | tf_op jit(solution)/shard_map/ppermute | solution.py:50
  117.1 151.5 %collective-permute-start.2 = (bf16[192,96,128]{2,1,0:T(8,128)(2,1)}, bf16[192,96,128]{2,1,0:T(8,128)(2,1)}, u32[]{:S(2)}, u32[]{:S(2)}) collective-permute-start(bf16[192,96,128]{2,1,0:T(8,128)(2,1)} %collective-permute-done.1.refs_1_.refs_3_), channel_id=1, source_target_pairs={{4,8},{5,9},{6,10},{7,11},{8,4},{9,5},{10,6},{11,7},{20,24},{21,25... | collective-permute-start | bytes 14155784 | tf_op jit(solution)/shard_map/ppermute | solution.py:50
  291.8 184.9 %collective-permute-start.5 = (bf16[128,96,384]{2,1,0:T(8,128)(2,1)}, bf16[128,96,384]{2,1,0:T(8,128)(2,1)}, u32[]{:S(2)}, u32[]{:S(2)}) collective-permute-start(bf16[128,96,384]{2,1,0:T(8,128)(2,1)} %project.10.refs_1_), channel_id=1, source_target_pairs={{0,1},{1,0},{2,3},{3,2},{4,5},{5,4},{6,7},{7,6},{8,9},{9,8},{10,11... | collective-permute-start | bytes 28311560 | tf_op jit(solution)/shard_map/ppermute | solution.py:50
  291.8 184.9 %collective-permute-start.6 = (bf16[128,96,384]{2,1,0:T(8,128)(2,1)}, bf16[128,96,384]{2,1,0:T(8,128)(2,1)}, u32[]{:S(2)}, u32[]{:S(2)}) collective-permute-start(bf16[128,96,384]{2,1,0:T(8,128)(2,1)} %project.9), channel_id=1, source_target_pairs={{0,1},{1,0},{2,3},{3,2},{4,5},{5,4},{6,7},{7,6},{8,9},{9,8},{10,11... | collective-permute-start | bytes 28311560 | tf_op jit(solution)/shard_map/ppermute | solution.py:50
  292.3 104.1 %collective-permute-start.8 = (bf16[192,96,128]{2,1,0:T(8,128)(2,1)}, bf16[192,96,128]{2,1,0:T(8,128)(2,1)}, u32[]{:S(2)}, u32[]{:S(2)}) collective-permute-start(bf16[192,96,128]{2,1,0:T(8,128)(2,1)} %select_select_fusion.refs_0_.refs_2_), channel_id=1, source_target_pairs={{0,2},{1,3},{2,0},{3,1},{4,6},{5,7},{6,4},{7,5},{8,10},{9,11},{10,... | collective-permute-start | bytes 14155784 | tf_op jit(solution)/shard_map/ppermute | solution.py:50
  396.4 106.0 %collective-permute-start.10 = (bf16[192,96,128]{2,1,0:T(8,128)(2,1)}, bf16[192,96,128]{2,1,0:T(8,128)(2,1)}, u32[]{:S(2)}, u32[]{:S(2)}) collective-permute-start(bf16[192,96,128]{2,1,0:T(8,128)(2,1)} %collective-permute-done.3.refs_0_.refs_2_), channel_id=1, source_target_pairs={{0,2},{1,3},{2,0},{3,1},{4,6},{5,7},{6,4},{7,5},{8,10},{9,11},{10,... | collective-permute-start | bytes 14155784 | tf_op jit(solution)/shard_map/ppermute | solution.py:50
  396.7 154.9 %collective-permute-start.9 = (bf16[192,96,128]{2,1,0:T(8,128)(2,1)}, bf16[192,96,128]{2,1,0:T(8,128)(2,1)}, u32[]{:S(2)}, u32[]{:S(2)}) collective-permute-start(bf16[192,96,128]{2,1,0:T(8,128)(2,1)} %select_select_fusion.1.refs_0_), channel_id=1, source_target_pairs={{0,4},{1,5},{2,6},{3,7},{4,0},{5,1},{6,2},{7,3},{8,12},{9,13},{10,... | collective-permute-start | bytes 14155784 | tf_op jit(solution)/shard_map/ppermute | solution.py:50
  450.5 126.5 %collective-permute-start.14 = (bf16[128,64,384]{2,1,0:T(8,128)(2,1)}, bf16[128,64,384]{2,1,0:T(8,128)(2,1)}, u32[]{:S(2)}, u32[]{:S(2)}) collective-permute-start(bf16[128,64,384]{2,1,0:T(8,128)(2,1)} %project.7.refs_3_), channel_id=1, source_target_pairs={{4,8},{5,9},{6,10},{7,11},{8,4},{9,5},{10,6},{11,7},{20,24},{21,25... | collective-permute-start | bytes 18874376 | tf_op jit(solution)/shard_map/ppermute | solution.py:50
  574.6 33.3 %collective-permute-start.11 = (bf16[128,96,384]{2,1,0:T(8,128)(2,1)}, bf16[128,96,384]{2,1,0:T(8,128)(2,1)}, u32[]{:S(2)}, u32[]{:S(2)}) collective-permute-start(bf16[128,96,384]{2,1,0:T(8,128)(2,1)} %project.12), channel_id=1, source_target_pairs={{0,1},{1,0},{2,3},{3,2},{4,5},{5,4},{6,7},{7,6},{8,9},{9,8},{10,11... | collective-permute-start | bytes 28311560 | tf_op jit(solution)/shard_map/ppermute | solution.py:50
  574.6 59.0 %collective-permute-start.16 = (bf16[128,64,384]{2,1,0:T(8,128)(2,1)}, bf16[128,64,384]{2,1,0:T(8,128)(2,1)}, u32[]{:S(2)}, u32[]{:S(2)}) collective-permute-start(bf16[128,64,384]{2,1,0:T(8,128)(2,1)} %project.7.refs_3_), channel_id=1, source_target_pairs={{0,1},{1,0},{2,3},{3,2},{12,13},{13,12},{14,15},{15,14},{16,17},{1... | collective-permute-start | bytes 18874376 | tf_op jit(solution)/shard_map/ppermute | solution.py:50
  577.0 56.6 %collective-permute-start.15 = (bf16[128,64,384]{2,1,0:T(8,128)(2,1)}, bf16[128,64,384]{2,1,0:T(8,128)(2,1)}, u32[]{:S(2)}, u32[]{:S(2)}) collective-permute-start(bf16[128,64,384]{2,1,0:T(8,128)(2,1)} %collective-permute-done.14.refs_1_), channel_id=1, source_target_pairs={{4,5},{5,4},{6,7},{7,6},{8,9},{9,8},{10,11},{11,10},{20,21},{21,20... | collective-permute-start | bytes 18874376 | tf_op jit(solution)/shard_map/ppermute | solution.py:50
  580.3 85.6 %collective-permute-start.13 = (bf16[128,32,384]{2,1,0:T(8,128)(2,1)}, bf16[128,32,384]{2,1,0:T(8,128)(2,1)}, u32[]{:S(2)}, u32[]{:S(2)}) collective-permute-start(bf16[128,32,384]{2,1,0:T(8,128)(2,1)} %project.8.refs_3_), channel_id=1, source_target_pairs={{4,8},{5,9},{6,10},{7,11},{8,4},{9,5},{10,6},{11,7},{20,24},{21,25... | collective-permute-start | bytes 9437192 | tf_op jit(solution)/shard_map/ppermute | solution.py:50
  582.7 91.1 %collective-permute-start.18 = (bf16[128,32,384]{2,1,0:T(8,128)(2,1)}, bf16[128,32,384]{2,1,0:T(8,128)(2,1)}, u32[]{:S(2)}, u32[]{:S(2)}) collective-permute-start(bf16[128,32,384]{2,1,0:T(8,128)(2,1)} %project.8.refs_3_), channel_id=1, source_target_pairs={{0,1},{1,0},{2,3},{3,2},{12,13},{13,12},{14,15},{15,14},{16,17},{1... | collective-permute-start | bytes 9437192 | tf_op jit(solution)/shard_map/ppermute | solution.py:50
  633.5 34.8 %copy-start = (bf16[96,96,128]{2,1,0:T(8,128)(2,1)S(1)}, bf16[96,96,128]{2,1,0:T(8,128)(2,1)}, u32[]{:S(2)}) copy-start(bf16[96,96,128]{2,1,0:T(8,128)(2,1)} %triangle.4.refs_6_.refs_12_) | copy-start | bytes 7077892
  665.9 36.8 %collective-permute-start.17 = (bf16[128,32,384]{2,1,0:T(8,128)(2,1)}, bf16[128,32,384]{2,1,0:T(8,128)(2,1)}, u32[]{:S(2)}, u32[]{:S(2)}) collective-permute-start(bf16[128,32,384]{2,1,0:T(8,128)(2,1)} %collective-permute-done.13.refs_1_), channel_id=1, source_target_pairs={{4,5},{5,4},{6,7},{7,6},{8,9},{9,8},{10,11},{11,10},{20,21},{21,20... | collective-permute-start | bytes 9437192 | tf_op jit(solution)/shard_map/ppermute | solution.py:50
  668.3 30.7 %collective-permute-start.20 = (bf16[96,96,128]{2,1,0:T(8,128)(2,1)S(1)}, bf16[96,96,128]{2,1,0:T(8,128)(2,1)S(1)}, u32[]{:S(2)}, u32[]{:S(2)}) collective-permute-start(bf16[96,96,128]{2,1,0:T(8,128)(2,1)S(1)} %copy-done), channel_id=1, source_target_pairs={{2,0},{3,4},{6,2},{7,6},{10,9},{11,13},{14,11},{18,16},{19,20},{22... | collective-permute-start | bytes 7077896 | tf_op jit(solution)/shard_map/ppermute | solution.py:50
  669.6 62.1 %collective-permute-start.7 = (bf16[96,96,128]{2,1,0:T(8,128)(2,1)S(1)}, bf16[96,96,128]{2,1,0:T(8,128)(2,1)}, u32[]{:S(2)}, u32[]{:S(2)}) collective-permute-start(bf16[96,96,128]{2,1,0:T(8,128)(2,1)S(1)} %copy-done), channel_id=1, source_target_pairs={{1,4},{4,2},{5,6},{8,9},{9,13},{12,11},{13,15},{17,20},{20,18},{21... | collective-permute-start | bytes 7077896 | tf_op jit(solution)/shard_map/ppermute | solution.py:50
  671.7 61.4 %collective-permute-start.12 = (bf16[96,96,128]{2,1,0:T(8,128)(2,1)}, bf16[96,96,128]{2,1,0:T(8,128)(2,1)}, u32[]{:S(2)}, u32[]{:S(2)}) collective-permute-start(bf16[96,96,128]{2,1,0:T(8,128)(2,1)} %triangle.5.refs_7_.refs_13_), channel_id=1, source_target_pairs={{1,4},{4,2},{5,6},{8,9},{9,13},{12,11},{13,15},{17,20},{20,18},{21... | collective-permute-start | bytes 7077896 | tf_op jit(solution)/shard_map/ppermute | solution.py:50
  673.8 98.9 %collective-permute-start.23 = (bf16[64,192,128]{2,1,0:T(8,128)(2,1)}, bf16[64,192,128]{2,1,0:T(8,128)(2,1)}, u32[]{:S(2)}, u32[]{:S(2)}) collective-permute-start(bf16[64,192,128]{2,1,0:T(8,128)(2,1)} %triangle.6.refs_8_.refs_14_), channel_id=1, source_target_pairs={{0,1},{1,5},{4,3},{5,7},{9,12},{12,10},{13,14},{16,17},{17,21},{20... | collective-permute-start | bytes 9437192 | tf_op jit(solution)/shard_map/ppermute | solution.py:50
  699.0 1.4 copy-start.1
  700.4 72.3 %collective-permute-start.24 = (bf16[64,192,128]{2,1,0:T(8,128)(2,1)}, bf16[64,192,128]{2,1,0:T(8,128)(2,1)}, u32[]{:S(2)}, u32[]{:S(2)}) collective-permute-start(bf16[64,192,128]{2,1,0:T(8,128)(2,1)} %triangle.6.refs_8_.refs_14_), channel_id=1, source_target_pairs={{2,1},{3,5},{6,3},{10,8},{11,12},{14,10},{15,14},{18,17},{19,21},{... | collective-permute-start | bytes 9437192 | tf_op jit(solution)/shard_map/ppermute | solution.py:50
  702.7 70.0 %collective-permute-start.21 = (bf16[96,96,128]{2,1,0:T(8,128)(2,1)}, bf16[96,96,128]{2,1,0:T(8,128)(2,1)}, u32[]{:S(2)}, u32[]{:S(2)}) collective-permute-start(bf16[96,96,128]{2,1,0:T(8,128)(2,1)} %triangle.5.refs_7_.refs_13_), channel_id=1, source_target_pairs={{2,0},{3,4},{6,2},{7,6},{10,9},{11,13},{14,11},{18,16},{19,20},{22... | collective-permute-start | bytes 7077896 | tf_op jit(solution)/shard_map/ppermute | solution.py:50
  731.7 58.6 %collective-permute-start.19 = (bf16[32,192,128]{2,1,0:T(8,128)(2,1)}, bf16[32,192,128]{2,1,0:T(8,128)(2,1)S(1)}, u32[]{:S(2)}, u32[]{:S(2)}) collective-permute-start(bf16[32,192,128]{2,1,0:T(8,128)(2,1)} %triangle.7.refs_8_.refs_14_), channel_id=1, source_target_pairs={{0,1},{1,5},{4,3},{5,7},{9,12},{12,10},{13,14},{16,17},{17,21},{20... | collective-permute-start | bytes 4718600 | tf_op jit(solution)/shard_map/ppermute | solution.py:50
  733.1 57.2 %collective-permute-start.22 = (bf16[32,192,128]{2,1,0:T(8,128)(2,1)}, bf16[32,192,128]{2,1,0:T(8,128)(2,1)S(1)}, u32[]{:S(2)}, u32[]{:S(2)}) collective-permute-start(bf16[32,192,128]{2,1,0:T(8,128)(2,1)} %triangle.7.refs_8_.refs_14_), channel_id=1, source_target_pairs={{2,1},{3,5},{6,3},{10,8},{11,12},{14,10},{15,14},{18,17},{19,21},{... | collective-permute-start | bytes 4718600 | tf_op jit(solution)/shard_map/ppermute | solution.py:50
  790.3 1.2 copy-start.2
  791.5 1.2 copy-start.3

commit v3 on v2

--- a/solution.py
+++ b/solution.py
@@ -73,27 +73,51 @@
     return lax.dot_general(lhs, rhs, (((1,), (1,)), ((), ())), preferred_element_type=F32)
 
 
-def project_body(pieces, gain_ref, w_ref, out_ref, s_ref):
-    tri = s_ref.shape[1]
+def prepare(pieces, gain_ref):
     gain = gain_ref[...].astype(F32)
     x = jnp.concatenate([normed(p.astype(F32), gain) for p in pieces], axis=0)
-    x = jnp.swapaxes(x, 0, 1)
+    return jnp.swapaxes(x, 0, 1)
+
+
+def project_body(x, w_ref, out_ref, s_ref):
+    tri = s_ref.shape[1]
     for i in range(x.shape[0]):
         proj = dot_nt(w_ref[...], x[i])
         s_ref[i] = jax.nn.sigmoid(proj[tri:]) * proj[:tri]
     out_ref[...] = jnp.swapaxes(s_ref[...], 0, 1).astype(BF16)
 
 
-def project_kernel(flag_ref, *refs):
-    *piece_refs, gain_ref, w_ref, out_ref, s_ref = refs
+def norm_kernel(p0_ref, p1_ref, gain_ref, x_ref):
+    x_ref[...] = prepare((p0_ref[...], p1_ref[...]), gain_ref)
+
+
+def norm(pieces, gain, blk=16):
+    rows, cols, dim = pieces[0].shape
+    return pl.pallas_call(
+        norm_kernel,
+        grid=(cols // blk,),
+        in_specs=[pl.BlockSpec((rows, blk, dim), lambda g: (0, g, 0))] * 2 + [pl.BlockSpec((1, dim), lambda g: (0, 0))],
+        out_specs=pl.BlockSpec((blk, 2 * rows, dim), lambda g: (g, 0, 0)),
+        out_shape=jax.ShapeDtypeStruct((cols, 2 * rows, dim), BF16),
+        compiler_params=params(),
+        cost_estimate=cost(12, 8 * rows * cols * dim),
+        name='norm',
+    )(*pieces, gain)
+
+
+def project_kernel(n_piece, flag_ref, *refs):
+    piece_refs, (gain_ref, w_ref, out_ref, *x_refs, s_ref) = refs[:n_piece], refs[n_piece:]
     pieces = [ref[...] for ref in piece_refs]
     if len(pieces) == 4:
         pick = flag_ref[0] != 0
         pieces = [jnp.where(pick, yes, no) for yes, no in zip(pieces[:2], pieces[2:])]
-    project_body(pieces, gain_ref, w_ref, out_ref, s_ref)
-
-
-def project(flag, yes, no, gain, w_t, first=0, count=None, blk=16):
+    x = prepare(pieces, gain_ref)
+    for x_ref in x_refs:
+        x_ref[...] = x
+    project_body(x, w_ref, out_ref, s_ref)
+
+
+def project(flag, yes, no, gain, w_t, first=0, count=None, blk=16, with_x=False):
     rows, cols, dim = yes[0].shape
     count = count or cols
     blk = min(blk, count)
@@ -104,20 +128,56 @@
     if no:
         specs += [pl.BlockSpec((rows, blk, dim), lambda g, f: (0, at + g * (1 - f[0]), 0))] * 2
     whole = [pl.BlockSpec((1, dim), lambda g, f: (0, 0)), pl.BlockSpec((wide, dim), lambda g, f: (0, 0))]
-    return pl.pallas_call(
-        project_kernel,
+    out_specs = [pl.BlockSpec((tri, blk, 2 * rows), lambda g, f: (0, g, 0)), pl.BlockSpec((blk, 2 * rows, dim), lambda g, f: (g, 0, 0))]
+    out_shape = [jax.ShapeDtypeStruct((tri, count, 2 * rows), BF16), jax.ShapeDtypeStruct((count, 2 * rows, dim), BF16)]
+    n_piece, n_out = len(specs), 2 if with_x else 1
+    out = pl.pallas_call(
+        lambda *refs: project_kernel(n_piece, *refs),
         grid_spec=pltpu.PrefetchScalarGridSpec(
             num_scalar_prefetch=1,
             grid=(count // blk,),
             in_specs=specs + whole,
-            out_specs=pl.BlockSpec((tri, blk, 2 * rows), lambda g, f: (0, g, 0)),
+            out_specs=out_specs[:n_out],
             scratch_shapes=[pltpu.VMEM((blk, tri, 2 * rows), F32)],
         ),
-        out_shape=jax.ShapeDtypeStruct((tri, count, 2 * rows), BF16),
+        out_shape=out_shape[:n_out],
         compiler_params=params(),
         cost_estimate=cost(23 * count // cols, 4 * rows * count * (dim + tri)),
         name='project',
     )(flag, *yes, *(no or ()), gain, w_t)
+    return out if with_x else out[0]
+
+
+def project_x_kernel(n_first, flag_ref, yes_ref, no0_ref, no1_ref, w_ref, out_ref, s_ref):
+    no = jnp.where(pl.program_id(0) < n_first, no0_ref[...], no1_ref[...])
+    project_body(jnp.where(flag_ref[0] != 0, yes_ref[...], no), w_ref, out_ref, s_ref)
+
+
+def project_x(flag, yes, no, w_t, blk=16):
+    cols, deep, dim = yes.shape
+    wide = w_t.shape[0]
+    tri = wide // 2
+    blk = math.gcd(blk, math.gcd(no[0].shape[0], no[1].shape[0]))
+    n_first = no[0].shape[0] // blk
+    return pl.pallas_call(
+        lambda *refs: project_x_kernel(n_first, *refs),
+        grid_spec=pltpu.PrefetchScalarGridSpec(
+            num_scalar_prefetch=1,
+            grid=(cols // blk,),
+            in_specs=[
+                pl.BlockSpec((blk, deep, dim), lambda g, f: (g * f[0], 0, 0)),
+                pl.BlockSpec((blk, deep, dim), lambda g, f: (jnp.minimum(g, n_first - 1) * (1 - f[0]), 0, 0)),
+                pl.BlockSpec((blk, deep, dim), lambda g, f: (jnp.maximum(g - n_first, 0) * (1 - f[0]), 0, 0)),
+                pl.BlockSpec((wide, dim), lambda g, f: (0, 0)),
+            ],
+            out_specs=pl.BlockSpec((tri, blk, deep), lambda g, f: (0, g, 0)),
+            scratch_shapes=[pltpu.VMEM((blk, tri, deep), F32)],
+        ),
+        out_shape=jax.ShapeDtypeStruct((tri, cols, deep), BF16),
+        compiler_params=params(),
+        cost_estimate=cost(14, 2 * cols * deep * (dim + tri)),
+        name='project_x',
+    )(flag, yes, *no, w_t)
 
 
 def triangle_kernel(n_pair, n_part, flag_ref, *refs):
@@ -129,15 +189,19 @@
     tri, pitch = n_h * steps, n_i + 8
     spans = [(at, min(128, n_j - at)) for at in range(0, n_j, 128)]
     pick = flag_ref[0] != 0
-    for h in range(n_h):
-        a_0, a_1 = a_refs[0][h], a_refs[1][h]
-        if n_pair == 2:
-            a_0, a_1 = jnp.where(pick, a_0, a_refs[2][h]), jnp.where(pick, a_1, a_refs[3][h])
-        acc = dot_nt(a_0, jnp.concatenate([ref[h] for ref in b_refs[:n_part]], axis=0))
-        acc += dot_nt(a_1, jnp.concatenate([ref[h] for ref in b_refs[n_part:]], axis=0))
-        start = pl.multiple_of((step * n_h + h) * pitch, 8)
-        for (at, width), o_ref in zip(spans, o_refs):
-            o_ref[pl.ds(start, n_i), :width] = acc[:, at:at + width]
+
+    @pl.loop(0, n_h, step=8)
+    def _(group):
+        for k in range(8):
+            h = group + k
+            a_0, a_1 = a_refs[0][h], a_refs[1][h]
+            if n_pair == 2:
+                a_0, a_1 = jnp.where(pick, a_0, a_refs[2][h]), jnp.where(pick, a_1, a_refs[3][h])
+            acc = dot_nt(a_0, jnp.concatenate([ref[h] for ref in b_refs[:n_part]], axis=0))
+            acc += dot_nt(a_1, jnp.concatenate([ref[h] for ref in b_refs[n_part:]], axis=0))
+            start = pl.multiple_of((step * n_h + h) * pitch, 8)
+            for (at, width), o_ref in zip(spans, o_refs):
+                o_ref[pl.ds(start, n_i), :width] = acc[:, at:at + width]
 
     @pl.when(step == steps - 1)
     def _():
@@ -155,7 +219,7 @@
                     out_ref[first + i, pl.ds(at, width), :] = (unit.T * gain).astype(BF16)
 
 
-def triangle(flag, a_pairs, b_parts, gain, blk=8):
+def triangle(flag, a_pairs, b_parts, gain, blk=16):
     n_pair, n_part = len(a_pairs), len(b_parts) // 2
     tri, n_i, n_k = a_pairs[0][0].shape
     part_j = b_parts[0].shape[1]
@@ -293,24 +357,25 @@
         yz_b = send(after(z_a, y_b), TO_Y)
 
         keep = ((z % 2) == c).astype(jnp.int32)[None]
-        sets = [((t_a, y_a), (z_a, yz_a)), ((t_b, y_b), (z_b, yz_b))]
+        seconds = (t_b, y_b), (z_b, yz_b)
         big = half_cols * 2 // 3
         small = half_cols - big
-        a_1 = project(keep, (z_a, yz_a), None, gain_in, w_a, 0, big)
-        a_2 = project(keep, (z_a, yz_a), None, gain_in, after(w_a, a_1), big, small)
+        x_own = norm((t_a, y_a), gain_in)
+        a_1, x_1 = project(keep, (z_a, yz_a), None, gain_in, after(w_a, x_own), 0, big, with_x=True)
+        a_2, x_2 = project(keep, (z_a, yz_a), None, gain_in, after(w_a, a_1), big, small, with_x=True)
         got_1, got_2 = send(a_1, ACROSS), send(a_2, ACROSS)
-        give_0 = project(1 - keep, *sets[0], gain_in, after(w_b, a_2))
+        give_0 = project_x(1 - keep, x_own, (x_1, x_2), after(w_b, a_2))
         a_0 = project(inner_flag, (m_0, m_1), (t_a, y_a), gain_in, after(w_a, give_0))
         a_pair = [(a_0, send(a_0, TO_CORE))]
-        keep_0 = project(keep, *sets[0], gain_in, after(w_b, a_0))
+        keep_0 = project_x(keep, x_own, (x_1, x_2), after(w_b, a_0))
         b_0 = [keep_0, send(give_0, TO_CORE)]
         done_0 = triangle(inner_flag, a_pair, b_0, gain_out)
-        give_1 = project(1 - keep, *sets[1], gain_in, after(w_b, done_0))
-        keep_1 = project(keep, *sets[1], gain_in, after(w_b, give_1))
+        give_1 = project(1 - keep, *seconds, gain_in, after(w_b, done_0))
+        keep_1 = project(keep, *seconds, gain_in, after(w_b, give_1))
         b_1 = [keep_1, send(give_1, TO_CORE)]
         b_parts = [b_0[0], b_1[0], b_0[1], b_1[1]]
         done_1 = triangle(inner_flag, a_pair, b_1, gain_out)
-        pair_1 = [(got_1, send(got_1, INNER_CORE)), (a_1, send(a_1, OUTER_CORE))]
+        pair_1 = [(got_1, send(after(got_1, keep_1), INNER_CORE)), (a_1, send(a_1, OUTER_CORE))]
         done_2 = triangle(inner_flag, pair_1, b_parts, after(gain_out, done_1))
         pair_2 = [(got_2, send(after(got_2, done_2), INNER_CORE)), (a_2, send(a_2, OUTER_CORE))]
         done_3 = triangle(inner_flag, pair_2, b_parts, after(gain_out, done_2))

time: 806 us -> 805 us (level)
  starting transfers between devices: 111 us -> 196 us
  waiting for transfers between devices: 374 us -> 299 us
  Pallas kernels: 299 us -> 287 us
    ppermute x25, starting transfers between devices: 111 us -> 196 us  [send(): return lax.ppermute(value, AXES, pairs)]
    ppermute x25, waiting for transfers between devices: 374 us -> 299 us  [send(): return lax.ppermute(value, AXES, pairs)]
    pallas_call x4, Pallas kernels: 111 us -> 99.4 us  [triangle(): pl.pallas_call(lambda *refs: triangle_kernel(n_pair, n_part, *refs), grid...]
    pallas_call x7 -> x8, Pallas kernels: 139 us -> 140 us  [the longest x5 95.4 us: project(): pl.pallas_call(lambda *refs: project_kernel(n_piece, *refs), grid_spec=pl...]
  transfers between devices with their start and end apart: 25 -> 25, of which waited for: 7 -> 6; matrix products, arithmetic and copies ran while one was open for 1% -> 1% of each run, Pallas kernels for 33% -> 31%
where the time goes in v3:
time: 805 us; the launch traced here: 803 us
  waiting for transfers between devices  299 us (37%)
  Pallas kernels  287 us (36%)
  starting transfers between devices  196 us (24%)
  other arithmetic  15.6 us (2%)
    ppermute x25, waiting for transfers between devices, send(): return lax.ppermute(value, AXES, pairs)  299 us
    ppermute x25, starting transfers between devices, send(): return lax.ppermute(value, AXES, pairs)  196 us
    pallas_call x4, Pallas kernels, triangle(): pl.pallas_call(lambda *refs: triangle_kernel(n_pair, n_part, *refs), grid...  99.4 us
    pallas_call x5, Pallas kernels, project(): pl.pallas_call(lambda *refs: project_kernel(n_piece, *refs), grid_spec=pl...  95.4 us
    pallas_call x2, Pallas kernels, project_x(): pl.pallas_call(lambda *refs: project_x_kernel(n_first, *refs), grid_spec=...  29.7 us
    pallas_call x2, Pallas kernels, finish(): pl.pallas_call(lambda *refs: finish_kernel(sizes, *refs), grid_spec=pltpu...  29 us
    pallas_call x1, Pallas kernels, out_gate(): pl.pallas_call(gate_kernel, grid=(rows // blk,), in_specs=[spec, pl.Block...  18.9 us
  transfers between devices with their start and end apart: 25, of which 6 were waited for; matrix products, arithmetic and copies ran while one was open for 1% of the time, Pallas kernels for 31%

profile of v3, /device:TPU:0, one launch (start us, length us, event | category | flops | bytes accessed | tf_op | source)
XLA Modules:
  0.0 803.3 jit_solution(15133944268126915897)
XLA Ops:
  0.0 1.1 select_compare_fusion.1
  1.1 0.0 copy-start.4
  1.1 6.3 select_select_fusion.1.refs_1_
  7.4 3.0 collective-permute-start.1
  10.4 0.1 select_compare_fusion
  10.5 6.2 select_select_fusion.p0_ref.refs_3_
  16.7 1.6 collective-permute-start.3
  18.3 18.9 %out_gate.1.refs_2_ = f32[192,192,128]{2,1,0:T(8,128)} custom-call(bf16[192,192,128]{2,1,0:T(8,128)(2,1)} %refs_1_.3, bf16[1,128]{1,0:T(2,128)(2,1)} %bitcast.10, bf16[128,128]{1,0:T(8,128)(2,1)} %wg_ref.1), custom_call_target="tpu_custom_call" | custom-call | flops 90000000 | bytes 28311552 | tf_op jit(solution)/shard_map/out_gate/pallas_call | solution.py:256
  37.2 75.3 %collective-permute-done.1.p1_ref.refs_4_ = bf16[192,96,128]{2,1,0:T(8,128)(2,1)} collective-permute-done((bf16[192,96,128]{2,1,0:T(8,128)(2,1)}, bf16[192,96,128]{2,1,0:T(8,128)(2,1)}, u32[]{:S(2)}, u32[]{:S(2)}) %collective-permute-start.1) | collective-permute-done | bytes 4718624 | tf_op jit(solution)/shard_map/ppermute | solution.py:50
  112.5 1.8 collective-permute-start.4
  114.3 2.8 collective-permute-start
  117.1 2.8 collective-permute-start.2
  119.9 0.1 copy.13
  120.0 0.1 copy.12
  120.2 0.1 copy.15
  120.3 0.1 copy.14
  120.4 0.6 maximum_bitcast_fusion.refs_4_.refs_6_
  121.0 0.6 maximum_bitcast_fusion.1.refs_4_.refs_6_
  121.7 15.1 %norm.1.refs_1_ = bf16[96,384,128]{2,1,0:T(8,128)(2,1)} custom-call(bf16[192,96,128]{2,1,0:T(8,128)(2,1)} %select_select_fusion.p0_ref.refs_3_, bf16[192,96,128]{2,1,0:T(8,128)(2,1)} %collective-permute-done.1.p1_ref.refs_4_, bf16[1,128]{1,0:T(2,128)(2,1)} %bitcast.11), custom_call_target="tpu_custom_call" | custom-call | flops 60000000 | bytes 18874368 | tf_op jit(solution)/shard_map/norm/pallas_call | solution.py:96
  136.7 0.0 collective-permute-done.3.refs_1_
  136.7 84.7 %collective-permute-done.4.refs_2_ = bf16[192,96,128]{2,1,0:T(8,128)(2,1)} collective-permute-done((bf16[192,96,128]{2,1,0:T(8,128)(2,1)}, bf16[192,96,128]{2,1,0:T(8,128)(2,1)}, u32[]{:S(2)}, u32[]{:S(2)}) %collective-permute-start.4) | collective-permute-done | bytes 4718624 | tf_op jit(solution)/shard_map/ppermute | solution.py:50
  221.4 16.2 %project.5 = (bf16[128,64,384]{2,1,0:T(8,128)(2,1)}, bf16[64,384,128]{2,1,0:T(8,128)(2,1)}) custom-call(s32[1]{0:T(128)} %bitcast.5.refs_0_, bf16[192,96,128]{2,1,0:T(8,128)(2,1)} %collective-permute-done.3.refs_1_, bf16[192,96,128]{2,1,0:T(8,128)(2,1)} %collective-permute-done.4.refs_2_, bf16[1,128]{1,0:T(2,128)(2,1)} %bitcast.12, ...), custom_call_target="tpu_custom_call" | custom-call | flops 75000000 | bytes 12582912 | tf_op jit(solution)/shard_map/project/pallas_call | solution.py:134
  237.6 9.8 %project.6 = (bf16[128,32,384]{2,1,0:T(8,128)(2,1)}, bf16[32,384,128]{2,1,0:T(8,128)(2,1)}) custom-call(s32[1]{0:T(128)} %bitcast.5.refs_0_, bf16[192,96,128]{2,1,0:T(8,128)(2,1)} %collective-permute-done.3.refs_1_, bf16[192,96,128]{2,1,0:T(8,128)(2,1)} %collective-permute-done.4.refs_2_, bf16[1,128]{1,0:T(2,128)(2,1)} %bitcast.13, ...), custom_call_target="tpu_custom_call" | custom-call | flops 35000000 | bytes 6291456 | tf_op jit(solution)/shard_map/project/pallas_call | solution.py:134
  247.4 15.0 %project_x.2 = bf16[128,96,384]{2,1,0:T(8,128)(2,1)} custom-call(s32[1]{0:T(128)S(6)} %sub.17.refs_0_, bf16[96,384,128]{2,1,0:T(8,128)(2,1)} %norm.1.refs_1_, bf16[64,384,128]{2,1,0:T(8,128)(2,1)} %get-tuple-element.30.refs_2_, bf16[32,384,128]{2,1,0:T(8,128)(2,1)} %get-tuple-element.33.refs_3_, bf16[256,128]{1,0:T(8,128)(2,1)} %maximum_bitcast_fusion.1.refs_4_.refs_6_), custom_call_target="tpu_custom_call" | custom-call | flops 70000000 | bytes 18874368 | tf_op jit(solution)/shard_map/project_x/pallas_call | solution.py:162
  262.4 23.2 %project.7.refs_1_ = bf16[128,96,384]{2,1,0:T(8,128)(2,1)} custom-call(s32[1]{0:T(128)} %bitcast.3.refs_0_, bf16[192,96,128]{2,1,0:T(8,128)(2,1)} %collective-permute-done.refs_1_, bf16[192,96,128]{2,1,0:T(8,128)(2,1)} %collective-permute-done.2.refs_2_, bf16[192,96,128]{2,1,0:T(8,128)(2,1)} %select_select_fusion.p0_ref.refs_3_, ...), custom_call_target="tpu_custom_call" | custom-call | flops 115000000 | bytes 18874368 | tf_op jit(solution)/shard_map/project/pallas_call | solution.py:134
  285.6 0.0 collective-permute-start.5
  285.6 0.5 collective-permute-start.6
  286.1 0.3 collective-permute-start.8
  286.5 59.9 %collective-permute-start.9 = (bf16[192,96,128]{2,1,0:T(8,128)(2,1)}, bf16[192,96,128]{2,1,0:T(8,128)(2,1)}, u32[]{:S(2)}, u32[]{:S(2)}) collective-permute-start(bf16[192,96,128]{2,1,0:T(8,128)(2,1)} %select_select_fusion.1.refs_1_), channel_id=1, source_target_pairs={{0,4},{1,5},{2,6},{3,7},{4,0},{5,1},{6,2},{7,3},{8,12},{9,13},{10,... | collective-permute-start | bytes 14155784 | tf_op jit(solution)/shard_map/ppermute | solution.py:50
  346.4 43.8 %collective-permute-done.8.refs_2_ = bf16[192,96,128]{2,1,0:T(8,128)(2,1)} collective-permute-done((bf16[192,96,128]{2,1,0:T(8,128)(2,1)}, bf16[192,96,128]{2,1,0:T(8,128)(2,1)}, u32[]{:S(2)}, u32[]{:S(2)}) %collective-permute-start.8) | collective-permute-done | bytes 4718624 | tf_op jit(solution)/shard_map/ppermute | solution.py:50
  390.2 0.3 collective-permute-start.10
  390.6 3.3 collective-permute-start.14
  393.8 14.7 %project_x.3.refs_3_.refs_5_ = bf16[128,96,384]{2,1,0:T(8,128)(2,1)} custom-call(s32[1]{0:T(128)} %bitcast.5.refs_0_, bf16[96,384,128]{2,1,0:T(8,128)(2,1)} %norm.1.refs_1_, bf16[64,384,128]{2,1,0:T(8,128)(2,1)} %get-tuple-element.30.refs_2_, bf16[32,384,128]{2,1,0:T(8,128)(2,1)} %get-tuple-element.33.refs_3_, ...), custom_call_target="tpu_custom_call" | custom-call | flops 70000000 | bytes 18874368 | tf_op jit(solution)/shard_map/project_x/pallas_call | solution.py:162
  408.5 0.0 collective-permute-done.5.refs_2_
  408.5 0.0 collective-permute-done.6.refs_4_.refs_7_
  408.5 22.3 %triangle.4.refs_6_.refs_12_ = bf16[96,96,128]{2,1,0:T(8,128)(2,1)} custom-call(s32[1]{0:T(128)} %bitcast.3.refs_0_, bf16[128,96,384]{2,1,0:T(8,128)(2,1)} %project.7.refs_1_, bf16[128,96,384]{2,1,0:T(8,128)(2,1)} %collective-permute-done.5.refs_2_, bf16[128,96,384]{2,1,0:T(8,128)(2,1)} %project_x.3.refs_3_.refs_5_, ...), custom_call_target="tpu_custom_call" | custom-call | flops 200000000 | bytes 37748736 | tf_op jit(solution)/shard_map/triangle/pallas_call | solution.py:230
  430.9 17.6 %collective-permute-done.9.refs_3_ = bf16[192,96,128]{2,1,0:T(8,128)(2,1)} collective-permute-done((bf16[192,96,128]{2,1,0:T(8,128)(2,1)}, bf16[192,96,128]{2,1,0:T(8,128)(2,1)}, u32[]{:S(2)}, u32[]{:S(2)}) %collective-permute-start.9) | collective-permute-done | bytes 4718624 | tf_op jit(solution)/shard_map/ppermute | solution.py:50
  448.4 45.0 %collective-permute-done.10.refs_4_ = bf16[192,96,128]{2,1,0:T(8,128)(2,1)} collective-permute-done((bf16[192,96,128]{2,1,0:T(8,128)(2,1)}, bf16[192,96,128]{2,1,0:T(8,128)(2,1)}, u32[]{:S(2)}, u32[]{:S(2)}) %collective-permute-start.10) | collective-permute-done | bytes 4718624 | tf_op jit(solution)/shard_map/ppermute | solution.py:50
  493.4 22.9 %project.8 = bf16[128,96,384]{2,1,0:T(8,128)(2,1)} custom-call(s32[1]{0:T(128)S(6)} %sub.17.refs_0_, bf16[192,96,128]{2,1,0:T(8,128)(2,1)} %select_select_fusion.1.refs_1_, bf16[192,96,128]{2,1,0:T(8,128)(2,1)} %collective-permute-done.8.refs_2_, bf16[192,96,128]{2,1,0:T(8,128)(2,1)} %collective-permute-done.9.refs_3_, ...), custom_call_target="tpu_custom_call" | custom-call | flops 115000000 | bytes 18874368 | tf_op jit(solution)/shard_map/project/pallas_call | solution.py:134
  516.4 0.0 collective-permute-start.11
  516.4 2.4 collective-permute-start.16
  518.8 23.3 %project.9.refs_3_.refs_6_ = bf16[128,96,384]{2,1,0:T(8,128)(2,1)} custom-call(s32[1]{0:T(128)} %bitcast.5.refs_0_, bf16[192,96,128]{2,1,0:T(8,128)(2,1)} %select_select_fusion.1.refs_1_, bf16[192,96,128]{2,1,0:T(8,128)(2,1)} %collective-permute-done.8.refs_2_, bf16[192,96,128]{2,1,0:T(8,128)(2,1)} %collective-permute-done.9.refs_3_, ...), custom_call_target="tpu_custom_call" | custom-call | flops 115000000 | bytes 18874368 | tf_op jit(solution)/shard_map/project/pallas_call | solution.py:134
  542.1 3.4 collective-permute-start.15
  545.4 2.3 collective-permute-start.13
  547.7 1.9 collective-permute-start.18
  549.6 22.4 %triangle.5.refs_7_.refs_13_ = bf16[96,96,128]{2,1,0:T(8,128)(2,1)} custom-call(s32[1]{0:T(128)} %bitcast.3.refs_0_, bf16[128,96,384]{2,1,0:T(8,128)(2,1)} %project.7.refs_1_, bf16[128,96,384]{2,1,0:T(8,128)(2,1)} %collective-permute-done.5.refs_2_, bf16[128,96,384]{2,1,0:T(8,128)(2,1)} %project.9.refs_3_.refs_6_, ...), custom_call_target="tpu_custom_call" | custom-call | flops 200000000 | bytes 37748736 | tf_op jit(solution)/shard_map/triangle/pallas_call | solution.py:230
  572.1 29.8 %triangle.6.refs_8_.refs_14_ = bf16[64,192,128]{2,1,0:T(8,128)(2,1)} custom-call(s32[1]{0:T(128)} %bitcast.3.refs_0_, bf16[128,64,384]{2,1,0:T(8,128)(2,1)} %collective-permute-done.14.refs_1_, bf16[128,64,384]{2,1,0:T(8,128)(2,1)} %collective-permute-done.15.refs_2_, bf16[128,64,384]{2,1,0:T(8,128)(2,1)} %get-tuple-element.31.refs_3_, ...), custom_call_target="tpu_custom_call" | custom-call | flops 200000000 | bytes 50331648 | tf_op jit(solution)/shard_map/triangle/pallas_call | solution.py:230
  601.9 2.3 collective-permute-start.17
  604.2 0.8 collective-permute-start.7
  605.0 1.3 collective-permute-start.20
  606.3 2.1 collective-permute-start.12
  608.4 80.1 %collective-permute-start.23 = (bf16[64,192,128]{2,1,0:T(8,128)(2,1)}, bf16[64,192,128]{2,1,0:T(8,128)(2,1)}, u32[]{:S(2)}, u32[]{:S(2)}) collective-permute-start(bf16[64,192,128]{2,1,0:T(8,128)(2,1)} %triangle.6.refs_8_.refs_14_), channel_id=1, source_target_pairs={{0,1},{1,5},{4,3},{5,7},{9,12},{12,10},{13,14},{16,17},{17,21},{20... | collective-permute-start | bytes 9437192 | tf_op jit(solution)/shard_map/ppermute | solution.py:50
  688.5 1.4 copy-done.1
  689.9 2.3 collective-permute-start.24
  692.2 1.3 collective-permute-start.21
  693.5 24.8 %triangle.7.refs_8_.refs_14_ = bf16[32,192,128]{2,1,0:T(8,128)(2,1)} custom-call(s32[1]{0:T(128)} %bitcast.3.refs_0_, bf16[128,32,384]{2,1,0:T(8,128)(2,1)} %collective-permute-done.13.refs_1_, bf16[128,32,384]{2,1,0:T(8,128)(2,1)} %collective-permute-done.17.refs_2_, bf16[128,32,384]{2,1,0:T(8,128)(2,1)} %get-tuple-element.34.refs_3_, ...), custom_call_target="tpu_custom_call" | custom-call | flops 200000000 | bytes 44040192 | tf_op jit(solution)/shard_map/triangle/pallas_call | solution.py:230
  718.4 19.0 %collective-permute-start.19 = (bf16[32,192,128]{2,1,0:T(8,128)(2,1)}, bf16[32,192,128]{2,1,0:T(8,128)(2,1)S(1)}, u32[]{:S(2)}, u32[]{:S(2)}) collective-permute-start(bf16[32,192,128]{2,1,0:T(8,128)(2,1)} %triangle.7.refs_8_.refs_14_), channel_id=1, source_target_pairs={{0,1},{1,5},{4,3},{5,7},{9,12},{12,10},{13,14},{16,17},{17,21},{20... | collective-permute-start | bytes 4718600 | tf_op jit(solution)/shard_map/ppermute | solution.py:50
  737.4 0.8 collective-permute-start.22
  738.2 0.7 pad_add_fusion.refs_0_
  738.9 32.8 %collective-permute-done.21.refs_10_ = bf16[96,96,128]{2,1,0:T(8,128)(2,1)} collective-permute-done((bf16[96,96,128]{2,1,0:T(8,128)(2,1)}, bf16[96,96,128]{2,1,0:T(8,128)(2,1)}, u32[]{:S(2)}, u32[]{:S(2)}) %collective-permute-start.21) | collective-permute-done | bytes 2359328 | tf_op jit(solution)/shard_map/ppermute | solution.py:50
  771.7 17.5 %finish.2.refs_16_ = bf16[192,192,128]{2,1,0:T(8,128)(2,1)} custom-call(s32[2]{0:T(128)} %pad_add_fusion.refs_0_, bf16[192,192,128]{2,1,0:T(8,128)(2,1)} %refs_1_.3, f32[192,192,128]{2,1,0:T(8,128)} %out_gate.1.refs_2_, bf16[96,96,128]{2,1,0:T(8,128)(2,1)} %copy-done.1, bf16[96,96,128]{2,1,0:T(8,128)(2,1)} %collective-permute-done.12.refs_4_, ...), custom_call_target="tpu_custom_call" | custom-call | flops 40000000 | bytes 23592960 | tf_op jit(solution)/shard_map/finish/pallas_call | solution.py:313
  789.2 1.1 copy-done.2
  790.3 1.3 copy-done.3
  791.6 11.5 %finish.3 = bf16[192,192,128]{2,1,0:T(8,128)(2,1)} custom-call(s32[2]{0:T(128)} %pad_add_fusion.refs_0_, bf16[192,192,128]{2,1,0:T(8,128)(2,1)} %refs_1_.3, f32[192,192,128]{2,1,0:T(8,128)} %out_gate.1.refs_2_, bf16[96,96,128]{2,1,0:T(8,128)(2,1)} %copy-done.1, ...), custom_call_target="tpu_custom_call", output_to_operand_aliasing={{}: (16, {})} | custom-call | flops 40000000 | bytes 23592960 | tf_op jit(solution)/shard_map/finish/pallas_call | solution.py:313
  (30 shorter events, 0.1 us)
Async XLA Ops:
  1.1 9.3 %copy-start.4 = (s32[192,192]{1,0:T(8,128)S(1)}, s32[192,192]{1,0:T(8,128)}, u32[]{:S(2)}) copy-start(s32[192,192]{1,0:T(8,128)} %param.11) | copy-start | bytes 442372
  7.4 105.1 %collective-permute-start.1 = (bf16[192,96,128]{2,1,0:T(8,128)(2,1)}, bf16[192,96,128]{2,1,0:T(8,128)(2,1)}, u32[]{:S(2)}, u32[]{:S(2)}) collective-permute-start(bf16[192,96,128]{2,1,0:T(8,128)(2,1)} %select_select_fusion.1.refs_1_), channel_id=1, source_target_pairs={{0,2},{1,3},{2,0},{3,1},{4,6},{5,7},{6,4},{7,5},{8,10},{9,11},{10,... | collective-permute-start | bytes 14155784 | tf_op jit(solution)/shard_map/ppermute | solution.py:50
  16.7 120.0 %collective-permute-start.3 = (bf16[192,96,128]{2,1,0:T(8,128)(2,1)}, bf16[192,96,128]{2,1,0:T(8,128)(2,1)}, u32[]{:S(2)}, u32[]{:S(2)}) collective-permute-start(bf16[192,96,128]{2,1,0:T(8,128)(2,1)} %select_select_fusion.p0_ref.refs_3_), channel_id=1, source_target_pairs={{0,4},{1,5},{2,6},{3,7},{4,0},{5,1},{6,2},{7,3},{8,12},{9,13},{10,... | collective-permute-start | bytes 14155784 | tf_op jit(solution)/shard_map/ppermute | solution.py:50
  18.3 101.6 %copy-start.5 = (bf16[128,128]{1,0:T(8,128)(2,1)S(1)}, bf16[128,128]{1,0:T(8,128)(2,1)}, u32[]{:S(2)}) copy-start(bf16[128,128]{1,0:T(8,128)(2,1)} %param.14) | copy-start | bytes 98308
  18.3 101.7 %copy-start.6 = (bf16[128,128]{1,0:T(8,128)(2,1)S(1)}, bf16[128,128]{1,0:T(8,128)(2,1)}, u32[]{:S(2)}) copy-start(bf16[128,128]{1,0:T(8,128)(2,1)} %param.13) | copy-start | bytes 98308
  18.3 101.9 %copy-start.7 = (bf16[128,128]{1,0:T(8,128)(2,1)S(1)}, bf16[128,128]{1,0:T(8,128)(2,1)}, u32[]{:S(2)}) copy-start(bf16[128,128]{1,0:T(8,128)(2,1)} %param.16) | copy-start | bytes 98308
  18.3 102.0 %copy-start.8 = (bf16[128,128]{1,0:T(8,128)(2,1)S(1)}, bf16[128,128]{1,0:T(8,128)(2,1)}, u32[]{:S(2)}) copy-start(bf16[128,128]{1,0:T(8,128)(2,1)} %param.15) | copy-start | bytes 98308
  112.5 108.9 %collective-permute-start.4 = (bf16[192,96,128]{2,1,0:T(8,128)(2,1)}, bf16[192,96,128]{2,1,0:T(8,128)(2,1)}, u32[]{:S(2)}, u32[]{:S(2)}) collective-permute-start(bf16[192,96,128]{2,1,0:T(8,128)(2,1)} %collective-permute-done.1.p1_ref.refs_4_), channel_id=1, source_target_pairs={{0,4},{1,5},{2,6},{3,7},{4,0},{5,1},{6,2},{7,3},{8,12},{9,13},{10,... | collective-permute-start | bytes 14155784 | tf_op jit(solution)/shard_map/ppermute | solution.py:50
  114.3 148.1 %collective-permute-start = (bf16[192,96,128]{2,1,0:T(8,128)(2,1)}, bf16[192,96,128]{2,1,0:T(8,128)(2,1)}, u32[]{:S(2)}, u32[]{:S(2)}) collective-permute-start(bf16[192,96,128]{2,1,0:T(8,128)(2,1)} %select_select_fusion.p0_ref.refs_3_), channel_id=1, source_target_pairs={{4,8},{5,9},{6,10},{7,11},{8,4},{9,5},{10,6},{11,7},{20,24},{21,25... | collective-permute-start | bytes 14155784 | tf_op jit(solution)/shard_map/ppermute | solution.py:50
  117.1 145.4 %collective-permute-start.2 = (bf16[192,96,128]{2,1,0:T(8,128)(2,1)}, bf16[192,96,128]{2,1,0:T(8,128)(2,1)}, u32[]{:S(2)}, u32[]{:S(2)}) collective-permute-start(bf16[192,96,128]{2,1,0:T(8,128)(2,1)} %collective-permute-done.1.p1_ref.refs_4_), channel_id=1, source_target_pairs={{4,8},{5,9},{6,10},{7,11},{8,4},{9,5},{10,6},{11,7},{20,24},{21,25... | collective-permute-start | bytes 14155784 | tf_op jit(solution)/shard_map/ppermute | solution.py:50
  285.6 122.9 %collective-permute-start.5 = (bf16[128,96,384]{2,1,0:T(8,128)(2,1)}, bf16[128,96,384]{2,1,0:T(8,128)(2,1)}, u32[]{:S(2)}, u32[]{:S(2)}) collective-permute-start(bf16[128,96,384]{2,1,0:T(8,128)(2,1)} %project.7.refs_1_), channel_id=1, source_target_pairs={{0,1},{1,0},{2,3},{3,2},{4,5},{5,4},{6,7},{7,6},{8,9},{9,8},{10,11... | collective-permute-start | bytes 28311560 | tf_op jit(solution)/shard_map/ppermute | solution.py:50
  285.6 122.9 %collective-permute-start.6 = (bf16[128,96,384]{2,1,0:T(8,128)(2,1)}, bf16[128,96,384]{2,1,0:T(8,128)(2,1)}, u32[]{:S(2)}, u32[]{:S(2)}) collective-permute-start(bf16[128,96,384]{2,1,0:T(8,128)(2,1)} %project_x.2), channel_id=1, source_target_pairs={{0,1},{1,0},{2,3},{3,2},{4,5},{5,4},{6,7},{7,6},{8,9},{9,8},{10,11... | collective-permute-start | bytes 28311560 | tf_op jit(solution)/shard_map/ppermute | solution.py:50
  286.1 104.1 %collective-permute-start.8 = (bf16[192,96,128]{2,1,0:T(8,128)(2,1)}, bf16[192,96,128]{2,1,0:T(8,128)(2,1)}, u32[]{:S(2)}, u32[]{:S(2)}) collective-permute-start(bf16[192,96,128]{2,1,0:T(8,128)(2,1)} %select_select_fusion.p0_ref.refs_3_), channel_id=1, source_target_pairs={{0,2},{1,3},{2,0},{3,1},{4,6},{5,7},{6,4},{7,5},{8,10},{9,11},{10,... | collective-permute-start | bytes 14155784 | tf_op jit(solution)/shard_map/ppermute | solution.py:50
  286.5 162.0 %collective-permute-start.9 = (bf16[192,96,128]{2,1,0:T(8,128)(2,1)}, bf16[192,96,128]{2,1,0:T(8,128)(2,1)}, u32[]{:S(2)}, u32[]{:S(2)}) collective-permute-start(bf16[192,96,128]{2,1,0:T(8,128)(2,1)} %select_select_fusion.1.refs_1_), channel_id=1, source_target_pairs={{0,4},{1,5},{2,6},{3,7},{4,0},{5,1},{6,2},{7,3},{8,12},{9,13},{10,... | collective-permute-start | bytes 14155784 | tf_op jit(solution)/shard_map/ppermute | solution.py:50
  390.2 103.2 %collective-permute-start.10 = (bf16[192,96,128]{2,1,0:T(8,128)(2,1)}, bf16[192,96,128]{2,1,0:T(8,128)(2,1)}, u32[]{:S(2)}, u32[]{:S(2)}) collective-permute-start(bf16[192,96,128]{2,1,0:T(8,128)(2,1)} %collective-permute-done.3.refs_1_), channel_id=1, source_target_pairs={{0,2},{1,3},{2,0},{3,1},{4,6},{5,7},{6,4},{7,5},{8,10},{9,11},{10,... | collective-permute-start | bytes 14155784 | tf_op jit(solution)/shard_map/ppermute | solution.py:50
  390.6 151.5 %collective-permute-start.14 = (bf16[128,64,384]{2,1,0:T(8,128)(2,1)}, bf16[128,64,384]{2,1,0:T(8,128)(2,1)}, u32[]{:S(2)}, u32[]{:S(2)}) collective-permute-start(bf16[128,64,384]{2,1,0:T(8,128)(2,1)} %get-tuple-element.31.refs_3_), channel_id=1, source_target_pairs={{4,8},{5,9},{6,10},{7,11},{8,4},{9,5},{10,6},{11,7},{20,24},{21,25... | collective-permute-start | bytes 18874376 | tf_op jit(solution)/shard_map/ppermute | solution.py:50
  516.4 33.3 %collective-permute-start.11 = (bf16[128,96,384]{2,1,0:T(8,128)(2,1)}, bf16[128,96,384]{2,1,0:T(8,128)(2,1)}, u32[]{:S(2)}, u32[]{:S(2)}) collective-permute-start(bf16[128,96,384]{2,1,0:T(8,128)(2,1)} %project.8), channel_id=1, source_target_pairs={{0,1},{1,0},{2,3},{3,2},{4,5},{5,4},{6,7},{7,6},{8,9},{9,8},{10,11... | collective-permute-start | bytes 28311560 | tf_op jit(solution)/shard_map/ppermute | solution.py:50
  516.4 55.7 %collective-permute-start.16 = (bf16[128,64,384]{2,1,0:T(8,128)(2,1)}, bf16[128,64,384]{2,1,0:T(8,128)(2,1)}, u32[]{:S(2)}, u32[]{:S(2)}) collective-permute-start(bf16[128,64,384]{2,1,0:T(8,128)(2,1)} %get-tuple-element.31.refs_3_), channel_id=1, source_target_pairs={{0,1},{1,0},{2,3},{3,2},{12,13},{13,12},{14,15},{15,14},{16,17},{1... | collective-permute-start | bytes 18874376 | tf_op jit(solution)/shard_map/ppermute | solution.py:50
  542.1 30.0 %collective-permute-start.15 = (bf16[128,64,384]{2,1,0:T(8,128)(2,1)}, bf16[128,64,384]{2,1,0:T(8,128)(2,1)}, u32[]{:S(2)}, u32[]{:S(2)}) collective-permute-start(bf16[128,64,384]{2,1,0:T(8,128)(2,1)} %collective-permute-done.14.refs_1_), channel_id=1, source_target_pairs={{4,5},{5,4},{6,7},{7,6},{8,9},{9,8},{10,11},{11,10},{20,21},{21,20... | collective-permute-start | bytes 18874376 | tf_op jit(solution)/shard_map/ppermute | solution.py:50
  545.4 56.5 %collective-permute-start.13 = (bf16[128,32,384]{2,1,0:T(8,128)(2,1)}, bf16[128,32,384]{2,1,0:T(8,128)(2,1)}, u32[]{:S(2)}, u32[]{:S(2)}) collective-permute-start(bf16[128,32,384]{2,1,0:T(8,128)(2,1)} %get-tuple-element.34.refs_3_), channel_id=1, source_target_pairs={{4,8},{5,9},{6,10},{7,11},{8,4},{9,5},{10,6},{11,7},{20,24},{21,25... | collective-permute-start | bytes 9437192 | tf_op jit(solution)/shard_map/ppermute | solution.py:50
  547.7 60.7 %collective-permute-start.18 = (bf16[128,32,384]{2,1,0:T(8,128)(2,1)}, bf16[128,32,384]{2,1,0:T(8,128)(2,1)}, u32[]{:S(2)}, u32[]{:S(2)}) collective-permute-start(bf16[128,32,384]{2,1,0:T(8,128)(2,1)} %get-tuple-element.34.refs_3_), channel_id=1, source_target_pairs={{0,1},{1,0},{2,3},{3,2},{12,13},{13,12},{14,15},{15,14},{16,17},{1... | collective-permute-start | bytes 9437192 | tf_op jit(solution)/shard_map/ppermute | solution.py:50
  572.0 32.2 %copy-start = (bf16[96,96,128]{2,1,0:T(8,128)(2,1)S(1)}, bf16[96,96,128]{2,1,0:T(8,128)(2,1)}, u32[]{:S(2)}) copy-start(bf16[96,96,128]{2,1,0:T(8,128)(2,1)} %triangle.4.refs_6_.refs_12_) | copy-start | bytes 7077892
  601.9 90.4 %collective-permute-start.17 = (bf16[128,32,384]{2,1,0:T(8,128)(2,1)}, bf16[128,32,384]{2,1,0:T(8,128)(2,1)}, u32[]{:S(2)}, u32[]{:S(2)}) collective-permute-start(bf16[128,32,384]{2,1,0:T(8,128)(2,1)} %collective-permute-done.13.refs_1_), channel_id=1, source_target_pairs={{4,5},{5,4},{6,7},{7,6},{8,9},{9,8},{10,11},{11,10},{20,21},{21,20... | collective-permute-start | bytes 9437192 | tf_op jit(solution)/shard_map/ppermute | solution.py:50
  604.2 84.3 %collective-permute-start.7 = (bf16[96,96,128]{2,1,0:T(8,128)(2,1)S(1)}, bf16[96,96,128]{2,1,0:T(8,128)(2,1)S(1)}, u32[]{:S(2)}, u32[]{:S(2)}) collective-permute-start(bf16[96,96,128]{2,1,0:T(8,128)(2,1)S(1)} %copy-done), channel_id=1, source_target_pairs={{1,4},{4,2},{5,6},{8,9},{9,13},{12,11},{13,15},{17,20},{20,18},{21... | collective-permute-start | bytes 7077896 | tf_op jit(solution)/shard_map/ppermute | solution.py:50
  605.0 113.4 %collective-permute-start.20 = (bf16[96,96,128]{2,1,0:T(8,128)(2,1)S(1)}, bf16[96,96,128]{2,1,0:T(8,128)(2,1)}, u32[]{:S(2)}, u32[]{:S(2)}) collective-permute-start(bf16[96,96,128]{2,1,0:T(8,128)(2,1)S(1)} %copy-done), channel_id=1, source_target_pairs={{2,0},{3,4},{6,2},{7,6},{10,9},{11,13},{14,11},{18,16},{19,20},{22... | collective-permute-start | bytes 7077896 | tf_op jit(solution)/shard_map/ppermute | solution.py:50
  606.3 131.1 %collective-permute-start.12 = (bf16[96,96,128]{2,1,0:T(8,128)(2,1)}, bf16[96,96,128]{2,1,0:T(8,128)(2,1)}, u32[]{:S(2)}, u32[]{:S(2)}) collective-permute-start(bf16[96,96,128]{2,1,0:T(8,128)(2,1)} %triangle.5.refs_7_.refs_13_), channel_id=1, source_target_pairs={{1,4},{4,2},{5,6},{8,9},{9,13},{12,11},{13,15},{17,20},{20,18},{21... | collective-permute-start | bytes 7077896 | tf_op jit(solution)/shard_map/ppermute | solution.py:50
  608.4 163.2 %collective-permute-start.23 = (bf16[64,192,128]{2,1,0:T(8,128)(2,1)}, bf16[64,192,128]{2,1,0:T(8,128)(2,1)}, u32[]{:S(2)}, u32[]{:S(2)}) collective-permute-start(bf16[64,192,128]{2,1,0:T(8,128)(2,1)} %triangle.6.refs_8_.refs_14_), channel_id=1, source_target_pairs={{0,1},{1,5},{4,3},{5,7},{9,12},{12,10},{13,14},{16,17},{17,21},{20... | collective-permute-start | bytes 9437192 | tf_op jit(solution)/shard_map/ppermute | solution.py:50
  688.5 1.4 copy-start.1
  689.9 81.7 %collective-permute-start.24 = (bf16[64,192,128]{2,1,0:T(8,128)(2,1)}, bf16[64,192,128]{2,1,0:T(8,128)(2,1)}, u32[]{:S(2)}, u32[]{:S(2)}) collective-permute-start(bf16[64,192,128]{2,1,0:T(8,128)(2,1)} %triangle.6.refs_8_.refs_14_), channel_id=1, source_target_pairs={{2,1},{3,5},{6,3},{10,8},{11,12},{14,10},{15,14},{18,17},{19,21},{... | collective-permute-start | bytes 9437192 | tf_op jit(solution)/shard_map/ppermute | solution.py:50
  692.2 79.4 %collective-permute-start.21 = (bf16[96,96,128]{2,1,0:T(8,128)(2,1)}, bf16[96,96,128]{2,1,0:T(8,128)(2,1)}, u32[]{:S(2)}, u32[]{:S(2)}) collective-permute-start(bf16[96,96,128]{2,1,0:T(8,128)(2,1)} %triangle.5.refs_7_.refs_13_), channel_id=1, source_target_pairs={{2,0},{3,4},{6,2},{7,6},{10,9},{11,13},{14,11},{18,16},{19,20},{22... | collective-permute-start | bytes 7077896 | tf_op jit(solution)/shard_map/ppermute | solution.py:50
  718.4 70.8 %collective-permute-start.19 = (bf16[32,192,128]{2,1,0:T(8,128)(2,1)}, bf16[32,192,128]{2,1,0:T(8,128)(2,1)S(1)}, u32[]{:S(2)}, u32[]{:S(2)}) collective-permute-start(bf16[32,192,128]{2,1,0:T(8,128)(2,1)} %triangle.7.refs_8_.refs_14_), channel_id=1, source_target_pairs={{0,1},{1,5},{4,3},{5,7},{9,12},{12,10},{13,14},{16,17},{17,21},{20... | collective-permute-start | bytes 4718600 | tf_op jit(solution)/shard_map/ppermute | solution.py:50
  737.4 51.7 %collective-permute-start.22 = (bf16[32,192,128]{2,1,0:T(8,128)(2,1)}, bf16[32,192,128]{2,1,0:T(8,128)(2,1)S(1)}, u32[]{:S(2)}, u32[]{:S(2)}) collective-permute-start(bf16[32,192,128]{2,1,0:T(8,128)(2,1)} %triangle.7.refs_8_.refs_14_), channel_id=1, source_target_pairs={{2,1},{3,5},{6,3},{10,8},{11,12},{14,10},{15,14},{18,17},{19,21},{... | collective-permute-start | bytes 4718600 | tf_op jit(solution)/shard_map/ppermute | solution.py:50
  789.1 1.2 copy-start.2
  790.3 1.3 copy-start.3

commit v4 on v3

--- a/solution.py
+++ b/solution.py
@@ -243,30 +243,30 @@
     )(flag, *[a for pair in a_pairs for a in pair], *b_parts, gain)
 
 
-def gate_kernel(z_ref, gain_ref, wg_ref, out_ref):
+def gate_in_kernel(z_ref, gain_ref, out_ref):
     rows, cols, dim = z_ref.shape
-    x = normed(z_ref[...].astype(F32).reshape(rows * cols, dim), gain_ref[...].astype(F32))
-    out_ref[...] = jax.nn.sigmoid(jnp.dot(x, wg_ref[...], preferred_element_type=F32)).reshape(rows, cols, dim)
-
-
-def out_gate(pair_tile, gain, w_gate, blk=16):
+    out_ref[...] = normed(z_ref[...].astype(F32).reshape(rows * cols, dim), gain_ref[...].astype(F32)).reshape(rows, cols, dim)
+
+
+def gate_in(pair_tile, gain, blk=16):
     rows, cols, dim = pair_tile.shape
     blk = min(blk, rows)
     spec = pl.BlockSpec((blk, cols, dim), lambda g: (g, 0, 0))
     return pl.pallas_call(
-        gate_kernel,
+        gate_in_kernel,
         grid=(rows // blk,),
-        in_specs=[spec, pl.BlockSpec((1, dim), lambda g: (0, 0)), pl.BlockSpec((dim, dim), lambda g: (0, 0))],
+        in_specs=[spec, pl.BlockSpec((1, dim), lambda g: (0, 0))],
         out_specs=spec,
-        out_shape=jax.ShapeDtypeStruct(pair_tile.shape, F32),
-        compiler_params=params(),
-        cost_estimate=cost(18, 6 * rows * cols * dim),
-        name='out_gate',
-    )(pair_tile, gain, w_gate)
-
-
-def finish_kernel(sizes, pick_ref, z_ref, gate_ref, *refs):
-    wo_ref, out_ref = refs[2 * sum(sizes)], refs[-1]
+        out_shape=jax.ShapeDtypeStruct(pair_tile.shape, BF16),
+        compiler_params=params(),
+        cost_estimate=cost(15, 4 * rows * cols * dim),
+        name='gate_in',
+    )(pair_tile, gain)
+
+
+def finish_kernel(sizes, pick_ref, z_ref, x_ref, *refs):
+    wo_ref, wg_ref, out_ref = refs[2 * sum(sizes)], refs[2 * sum(sizes) + 1], refs[-2]
+    y_ref = refs[-1]
     rows, cols, dim = z_ref.shape
     half_cols = cols // 2
     for s in (0, 1):
@@ -275,18 +275,20 @@
 
             @pl.when((pl.program_id(0) == s) & (pick_ref[s] == q))
             def _(s=s, y_refs=refs[first:first + size]):
-                @pl.loop(0, rows, step=4)
-                def _(r):
-                    at = pl.ds(r, 4)
-                    for j in (0, 1):
-                        to, part = pl.ds(j * half_cols, half_cols), j ^ s
-                        y_part = y_refs[part][at] if len(y_refs) == 2 else y_refs[0][at, pl.ds(part * half_cols, half_cols), :]
-                        update = jnp.dot(y_part.reshape(4 * half_cols, -1), wo_ref[...], preferred_element_type=F32)
-                        total = z_ref[at, to, :].astype(F32) + gate_ref[at, to, :] * update.reshape(4, half_cols, dim)
-                        out_ref[at, to, :] = total.astype(BF16)
-
-
-def finish(pick, pair_tile, gate, candidates, w_out, first, count, so_far=None, blk=16):
+                for j in (0, 1):
+                    to, part = pl.ds(j * half_cols, half_cols), j ^ s
+                    y_ref[:, to, :] = y_refs[part][...] if len(y_refs) == 2 else y_refs[0][:, pl.ds(part * half_cols, half_cols), :]
+
+    @pl.loop(0, rows, step=8)
+    def _(r):
+        at, deep = pl.ds(r, 8), 8 * cols
+        update = jnp.dot(y_ref[at].reshape(deep, -1), wo_ref[...], preferred_element_type=F32)
+        gate = jax.nn.sigmoid(jnp.dot(x_ref[at].reshape(deep, dim), wg_ref[...], preferred_element_type=F32))
+        total = z_ref[at].astype(F32).reshape(deep, dim) + gate * update
+        out_ref[at] = total.astype(BF16).reshape(8, cols, dim)
+
+
+def finish(pick, pair_tile, x, candidates, w_out, w_gate, first, count, so_far=None, blk=16):
     rows, cols, dim = pair_tile.shape
     half_rows = rows // 2
     blk = math.gcd(blk, math.gcd(first, count))
@@ -303,8 +305,8 @@
 
     tile_spec = pl.BlockSpec((blk, cols, dim), lambda s, g, pick_ref: (s * (half_rows // blk) + first // blk + g, 0, 0))
     y_specs = [y_spec(s, q, v) for s in (0, 1) for q, c in enumerate(candidates[s]) for v in c]
-    operands = [pick, pair_tile, gate] + [v for s in (0, 1) for c in candidates[s] for v in c] + [w_out]
-    specs = [tile_spec, tile_spec] + y_specs + [pl.BlockSpec(w_out.shape, lambda s, g, pick_ref: (0, 0))]
+    operands = [pick, pair_tile, x] + [v for s in (0, 1) for c in candidates[s] for v in c] + [w_out, w_gate]
+    specs = [tile_spec, tile_spec] + y_specs + [pl.BlockSpec(w.shape, lambda s, g, pick_ref: (0, 0)) for w in (w_out, w_gate)]
     aliases = {}
     if so_far is not None:
         aliases = {len(operands): 0}
@@ -312,7 +314,8 @@
         specs.append(pl.BlockSpec(memory_space=pl.ANY))
     return pl.pallas_call(
         lambda *refs: finish_kernel(sizes, *refs),
-        grid_spec=pltpu.PrefetchScalarGridSpec(num_scalar_prefetch=1, grid=(2, count // blk), in_specs=specs, out_specs=tile_spec),
+        grid_spec=pltpu.PrefetchScalarGridSpec(num_scalar_prefetch=1, grid=(2, count // blk), in_specs=specs, out_specs=tile_spec,
+                                              scratch_shapes=[pltpu.VMEM((blk, cols, tri), BF16)]),
         out_shape=jax.ShapeDtypeStruct(pair_tile.shape, BF16),
         input_output_aliases=aliases,
         compiler_params=params(),
@@ -349,9 +352,9 @@
         y_a = send(t_b, TO_Y)
         z_a = send(t_a, TO_Z)
         m_0 = send(t_a, ACROSS)
-        gate = out_gate(pair_tile, gain_in, w_out_gate)
+        x_gate = gate_in(pair_tile, gain_in)
         y_b = send(after(t_a, z_a), TO_Y)
-        yz_a = send(after(y_a, gate), TO_Z)
+        yz_a = send(after(y_a, x_gate), TO_Z)
         m_1 = send(y_a, ACROSS)
         z_b = send(after(t_b, yz_a), TO_Z)
         yz_b = send(after(z_a, y_b), TO_Y)
@@ -389,7 +392,7 @@
         out = None
         for n, first, count in ((2, 0, big), (3, big, small)):
             candidates = [(tuple(got[s][:2]), (got[s][n],), (done_0, done_1), (done[n],)) for s in (0, 1)]
-            out = finish(pick, pair_tile, gate, candidates, w_out, first, count, out)
+            out = finish(pick, pair_tile, x_gate, candidates, w_out, w_out_gate, first, count, out)
         return out
 
     return jax.shard_map(local_step, mesh=mesh, in_specs=(tile_spec, mask_spec) + (replicated,) * 8, out_specs=tile_spec, check_vma=False)

time: 805 us -> 803 us (level)
  no operation moved by 1% of the time
where the time goes in v4:
time: 803 us; the launch traced here: 801 us
  waiting for transfers between devices  302 us (38%)
  Pallas kernels  282 us (35%)
  starting transfers between devices  197 us (25%)
  other arithmetic  15.5 us (2%)
    ppermute x25, waiting for transfers between devices, send(): return lax.ppermute(value, AXES, pairs)  302 us
    ppermute x25, starting transfers between devices, send(): return lax.ppermute(value, AXES, pairs)  197 us
    pallas_call x4, Pallas kernels, triangle(): pl.pallas_call(lambda *refs: triangle_kernel(n_pair, n_part, *refs), grid...  99.5 us
    pallas_call x5, Pallas kernels, project(): pl.pallas_call(lambda *refs: project_kernel(n_piece, *refs), grid_spec=pl...  95.2 us
    pallas_call x2, Pallas kernels, project_x(): pl.pallas_call(lambda *refs: project_x_kernel(n_first, *refs), grid_spec=...  29.8 us
    pallas_call x2, Pallas kernels, finish(): pl.pallas_call(lambda *refs: finish_kernel(sizes, *refs), grid_spec=pltpu...  26.7 us
    pallas_call x1, Pallas kernels, gate_in(): pl.pallas_call(gate_in_kernel, grid=(rows // blk,), in_specs=[spec, pl.Bl...  16.1 us
  transfers between devices with their start and end apart: 25, of which 6 were waited for; matrix products, arithmetic and copies ran while one was open for 1% of the time, Pallas kernels for 31%

profile of v4, /device:TPU:0, one launch (start us, length us, event | category | flops | bytes accessed | tf_op | source)
XLA Modules:
  0.0 801.0 jit_solution(5881777634774778329)
XLA Ops:
  0.0 1.1 select_compare_fusion.1
  1.1 0.0 copy-start.4
  1.1 6.3 select_select_fusion.1.refs_1_
  7.4 3.0 collective-permute-start.1
  10.4 0.1 select_compare_fusion
  10.5 6.2 select_select_fusion.p0_ref.refs_3_
  16.7 1.6 collective-permute-start.3
  18.2 16.1 %gate_in.1.refs_2_ = bf16[192,192,128]{2,1,0:T(8,128)(2,1)} custom-call(bf16[192,192,128]{2,1,0:T(8,128)(2,1)} %refs_1_.3, bf16[1,128]{1,0:T(2,128)(2,1)} %bitcast.10), custom_call_target="tpu_custom_call" | custom-call | flops 75000000 | bytes 18874368 | tf_op jit(solution)/shard_map/gate_in/pallas_call | solution.py:255
  34.3 78.1 %collective-permute-done.1.p1_ref.refs_4_ = bf16[192,96,128]{2,1,0:T(8,128)(2,1)} collective-permute-done((bf16[192,96,128]{2,1,0:T(8,128)(2,1)}, bf16[192,96,128]{2,1,0:T(8,128)(2,1)}, u32[]{:S(2)}, u32[]{:S(2)}) %collective-permute-start.1) | collective-permute-done | bytes 4718624 | tf_op jit(solution)/shard_map/ppermute | solution.py:50
  112.5 1.8 collective-permute-start.4
  114.3 2.8 collective-permute-start
  117.1 2.9 collective-permute-start.2
  119.9 0.1 copy.13
  120.1 0.1 copy.12
  120.2 0.1 copy.15
  120.3 0.1 copy.14
  120.4 0.6 maximum_bitcast_fusion.refs_4_.refs_6_
  121.1 0.6 maximum_bitcast_fusion.1.refs_4_.refs_6_
  121.7 15.1 %norm.1.refs_1_ = bf16[96,384,128]{2,1,0:T(8,128)(2,1)} custom-call(bf16[192,96,128]{2,1,0:T(8,128)(2,1)} %select_select_fusion.p0_ref.refs_3_, bf16[192,96,128]{2,1,0:T(8,128)(2,1)} %collective-permute-done.1.p1_ref.refs_4_, bf16[1,128]{1,0:T(2,128)(2,1)} %bitcast.11), custom_call_target="tpu_custom_call" | custom-call | flops 60000000 | bytes 18874368 | tf_op jit(solution)/shard_map/norm/pallas_call | solution.py:96
  136.8 0.0 collective-permute-done.3.refs_1_
  136.8 84.6 %collective-permute-done.4.refs_2_ = bf16[192,96,128]{2,1,0:T(8,128)(2,1)} collective-permute-done((bf16[192,96,128]{2,1,0:T(8,128)(2,1)}, bf16[192,96,128]{2,1,0:T(8,128)(2,1)}, u32[]{:S(2)}, u32[]{:S(2)}) %collective-permute-start.4) | collective-permute-done | bytes 4718624 | tf_op jit(solution)/shard_map/ppermute | solution.py:50
  221.4 16.3 %project.5 = (bf16[128,64,384]{2,1,0:T(8,128)(2,1)}, bf16[64,384,128]{2,1,0:T(8,128)(2,1)}) custom-call(s32[1]{0:T(128)} %bitcast.5.refs_0_, bf16[192,96,128]{2,1,0:T(8,128)(2,1)} %collective-permute-done.3.refs_1_, bf16[192,96,128]{2,1,0:T(8,128)(2,1)} %collective-permute-done.4.refs_2_, bf16[1,128]{1,0:T(2,128)(2,1)} %bitcast.12, ...), custom_call_target="tpu_custom_call" | custom-call | flops 75000000 | bytes 12582912 | tf_op jit(solution)/shard_map/project/pallas_call | solution.py:134
  237.6 9.6 %project.6 = (bf16[128,32,384]{2,1,0:T(8,128)(2,1)}, bf16[32,384,128]{2,1,0:T(8,128)(2,1)}) custom-call(s32[1]{0:T(128)} %bitcast.5.refs_0_, bf16[192,96,128]{2,1,0:T(8,128)(2,1)} %collective-permute-done.3.refs_1_, bf16[192,96,128]{2,1,0:T(8,128)(2,1)} %collective-permute-done.4.refs_2_, bf16[1,128]{1,0:T(2,128)(2,1)} %bitcast.13, ...), custom_call_target="tpu_custom_call" | custom-call | flops 35000000 | bytes 6291456 | tf_op jit(solution)/shard_map/project/pallas_call | solution.py:134
  247.3 15.0 %project_x.2 = bf16[128,96,384]{2,1,0:T(8,128)(2,1)} custom-call(s32[1]{0:T(128)S(6)} %sub.17.refs_0_, bf16[96,384,128]{2,1,0:T(8,128)(2,1)} %norm.1.refs_1_, bf16[64,384,128]{2,1,0:T(8,128)(2,1)} %get-tuple-element.30.refs_2_, bf16[32,384,128]{2,1,0:T(8,128)(2,1)} %get-tuple-element.33.refs_3_, bf16[256,128]{1,0:T(8,128)(2,1)} %maximum_bitcast_fusion.1.refs_4_.refs_6_), custom_call_target="tpu_custom_call" | custom-call | flops 70000000 | bytes 18874368 | tf_op jit(solution)/shard_map/project_x/pallas_call | solution.py:162
  262.3 0.0 collective-permute-done.2.refs_2_
  262.3 23.1 %project.7.refs_1_ = bf16[128,96,384]{2,1,0:T(8,128)(2,1)} custom-call(s32[1]{0:T(128)} %bitcast.3.refs_0_, bf16[192,96,128]{2,1,0:T(8,128)(2,1)} %collective-permute-done.refs_1_, bf16[192,96,128]{2,1,0:T(8,128)(2,1)} %collective-permute-done.2.refs_2_, bf16[192,96,128]{2,1,0:T(8,128)(2,1)} %select_select_fusion.p0_ref.refs_3_, ...), custom_call_target="tpu_custom_call" | custom-call | flops 115000000 | bytes 18874368 | tf_op jit(solution)/shard_map/project/pallas_call | solution.py:134
  285.4 0.0 collective-permute-start.5
  285.4 0.5 collective-permute-start.6
  285.9 0.3 collective-permute-start.8
  286.3 60.1 %collective-permute-start.9 = (bf16[192,96,128]{2,1,0:T(8,128)(2,1)}, bf16[192,96,128]{2,1,0:T(8,128)(2,1)}, u32[]{:S(2)}, u32[]{:S(2)}) collective-permute-start(bf16[192,96,128]{2,1,0:T(8,128)(2,1)} %select_select_fusion.1.refs_1_), channel_id=1, source_target_pairs={{0,4},{1,5},{2,6},{3,7},{4,0},{5,1},{6,2},{7,3},{8,12},{9,13},{10,... | collective-permute-start | bytes 14155784 | tf_op jit(solution)/shard_map/ppermute | solution.py:50
  346.3 43.7 %collective-permute-done.8.refs_2_ = bf16[192,96,128]{2,1,0:T(8,128)(2,1)} collective-permute-done((bf16[192,96,128]{2,1,0:T(8,128)(2,1)}, bf16[192,96,128]{2,1,0:T(8,128)(2,1)}, u32[]{:S(2)}, u32[]{:S(2)}) %collective-permute-start.8) | collective-permute-done | bytes 4718624 | tf_op jit(solution)/shard_map/ppermute | solution.py:50
  390.0 0.3 collective-permute-start.10
  390.4 3.2 collective-permute-start.14
  393.6 14.8 %project_x.3.refs_3_.refs_5_ = bf16[128,96,384]{2,1,0:T(8,128)(2,1)} custom-call(s32[1]{0:T(128)} %bitcast.5.refs_0_, bf16[96,384,128]{2,1,0:T(8,128)(2,1)} %norm.1.refs_1_, bf16[64,384,128]{2,1,0:T(8,128)(2,1)} %get-tuple-element.30.refs_2_, bf16[32,384,128]{2,1,0:T(8,128)(2,1)} %get-tuple-element.33.refs_3_, ...), custom_call_target="tpu_custom_call" | custom-call | flops 70000000 | bytes 18874368 | tf_op jit(solution)/shard_map/project_x/pallas_call | solution.py:162
  408.4 22.4 %triangle.4.refs_6_.refs_12_ = bf16[96,96,128]{2,1,0:T(8,128)(2,1)} custom-call(s32[1]{0:T(128)} %bitcast.3.refs_0_, bf16[128,96,384]{2,1,0:T(8,128)(2,1)} %project.7.refs_1_, bf16[128,96,384]{2,1,0:T(8,128)(2,1)} %collective-permute-done.5.refs_2_, bf16[128,96,384]{2,1,0:T(8,128)(2,1)} %project_x.3.refs_3_.refs_5_, ...), custom_call_target="tpu_custom_call" | custom-call | flops 200000000 | bytes 37748736 | tf_op jit(solution)/shard_map/triangle/pallas_call | solution.py:230
  430.7 17.7 %collective-permute-done.9.refs_3_ = bf16[192,96,128]{2,1,0:T(8,128)(2,1)} collective-permute-done((bf16[192,96,128]{2,1,0:T(8,128)(2,1)}, bf16[192,96,128]{2,1,0:T(8,128)(2,1)}, u32[]{:S(2)}, u32[]{:S(2)}) %collective-permute-start.9) | collective-permute-done | bytes 4718624 | tf_op jit(solution)/shard_map/ppermute | solution.py:50
  448.4 44.8 %collective-permute-done.10.refs_4_ = bf16[192,96,128]{2,1,0:T(8,128)(2,1)} collective-permute-done((bf16[192,96,128]{2,1,0:T(8,128)(2,1)}, bf16[192,96,128]{2,1,0:T(8,128)(2,1)}, u32[]{:S(2)}, u32[]{:S(2)}) %collective-permute-start.10) | collective-permute-done | bytes 4718624 | tf_op jit(solution)/shard_map/ppermute | solution.py:50
  493.3 23.0 %project.8 = bf16[128,96,384]{2,1,0:T(8,128)(2,1)} custom-call(s32[1]{0:T(128)S(6)} %sub.17.refs_0_, bf16[192,96,128]{2,1,0:T(8,128)(2,1)} %select_select_fusion.1.refs_1_, bf16[192,96,128]{2,1,0:T(8,128)(2,1)} %collective-permute-done.8.refs_2_, bf16[192,96,128]{2,1,0:T(8,128)(2,1)} %collective-permute-done.9.refs_3_, ...), custom_call_target="tpu_custom_call" | custom-call | flops 115000000 | bytes 18874368 | tf_op jit(solution)/shard_map/project/pallas_call | solution.py:134
  516.2 2.4 collective-permute-start.16
  518.6 23.2 %project.9.refs_3_.refs_6_ = bf16[128,96,384]{2,1,0:T(8,128)(2,1)} custom-call(s32[1]{0:T(128)} %bitcast.5.refs_0_, bf16[192,96,128]{2,1,0:T(8,128)(2,1)} %select_select_fusion.1.refs_1_, bf16[192,96,128]{2,1,0:T(8,128)(2,1)} %collective-permute-done.8.refs_2_, bf16[192,96,128]{2,1,0:T(8,128)(2,1)} %collective-permute-done.9.refs_3_, ...), custom_call_target="tpu_custom_call" | custom-call | flops 115000000 | bytes 18874368 | tf_op jit(solution)/shard_map/project/pallas_call | solution.py:134
  541.9 0.0 collective-permute-done.14.refs_1_
  541.9 3.3 collective-permute-start.15
  545.1 2.5 collective-permute-start.13
  547.6 1.9 collective-permute-start.18
  549.5 0.0 collective-permute-done.11.refs_4_.refs_8_
  549.6 22.4 %triangle.5.refs_7_.refs_13_ = bf16[96,96,128]{2,1,0:T(8,128)(2,1)} custom-call(s32[1]{0:T(128)} %bitcast.3.refs_0_, bf16[128,96,384]{2,1,0:T(8,128)(2,1)} %project.7.refs_1_, bf16[128,96,384]{2,1,0:T(8,128)(2,1)} %collective-permute-done.5.refs_2_, bf16[128,96,384]{2,1,0:T(8,128)(2,1)} %project.9.refs_3_.refs_6_, ...), custom_call_target="tpu_custom_call" | custom-call | flops 200000000 | bytes 37748736 | tf_op jit(solution)/shard_map/triangle/pallas_call | solution.py:230
  572.0 29.9 %triangle.6.refs_8_.refs_14_ = bf16[64,192,128]{2,1,0:T(8,128)(2,1)} custom-call(s32[1]{0:T(128)} %bitcast.3.refs_0_, bf16[128,64,384]{2,1,0:T(8,128)(2,1)} %collective-permute-done.14.refs_1_, bf16[128,64,384]{2,1,0:T(8,128)(2,1)} %collective-permute-done.15.refs_2_, bf16[128,64,384]{2,1,0:T(8,128)(2,1)} %get-tuple-element.31.refs_3_, ...), custom_call_target="tpu_custom_call" | custom-call | flops 200000000 | bytes 50331648 | tf_op jit(solution)/shard_map/triangle/pallas_call | solution.py:230
  601.9 2.3 collective-permute-start.17
  604.2 0.8 collective-permute-start.7
  605.0 1.3 collective-permute-start.20
  606.3 2.0 collective-permute-start.12
  608.3 80.1 %collective-permute-start.23 = (bf16[64,192,128]{2,1,0:T(8,128)(2,1)}, bf16[64,192,128]{2,1,0:T(8,128)(2,1)}, u32[]{:S(2)}, u32[]{:S(2)}) collective-permute-start(bf16[64,192,128]{2,1,0:T(8,128)(2,1)} %triangle.6.refs_8_.refs_14_), channel_id=1, source_target_pairs={{0,1},{1,5},{4,3},{5,7},{9,12},{12,10},{13,14},{16,17},{17,21},{20... | collective-permute-start | bytes 9437192 | tf_op jit(solution)/shard_map/ppermute | solution.py:50
  688.5 1.5 copy-done.1
  689.9 2.3 collective-permute-start.24
  692.2 1.3 collective-permute-start.21
  693.5 24.8 %triangle.7.refs_8_.refs_14_ = bf16[32,192,128]{2,1,0:T(8,128)(2,1)} custom-call(s32[1]{0:T(128)} %bitcast.3.refs_0_, bf16[128,32,384]{2,1,0:T(8,128)(2,1)} %collective-permute-done.13.refs_1_, bf16[128,32,384]{2,1,0:T(8,128)(2,1)} %collective-permute-done.17.refs_2_, bf16[128,32,384]{2,1,0:T(8,128)(2,1)} %get-tuple-element.34.refs_3_, ...), custom_call_target="tpu_custom_call" | custom-call | flops 200000000 | bytes 44040192 | tf_op jit(solution)/shard_map/triangle/pallas_call | solution.py:230
  718.4 19.1 %collective-permute-start.19 = (bf16[32,192,128]{2,1,0:T(8,128)(2,1)}, bf16[32,192,128]{2,1,0:T(8,128)(2,1)S(1)}, u32[]{:S(2)}, u32[]{:S(2)}) collective-permute-start(bf16[32,192,128]{2,1,0:T(8,128)(2,1)} %triangle.7.refs_8_.refs_14_), channel_id=1, source_target_pairs={{0,1},{1,5},{4,3},{5,7},{9,12},{12,10},{13,14},{16,17},{17,21},{20... | collective-permute-start | bytes 4718600 | tf_op jit(solution)/shard_map/ppermute | solution.py:50
  737.5 0.8 collective-permute-start.22
  738.3 0.6 pad_add_fusion.refs_0_
  738.9 32.9 %collective-permute-done.21.refs_10_ = bf16[96,96,128]{2,1,0:T(8,128)(2,1)} collective-permute-done((bf16[96,96,128]{2,1,0:T(8,128)(2,1)}, bf16[96,96,128]{2,1,0:T(8,128)(2,1)}, u32[]{:S(2)}, u32[]{:S(2)}) %collective-permute-start.21) | collective-permute-done | bytes 2359328 | tf_op jit(solution)/shard_map/ppermute | solution.py:50
  771.8 16.1 %finish.2.refs_17_ = bf16[192,192,128]{2,1,0:T(8,128)(2,1)} custom-call(s32[2]{0:T(128)} %pad_add_fusion.refs_0_, bf16[192,192,128]{2,1,0:T(8,128)(2,1)} %refs_1_.3, bf16[192,192,128]{2,1,0:T(8,128)(2,1)} %gate_in.1.refs_2_, bf16[96,96,128]{2,1,0:T(8,128)(2,1)} %copy-done.1, bf16[96,96,128]{2,1,0:T(8,128)(2,1)} %collective-permute-done.12.refs_4_, ...), custom_call_target="tpu_custom_call" | custom-call | flops 40000000 | bytes 23592960 | tf_op jit(solution)/shard_map/finish/pallas_call | solution.py:315
  787.9 1.2 copy-done.2
  789.1 1.2 copy-done.3
  790.2 10.6 %finish.3 = bf16[192,192,128]{2,1,0:T(8,128)(2,1)} custom-call(s32[2]{0:T(128)} %pad_add_fusion.refs_0_, bf16[192,192,128]{2,1,0:T(8,128)(2,1)} %refs_1_.3, bf16[192,192,128]{2,1,0:T(8,128)(2,1)} %gate_in.1.refs_2_, bf16[96,96,128]{2,1,0:T(8,128)(2,1)} %copy-done.1, ...), custom_call_target="tpu_custom_call", output_to_operand_aliasing={{}: (17, {})} | custom-call | flops 40000000 | bytes 23592960 | tf_op jit(solution)/shard_map/finish/pallas_call | solution.py:315
  (30 shorter events, 0.1 us)
Async XLA Ops:
  1.1 9.3 %copy-start.4 = (s32[192,192]{1,0:T(8,128)S(1)}, s32[192,192]{1,0:T(8,128)}, u32[]{:S(2)}) copy-start(s32[192,192]{1,0:T(8,128)} %param.11) | copy-start | bytes 442372
  7.4 105.1 %collective-permute-start.1 = (bf16[192,96,128]{2,1,0:T(8,128)(2,1)}, bf16[192,96,128]{2,1,0:T(8,128)(2,1)}, u32[]{:S(2)}, u32[]{:S(2)}) collective-permute-start(bf16[192,96,128]{2,1,0:T(8,128)(2,1)} %select_select_fusion.1.refs_1_), channel_id=1, source_target_pairs={{0,2},{1,3},{2,0},{3,1},{4,6},{5,7},{6,4},{7,5},{8,10},{9,11},{10,... | collective-permute-start | bytes 14155784 | tf_op jit(solution)/shard_map/ppermute | solution.py:50
  16.7 120.1 %collective-permute-start.3 = (bf16[192,96,128]{2,1,0:T(8,128)(2,1)}, bf16[192,96,128]{2,1,0:T(8,128)(2,1)}, u32[]{:S(2)}, u32[]{:S(2)}) collective-permute-start(bf16[192,96,128]{2,1,0:T(8,128)(2,1)} %select_select_fusion.p0_ref.refs_3_), channel_id=1, source_target_pairs={{0,4},{1,5},{2,6},{3,7},{4,0},{5,1},{6,2},{7,3},{8,12},{9,13},{10,... | collective-permute-start | bytes 14155784 | tf_op jit(solution)/shard_map/ppermute | solution.py:50
  18.2 101.7 %copy-start.5 = (bf16[128,128]{1,0:T(8,128)(2,1)S(1)}, bf16[128,128]{1,0:T(8,128)(2,1)}, u32[]{:S(2)}) copy-start(bf16[128,128]{1,0:T(8,128)(2,1)} %param.14) | copy-start | bytes 98308
  18.2 101.8 %copy-start.6 = (bf16[128,128]{1,0:T(8,128)(2,1)S(1)}, bf16[128,128]{1,0:T(8,128)(2,1)}, u32[]{:S(2)}) copy-start(bf16[128,128]{1,0:T(8,128)(2,1)} %param.13) | copy-start | bytes 98308
  18.2 102.0 %copy-start.7 = (bf16[128,128]{1,0:T(8,128)(2,1)S(1)}, bf16[128,128]{1,0:T(8,128)(2,1)}, u32[]{:S(2)}) copy-start(bf16[128,128]{1,0:T(8,128)(2,1)} %param.16) | copy-start | bytes 98308
  18.2 102.1 %copy-start.8 = (bf16[128,128]{1,0:T(8,128)(2,1)S(1)}, bf16[128,128]{1,0:T(8,128)(2,1)}, u32[]{:S(2)}) copy-start(bf16[128,128]{1,0:T(8,128)(2,1)} %param.15) | copy-start | bytes 98308
  112.5 108.9 %collective-permute-start.4 = (bf16[192,96,128]{2,1,0:T(8,128)(2,1)}, bf16[192,96,128]{2,1,0:T(8,128)(2,1)}, u32[]{:S(2)}, u32[]{:S(2)}) collective-permute-start(bf16[192,96,128]{2,1,0:T(8,128)(2,1)} %collective-permute-done.1.p1_ref.refs_4_), channel_id=1, source_target_pairs={{0,4},{1,5},{2,6},{3,7},{4,0},{5,1},{6,2},{7,3},{8,12},{9,13},{10,... | collective-permute-start | bytes 14155784 | tf_op jit(solution)/shard_map/ppermute | solution.py:50
  114.3 148.0 %collective-permute-start = (bf16[192,96,128]{2,1,0:T(8,128)(2,1)}, bf16[192,96,128]{2,1,0:T(8,128)(2,1)}, u32[]{:S(2)}, u32[]{:S(2)}) collective-permute-start(bf16[192,96,128]{2,1,0:T(8,128)(2,1)} %select_select_fusion.p0_ref.refs_3_), channel_id=1, source_target_pairs={{4,8},{5,9},{6,10},{7,11},{8,4},{9,5},{10,6},{11,7},{20,24},{21,25... | collective-permute-start | bytes 14155784 | tf_op jit(solution)/shard_map/ppermute | solution.py:50
  117.1 145.2 %collective-permute-start.2 = (bf16[192,96,128]{2,1,0:T(8,128)(2,1)}, bf16[192,96,128]{2,1,0:T(8,128)(2,1)}, u32[]{:S(2)}, u32[]{:S(2)}) collective-permute-start(bf16[192,96,128]{2,1,0:T(8,128)(2,1)} %collective-permute-done.1.p1_ref.refs_4_), channel_id=1, source_target_pairs={{4,8},{5,9},{6,10},{7,11},{8,4},{9,5},{10,6},{11,7},{20,24},{21,25... | collective-permute-start | bytes 14155784 | tf_op jit(solution)/shard_map/ppermute | solution.py:50
  285.4 122.9 %collective-permute-start.5 = (bf16[128,96,384]{2,1,0:T(8,128)(2,1)}, bf16[128,96,384]{2,1,0:T(8,128)(2,1)}, u32[]{:S(2)}, u32[]{:S(2)}) collective-permute-start(bf16[128,96,384]{2,1,0:T(8,128)(2,1)} %project.7.refs_1_), channel_id=1, source_target_pairs={{0,1},{1,0},{2,3},{3,2},{4,5},{5,4},{6,7},{7,6},{8,9},{9,8},{10,11... | collective-permute-start | bytes 28311560 | tf_op jit(solution)/shard_map/ppermute | solution.py:50
  285.4 122.9 %collective-permute-start.6 = (bf16[128,96,384]{2,1,0:T(8,128)(2,1)}, bf16[128,96,384]{2,1,0:T(8,128)(2,1)}, u32[]{:S(2)}, u32[]{:S(2)}) collective-permute-start(bf16[128,96,384]{2,1,0:T(8,128)(2,1)} %project_x.2), channel_id=1, source_target_pairs={{0,1},{1,0},{2,3},{3,2},{4,5},{5,4},{6,7},{7,6},{8,9},{9,8},{10,11... | collective-permute-start | bytes 28311560 | tf_op jit(solution)/shard_map/ppermute | solution.py:50
  285.9 104.1 %collective-permute-start.8 = (bf16[192,96,128]{2,1,0:T(8,128)(2,1)}, bf16[192,96,128]{2,1,0:T(8,128)(2,1)}, u32[]{:S(2)}, u32[]{:S(2)}) collective-permute-start(bf16[192,96,128]{2,1,0:T(8,128)(2,1)} %select_select_fusion.p0_ref.refs_3_), channel_id=1, source_target_pairs={{0,2},{1,3},{2,0},{3,1},{4,6},{5,7},{6,4},{7,5},{8,10},{9,11},{10,... | collective-permute-start | bytes 14155784 | tf_op jit(solution)/shard_map/ppermute | solution.py:50
  286.3 162.1 %collective-permute-start.9 = (bf16[192,96,128]{2,1,0:T(8,128)(2,1)}, bf16[192,96,128]{2,1,0:T(8,128)(2,1)}, u32[]{:S(2)}, u32[]{:S(2)}) collective-permute-start(bf16[192,96,128]{2,1,0:T(8,128)(2,1)} %select_select_fusion.1.refs_1_), channel_id=1, source_target_pairs={{0,4},{1,5},{2,6},{3,7},{4,0},{5,1},{6,2},{7,3},{8,12},{9,13},{10,... | collective-permute-start | bytes 14155784 | tf_op jit(solution)/shard_map/ppermute | solution.py:50
  390.0 103.2 %collective-permute-start.10 = (bf16[192,96,128]{2,1,0:T(8,128)(2,1)}, bf16[192,96,128]{2,1,0:T(8,128)(2,1)}, u32[]{:S(2)}, u32[]{:S(2)}) collective-permute-start(bf16[192,96,128]{2,1,0:T(8,128)(2,1)} %collective-permute-done.3.refs_1_), channel_id=1, source_target_pairs={{0,2},{1,3},{2,0},{3,1},{4,6},{5,7},{6,4},{7,5},{8,10},{9,11},{10,... | collective-permute-start | bytes 14155784 | tf_op jit(solution)/shard_map/ppermute | solution.py:50
  390.4 151.5 %collective-permute-start.14 = (bf16[128,64,384]{2,1,0:T(8,128)(2,1)}, bf16[128,64,384]{2,1,0:T(8,128)(2,1)}, u32[]{:S(2)}, u32[]{:S(2)}) collective-permute-start(bf16[128,64,384]{2,1,0:T(8,128)(2,1)} %get-tuple-element.31.refs_3_), channel_id=1, source_target_pairs={{4,8},{5,9},{6,10},{7,11},{8,4},{9,5},{10,6},{11,7},{20,24},{21,25... | collective-permute-start | bytes 18874376 | tf_op jit(solution)/shard_map/ppermute | solution.py:50
  516.2 33.3 %collective-permute-start.11 = (bf16[128,96,384]{2,1,0:T(8,128)(2,1)}, bf16[128,96,384]{2,1,0:T(8,128)(2,1)}, u32[]{:S(2)}, u32[]{:S(2)}) collective-permute-start(bf16[128,96,384]{2,1,0:T(8,128)(2,1)} %project.8), channel_id=1, source_target_pairs={{0,1},{1,0},{2,3},{3,2},{4,5},{5,4},{6,7},{7,6},{8,9},{9,8},{10,11... | collective-permute-start | bytes 28311560 | tf_op jit(solution)/shard_map/ppermute | solution.py:50
  516.2 55.8 %collective-permute-start.16 = (bf16[128,64,384]{2,1,0:T(8,128)(2,1)}, bf16[128,64,384]{2,1,0:T(8,128)(2,1)}, u32[]{:S(2)}, u32[]{:S(2)}) collective-permute-start(bf16[128,64,384]{2,1,0:T(8,128)(2,1)} %get-tuple-element.31.refs_3_), channel_id=1, source_target_pairs={{0,1},{1,0},{2,3},{3,2},{12,13},{13,12},{14,15},{15,14},{16,17},{1... | collective-permute-start | bytes 18874376 | tf_op jit(solution)/shard_map/ppermute | solution.py:50
  541.9 30.1 %collective-permute-start.15 = (bf16[128,64,384]{2,1,0:T(8,128)(2,1)}, bf16[128,64,384]{2,1,0:T(8,128)(2,1)}, u32[]{:S(2)}, u32[]{:S(2)}) collective-permute-start(bf16[128,64,384]{2,1,0:T(8,128)(2,1)} %collective-permute-done.14.refs_1_), channel_id=1, source_target_pairs={{4,5},{5,4},{6,7},{7,6},{8,9},{9,8},{10,11},{11,10},{20,21},{21,20... | collective-permute-start | bytes 18874376 | tf_op jit(solution)/shard_map/ppermute | solution.py:50
  545.1 56.7 %collective-permute-start.13 = (bf16[128,32,384]{2,1,0:T(8,128)(2,1)}, bf16[128,32,384]{2,1,0:T(8,128)(2,1)}, u32[]{:S(2)}, u32[]{:S(2)}) collective-permute-start(bf16[128,32,384]{2,1,0:T(8,128)(2,1)} %get-tuple-element.34.refs_3_), channel_id=1, source_target_pairs={{4,8},{5,9},{6,10},{7,11},{8,4},{9,5},{10,6},{11,7},{20,24},{21,25... | collective-permute-start | bytes 9437192 | tf_op jit(solution)/shard_map/ppermute | solution.py:50
  547.6 60.7 %collective-permute-start.18 = (bf16[128,32,384]{2,1,0:T(8,128)(2,1)}, bf16[128,32,384]{2,1,0:T(8,128)(2,1)}, u32[]{:S(2)}, u32[]{:S(2)}) collective-permute-start(bf16[128,32,384]{2,1,0:T(8,128)(2,1)} %get-tuple-element.34.refs_3_), channel_id=1, source_target_pairs={{0,1},{1,0},{2,3},{3,2},{12,13},{13,12},{14,15},{15,14},{16,17},{1... | collective-permute-start | bytes 9437192 | tf_op jit(solution)/shard_map/ppermute | solution.py:50
  572.0 32.2 %copy-start = (bf16[96,96,128]{2,1,0:T(8,128)(2,1)S(1)}, bf16[96,96,128]{2,1,0:T(8,128)(2,1)}, u32[]{:S(2)}) copy-start(bf16[96,96,128]{2,1,0:T(8,128)(2,1)} %triangle.4.refs_6_.refs_12_) | copy-start | bytes 7077892
  601.9 90.4 %collective-permute-start.17 = (bf16[128,32,384]{2,1,0:T(8,128)(2,1)}, bf16[128,32,384]{2,1,0:T(8,128)(2,1)}, u32[]{:S(2)}, u32[]{:S(2)}) collective-permute-start(bf16[128,32,384]{2,1,0:T(8,128)(2,1)} %collective-permute-done.13.refs_1_), channel_id=1, source_target_pairs={{4,5},{5,4},{6,7},{7,6},{8,9},{9,8},{10,11},{11,10},{20,21},{21,20... | collective-permute-start | bytes 9437192 | tf_op jit(solution)/shard_map/ppermute | solution.py:50
  604.2 84.3 %collective-permute-start.7 = (bf16[96,96,128]{2,1,0:T(8,128)(2,1)S(1)}, bf16[96,96,128]{2,1,0:T(8,128)(2,1)S(1)}, u32[]{:S(2)}, u32[]{:S(2)}) collective-permute-start(bf16[96,96,128]{2,1,0:T(8,128)(2,1)S(1)} %copy-done), channel_id=1, source_target_pairs={{1,4},{4,2},{5,6},{8,9},{9,13},{12,11},{13,15},{17,20},{20,18},{21... | collective-permute-start | bytes 7077896 | tf_op jit(solution)/shard_map/ppermute | solution.py:50
  605.0 113.4 %collective-permute-start.20 = (bf16[96,96,128]{2,1,0:T(8,128)(2,1)S(1)}, bf16[96,96,128]{2,1,0:T(8,128)(2,1)}, u32[]{:S(2)}, u32[]{:S(2)}) collective-permute-start(bf16[96,96,128]{2,1,0:T(8,128)(2,1)S(1)} %copy-done), channel_id=1, source_target_pairs={{2,0},{3,4},{6,2},{7,6},{10,9},{11,13},{14,11},{18,16},{19,20},{22... | collective-permute-start | bytes 7077896 | tf_op jit(solution)/shard_map/ppermute | solution.py:50
  606.3 131.2 %collective-permute-start.12 = (bf16[96,96,128]{2,1,0:T(8,128)(2,1)}, bf16[96,96,128]{2,1,0:T(8,128)(2,1)}, u32[]{:S(2)}, u32[]{:S(2)}) collective-permute-start(bf16[96,96,128]{2,1,0:T(8,128)(2,1)} %triangle.5.refs_7_.refs_13_), channel_id=1, source_target_pairs={{1,4},{4,2},{5,6},{8,9},{9,13},{12,11},{13,15},{17,20},{20,18},{21... | collective-permute-start | bytes 7077896 | tf_op jit(solution)/shard_map/ppermute | solution.py:50
  608.3 163.4 %collective-permute-start.23 = (bf16[64,192,128]{2,1,0:T(8,128)(2,1)}, bf16[64,192,128]{2,1,0:T(8,128)(2,1)}, u32[]{:S(2)}, u32[]{:S(2)}) collective-permute-start(bf16[64,192,128]{2,1,0:T(8,128)(2,1)} %triangle.6.refs_8_.refs_14_), channel_id=1, source_target_pairs={{0,1},{1,5},{4,3},{5,7},{9,12},{12,10},{13,14},{16,17},{17,21},{20... | collective-permute-start | bytes 9437192 | tf_op jit(solution)/shard_map/ppermute | solution.py:50
  688.5 1.5 copy-start.1
  689.9 81.8 %collective-permute-start.24 = (bf16[64,192,128]{2,1,0:T(8,128)(2,1)}, bf16[64,192,128]{2,1,0:T(8,128)(2,1)}, u32[]{:S(2)}, u32[]{:S(2)}) collective-permute-start(bf16[64,192,128]{2,1,0:T(8,128)(2,1)} %triangle.6.refs_8_.refs_14_), channel_id=1, source_target_pairs={{2,1},{3,5},{6,3},{10,8},{11,12},{14,10},{15,14},{18,17},{19,21},{... | collective-permute-start | bytes 9437192 | tf_op jit(solution)/shard_map/ppermute | solution.py:50
  692.2 79.5 %collective-permute-start.21 = (bf16[96,96,128]{2,1,0:T(8,128)(2,1)}, bf16[96,96,128]{2,1,0:T(8,128)(2,1)}, u32[]{:S(2)}, u32[]{:S(2)}) collective-permute-start(bf16[96,96,128]{2,1,0:T(8,128)(2,1)} %triangle.5.refs_7_.refs_13_), channel_id=1, source_target_pairs={{2,0},{3,4},{6,2},{7,6},{10,9},{11,13},{14,11},{18,16},{19,20},{22... | collective-permute-start | bytes 7077896 | tf_op jit(solution)/shard_map/ppermute | solution.py:50
  718.4 69.5 %collective-permute-start.19 = (bf16[32,192,128]{2,1,0:T(8,128)(2,1)}, bf16[32,192,128]{2,1,0:T(8,128)(2,1)S(1)}, u32[]{:S(2)}, u32[]{:S(2)}) collective-permute-start(bf16[32,192,128]{2,1,0:T(8,128)(2,1)} %triangle.7.refs_8_.refs_14_), channel_id=1, source_target_pairs={{0,1},{1,5},{4,3},{5,7},{9,12},{12,10},{13,14},{16,17},{17,21},{20... | collective-permute-start | bytes 4718600 | tf_op jit(solution)/shard_map/ppermute | solution.py:50
  737.5 50.4 %collective-permute-start.22 = (bf16[32,192,128]{2,1,0:T(8,128)(2,1)}, bf16[32,192,128]{2,1,0:T(8,128)(2,1)S(1)}, u32[]{:S(2)}, u32[]{:S(2)}) collective-permute-start(bf16[32,192,128]{2,1,0:T(8,128)(2,1)} %triangle.7.refs_8_.refs_14_), channel_id=1, source_target_pairs={{2,1},{3,5},{6,3},{10,8},{11,12},{14,10},{15,14},{18,17},{19,21},{... | collective-permute-start | bytes 4718600 | tf_op jit(solution)/shard_map/ppermute | solution.py:50
  787.9 1.2 copy-start.2
  789.1 1.2 copy-start.3
